TPU v7x, 64 devices: a 2x2x8 block of a 4x4x8 slice. The times are simulated.
64 devices in a mesh: rep: 8 (over x, y, core), dp: 8 (over z).
Axes of the slice: x: 2, y: 2, z: 8, core: 2. Of those that a mesh axis runs over, the one named last changes fastest.
The devices are a block of a 4x4x8 slice.
Arguments:
- x: bfloat16 [64, 4096, 640], P(('rep', 'dp')), parts along dimension 0
- dy: bfloat16 [64, 4096, 640], P(('rep', 'dp')), parts along dimension 0
- w_gate: bfloat16 [2, 640, 1536], replicated
- w_up: bfloat16 [2, 640, 1536], replicated
- w_down: bfloat16 [2, 1536, 640], replicated
- m_w_gate: float32 [2, 640, 1536], replicated
- m_w_up: float32 [2, 640, 1536], replicated
- m_w_down: float32 [2, 1536, 640], replicated
- v_w_gate: float32 [2, 640, 1536], replicated
- v_w_up: float32 [2, 640, 1536], replicated
- v_w_down: float32 [2, 1536, 640], replicated
Outputs:
- output 1: bfloat16 [16, 640, 1536], P('rep'), parts along dimension 0
- output 2: bfloat16 [16, 640, 1536], P('rep'), parts along dimension 0
- output 3: bfloat16 [16, 1536, 640], P('rep'), parts along dimension 0
- output 4: float32 [16, 640, 1536], P('rep'), parts along dimension 0
- output 5: float32 [16, 640, 1536], P('rep'), parts along dimension 0
- output 6: float32 [16, 1536, 640], P('rep'), parts along dimension 0
- output 7: float32 [16, 640, 1536], P('rep'), parts along dimension 0
- output 8: float32 [16, 640, 1536], P('rep'), parts along dimension 0
- output 9: float32 [16, 1536, 640], P('rep'), parts along dimension 0
There are 8 independent parts. A program takes and returns all parts, laid end to end along the dimension named above; an argument that names none is the same for every part.
All inputs are finite; a program needn't handle non-finite values.
Results may differ from a plain program's by a relative error of at most 0.022.
Values are sent between devices in bfloat16 or wider.
A program may use at most 768 MiB of HBM per device.

v0:
```python
import jax
import jax.numpy as jnp
from jax import lax
from jax.sharding import PartitionSpec as P

NAMES = ("w_gate", "w_up", "w_down")


def matmul(a, w):
    return jnp.dot(a, w, preferred_element_type=jnp.float32).astype(jnp.bfloat16)


def normed(h):
    wide = h.astype(jnp.float32)
    scale = lax.rsqrt(jnp.mean(wide**2, -1, keepdims=True) + 1e-6)
    return (wide * scale).astype(jnp.bfloat16)


def layer(h, w):
    a = normed(h)
    gate = jnp.dot(a, w["w_gate"], preferred_element_type=jnp.float32)
    up = jnp.dot(a, w["w_up"], preferred_element_type=jnp.float32)
    return h + matmul((jax.nn.silu(gate) * up).astype(jnp.bfloat16), w["w_down"])


def adamw(w, m, v, g):
    m = 0.9 * m + 0.1 * g
    v = 0.95 * v + 0.05 * g * g
    step = m * lax.rsqrt(v + 1e-8) + 0.1 * w
    return (w - 0.02 * step).astype(jnp.bfloat16), m, v


def clipped(gradients, sum_of_squares, count):
    factor = jnp.minimum(1.0, 0.5 * lax.rsqrt(sum_of_squares / count + 1e-30))
    return [g * factor for g in gradients]


def solution(mesh):
    def step(x, dy, *arrays):
        weights, m, v = (arrays[i : i + 3] for i in (0, 3, 6))
        layers = weights[0].shape[0]
        h, kept = x[0], []
        for number in range(layers):
            kept.append(h)
            h = layer(h, {name: w[number] for name, w in zip(NAMES, weights, strict=True)})
        by_h, summed = dy[0], [None] * layers
        for number in reversed(range(layers)):
            _, back = jax.vjp(lambda w, h: layer(h, w), {name: w[number] for name, w in zip(NAMES, weights, strict=True)}, kept[number])
            by_w, by_h = back(by_h)
            summed[number] = [lax.psum(by_w[name], "dp") for name in NAMES]
        gradients = [jnp.stack([summed[number][i] for number in range(layers)]).astype(jnp.float32) for i in range(3)]
        gradients = clipped(gradients, sum(jnp.sum(g * g) for g in gradients), sum(g.size for g in gradients))
        new = [adamw(w.astype(jnp.float32), m, v, g) for w, m, v, g in zip(weights, m, v, gradients, strict=True)]
        return tuple(one[which] for which in range(3) for one in new)

    return jax.shard_map(
        step,
        mesh=mesh,
        in_specs=(P(("rep", "dp"), None, None),) * 2 + (P(None, None, None),) * 9,
        out_specs=(P("rep", None, None),) * 9,
        check_vma=False,
    )
```

profile of v0, /device:TPU:28, one launch (start us, length us, event | category | flops | bytes accessed | tf_op | source)
XLA Modules:
  0.0 655.0 jit_solution(13258056656374228867)
XLA Ops:
  7.2 0.1 all-reduce.3.cloned.1.call-start
  7.3 7.9 %copy.20 = bf16[1,4096,640]{1,2,0:T(8,128)(2,1)} copy(bf16[1,4096,640]{2,1,0:T(8,128)(2,1)} %param.11) | data formatting | bytes 10485760 | tf_op args[0]
  15.1 3.6 fusion.15
  18.7 0.0 copy-start.14
  18.8 0.0 slice-start
  18.8 7.9 %copy.21 = bf16[1,4096,640]{1,2,0:T(8,128)(2,1)} copy(bf16[1,4096,640]{2,1,0:T(8,128)(2,1)} %param.12) | data formatting | bytes 10485760 | tf_op args[1]
  26.7 15.9 %convolution_convert_fusion.1 = bf16[4096,1536]{1,0:T(8,128)(2,1)} fusion(bf16[1,4096,640]{2,1,0:T(8,128)(2,1)} %param.12, bf16[2,1536,640]{2,1,0:T(8,128)(2,1)} %param.15), kind=kOutput, calls=%fused_computation.27 | convolution fusion | flops 8059355136 | bytes 19791872 | tf_op jit(solution)/shard_map/transpose(jvp())/dot_general | solution.py:10
  42.6 0.0 slice-done
  42.6 0.0 slice-done.1
  42.6 0.0 copy-done.10
  42.6 13.4 %fusion.96 = f32[4096,1536]{1,0:T(8,128)} fusion(bf16[1,4096,640]{2,1,0:T(8,128)(2,1)S(1)} %bitcast.83, f32[4096]{0:T(1024)S(1)} %add_rsqrt_fusion, bf16[2,640,1536]{2,1,0:T(8,128)(2,1)S(1)} %copy-done.10), kind=kOutput, calls=%fused_computation.105 | convolution fusion | flops 8060928000 | bytes 32391168 | tf_op jit(solution)/shard_map/dot_general | solution.py:21
  56.0 0.0 copy-done.14
  56.0 28.7 %multiply_convert_fusion.1 = (bf16[4096,1536]{1,0:T(8,128)(2,1)}, f32[4096,1536]{1,0:T(8,128)}) fusion(f32[4096,1536]{1,0:T(8,128)} %fusion.96, bf16[2,640,1536]{2,1,0:T(8,128)(2,1)} %param.14, bf16[1,4096,640]{2,1,0:T(8,128)(2,1)} %param.11, f32[4096]{0:T(1024)S(1)} %add_rsqrt_fusion), kind=kOutput, calls=%fused_computation.17 | convolution fusion | flops 8098676736 | bytes 70139904 | tf_op jit(solution)/shard_map/dot_general | solution.py:22
  84.7 0.0 copy-done.8
  84.7 13.6 %fusion.19 = (f32[4096]{0:T(1024)S(1)}, bf16[4096,640]{0,1:T(8,128)(2,1)S(1)}) fusion(bf16[4096,1536]{1,0:T(8,128)(2,1)} %get-tuple-element.24, bf16[2,1536,640]{2,1,0:T(8,128)(2,1)S(1)} %copy-done.8, bf16[1,4096,640]{1,2,0:T(8,128)(2,1)} %copy.20), kind=kOutput, calls=%fused_computation.40 | convolution fusion | flops 8066166784 | bytes 25051136 | tf_op jit(solution)/shard_map/dot_general | solution.py:10
  98.3 0.0 copy-start.5
  98.3 0.0 copy-start.12
  98.4 2.3 copy-done.5
  100.7 15.0 %fusion.55 = f32[4096,1536]{1,0:T(8,128)} fusion(bf16[4096,640]{0,1:T(8,128)(2,1)S(1)} %get-tuple-element.27, f32[4096]{0:T(1024)S(1)} %fusion.116, bf16[2,640,1536]{2,1,0:T(8,128)(2,1)} %param.14), kind=kOutput, calls=%fused_computation.90 | convolution fusion | flops 8060928000 | bytes 32391168 | tf_op jit(solution)/shard_map/jvp()/dot_general | solution.py:22
  115.7 0.0 copy-done.12
  115.7 39.6 %fusion.2 = (bf16[4096,1536]{1,0:T(8,128)(2,1)}, f32[4096,1536]{1,0:T(8,128)}) fusion(f32[4096,1536]{1,0:T(8,128)} %fusion.55, bf16[4096,1536]{1,0:T(8,128)(2,1)} %convolution_convert_fusion.1, bf16[2,640,1536]{2,1,0:T(8,128)(2,1)} %param.13, bf16[4096,640]{0,1:T(8,128)(2,1)} %copy-done.5, f32[4096]{0:T(1024)S(1)} %fusion.116), kind=kOutput, calls=%fused_computation.8 | convolution fusion | flops 8136425472 | bytes 82722816 | tf_op jit(solution)/shard_map/jvp()/dot_general | solution.py:21
  155.3 22.3 %fusion.86 = bf16[1,1536,640]{2,1,0:T(8,128)(2,1)} fusion(bf16[1,4096,640]{2,1,0:T(8,128)(2,1)} %param.12, f32[4096,1536]{1,0:T(8,128)} %fusion.55, f32[4096,1536]{1,0:T(8,128)} %get-tuple-element.29), kind=kOutput, calls=%fused_computation.102 | convolution fusion | flops 8091795456 | bytes 57540608 | tf_op jit(solution)/shard_map/transpose(jvp())/dot_general | solution.py:10
  177.6 19.4 %fusion.79 = bf16[1,640,1536]{2,1,0:T(8,128)(2,1)} fusion(bf16[4096,1536]{1,0:T(8,128)(2,1)} %convolution_convert_fusion.1, bf16[4096,640]{0,1:T(8,128)(2,1)} %copy-done.5, f32[4096]{0:T(1024)S(1)} %fusion.116, f32[4096,1536]{1,0:T(8,128)} %get-tuple-element.29), kind=kOutput, calls=%fused_computation.99 | convolution fusion | flops 8099659776 | bytes 44974080 | tf_op jit(solution)/shard_map/transpose(jvp())/dot_general | solution.py:22
  197.0 18.2 %fusion.43 = bf16[4096,640]{0,1:T(8,128)(2,1)} fusion(bf16[4096,1536]{1,0:T(8,128)(2,1)} %convolution_convert_fusion.1, bf16[2,640,1536]{2,1,0:T(8,128)(2,1)} %param.14, f32[4096,1536]{1,0:T(8,128)} %get-tuple-element.29), kind=kOutput, calls=%fused_computation.77 | convolution fusion | flops 8093433856 | bytes 44957696 | tf_op jit(solution)/shard_map/transpose(jvp())/dot_general | solution.py:22
  215.2 16.0 %fusion.82 = bf16[1,640,1536]{2,1,0:T(8,128)(2,1)} fusion(bf16[4096,1536]{1,0:T(8,128)(2,1)} %get-tuple-element.28, bf16[4096,640]{0,1:T(8,128)(2,1)} %copy-done.5, f32[4096]{0:T(1024)S(1)} %fusion.116), kind=kOutput, calls=%fused_computation.100 | convolution fusion | flops 8060928000 | bytes 19808256 | tf_op jit(solution)/shard_map/transpose(jvp())/dot_general | solution.py:21
  231.2 0.0 copy-done.6
  231.2 0.0 copy-done.11
  231.2 18.5 %fusion.21 = (f32[4096]{0:T(1024)S(1)}, bf16[4096,640]{0,1:T(8,128)(2,1)}) fusion(bf16[4096,640]{0,1:T(8,128)(2,1)S(1)} %copy-done.6, bf16[4096,640]{0,1:T(8,128)(2,1)} %fusion.43, bf16[4096,1536]{1,0:T(8,128)(2,1)} %get-tuple-element.28, bf16[2,640,1536]{2,1,0:T(8,128)(2,1)S(1)} %copy-done.11), kind=kOutput, calls=%fused_computation.42 | convolution fusion | flops 8066166784 | bytes 30294016 | tf_op jit(solution)/shard_map/transpose(jvp())/dot_general | solution.py:21
  249.7 0.0 copy-done.13
  249.7 11.9 %fusion.45 = bf16[4096,640]{0,1:T(8,128)(2,1)} fusion(bf16[4096,640]{0,1:T(8,128)(2,1)} %copy-done.5, bf16[4096,640]{0,1:T(8,128)(2,1)} %get-tuple-element.31, bf16[1,4096,640]{1,2,0:T(8,128)(2,1)} %copy.21, f32[4096]{0:T(1024)S(1)} %multiply_multiply_fusion.3, f32[4096]{0:T(1024)S(1)} %fusion.116), kind=kLoop, calls=%fused_computation.81 | loop fusion | flops 18350080 | bytes 21004288 | tf_op jit(solution)/shard_map/transpose(jvp())/add_any | solution.py:14
  261.7 17.5 %fusion.85 = bf16[1,1536,640]{2,1,0:T(8,128)(2,1)} fusion(bf16[4096,1536]{1,0:T(8,128)(2,1)} %get-tuple-element.24, bf16[4096,640]{0,1:T(8,128)(2,1)} %fusion.45), kind=kOutput, calls=%fused_computation.101 | convolution fusion | flops 8054046720 | bytes 19791872 | tf_op jit(solution)/shard_map/transpose(jvp())/dot_general | solution.py:10
  279.1 0.0 copy-done.7
  279.1 0.0 copy-done.9
  279.1 12.8 %convolution_convert_fusion = bf16[4096,1536]{1,0:T(8,128)(2,1)} fusion(bf16[4096,640]{0,1:T(8,128)(2,1)S(1)} %copy-done.7, bf16[2,1536,640]{2,1,0:T(8,128)(2,1)S(1)} %copy-done.9), kind=kOutput, calls=%fused_computation.26 | convolution fusion | flops 8059355136 | bytes 19791872 | tf_op jit(solution)/shard_map/transpose(jvp())/dot_general | solution.py:10
  292.0 0.0 copy-done.15
  292.0 19.4 %fusion.76 = bf16[1,640,1536]{2,1,0:T(8,128)(2,1)} fusion(bf16[4096,1536]{1,0:T(8,128)(2,1)} %convolution_convert_fusion, f32[4096,1536]{1,0:T(8,128)} %fusion.96, bf16[1,4096,640]{1,2,0:T(8,128)(2,1)} %copy.20, f32[4096]{0:T(1024)S(1)} %copy-done.15), kind=kOutput, calls=%fused_computation.98 | convolution fusion | flops 8099659776 | bytes 44974080 | tf_op jit(solution)/shard_map/transpose(jvp())/dot_general | solution.py:22
  311.3 28.8 %fusion.89 = bf16[1,640,1536]{2,1,0:T(8,128)(2,1)} fusion(f32[4096,1536]{1,0:T(8,128)} %fusion.96, f32[4096,1536]{1,0:T(8,128)} %get-tuple-element.25, bf16[4096,1536]{1,0:T(8,128)(2,1)} %convolution_convert_fusion, bf16[1,4096,640]{1,2,0:T(8,128)(2,1)} %copy.20, f32[4096]{0:T(1024)S(1)} %copy-done.15), kind=kOutput, calls=%fused_computation.103 | convolution fusion | flops 8131117056 | bytes 70139904 | tf_op jit(solution)/shard_map/transpose(jvp())/dot_general | solution.py:21
  340.2 0.1 all-reduce.3.cloned.1.call-update
  340.3 249.3 %all-reduce.3.cloned.1.call-done = (bf16[1,640,1536]{2,1,0:T(8,128)(2,1)}, bf16[1,640,1536]{2,1,0:T(8,128)(2,1)}, bf16[1,640,1536]{2,1,0:T(8,128)(2,1)}, bf16[1,...) async-done(((bf16[1,640,1536]{2,1,0:T(8,128)(2,1)}, bf16[1,640,1536]{2,1,0:T(8,128)(2,1)}, bf16[1,640,1536]{2,1,0:T(8,128)(2,1)}, ...) | async-done | bytes 11796496 | tf_op jit(solution)/shard_map/psum | solution.py:50
  589.5 4.9 fusion.33
  594.4 4.8 fusion.32
  599.2 0.0 copy-done
  599.2 0.0 copy-done.1
  599.2 2.6 fusion.31
  603.8 0.0 copy-start.2
  603.8 18.1 %fusion.39 = (bf16[2,1536,640]{2,1,0:T(8,128)(2,1)}, f32[2,1536,640]{2,1,0:T(8,128)}, f32[2,1536,640]{2,1,0:T(8,128)}) fusion(bf16[2,1536,640]{2,1,0:T(8,128)(2,1)} %param.15, f32[]{:T(128)S(6)} %min_shard_map.3, bf16[1,1536,640]{2,1,0:T(8,128)(2,1)} %get-tuple-element.13, bf16[1,1536,640]{2,1,0:T(8,128)(2,1)} %get-tuple-element.14, ...), kind=kLoop, calls=%fused_computation.73 | loop fusion | flops 39321600 | bytes 43253764 | tf_op jit(solution)/shard_map/convert_element_type | solution.py:30
  622.0 0.0 copy-done.2
  622.0 25.7 %fusion.30 = (bf16[2,640,1536]{2,1,0:T(8,128)(2,1)}, f32[2,640,1536]{2,1,0:T(8,128)}, f32[2,640,1536]{2,1,0:T(8,128)}, bf16[2,640,1536]{2,1,0:T(8,128)(2,1)}, f3...) fusion(bf16[2,640,1536]{2,1,0:T(8,128)(2,1)} %param.13, f32[]{:T(128)S(6)} %min_shard_map.3, ...), kind=kLoop, calls=%fused_computation.64 | loop fusion | flops 78643200 | bytes 86507520 | tf_op jit(solution)/shard_map/convert_element_type | solution.py:30
  (19 shorter events, 0.1 us)
Async XLA Ops:
  7.2 582.3 %all-reduce.3.cloned.1.call-start = ((), (), s32[]{:S(2)}) async-start(), calls=%async_computation | async-start | bytes 23592960 | tf_op jit(solution)/shard_map/psum | solution.py:50
  18.7 37.3 %copy-start.14 = (f32[4096]{0:T(1024)}, f32[4096]{0:T(1024)S(1)}, u32[]{:S(2)}) copy-start(f32[4096]{0:T(1024)S(1)} %add_rsqrt_fusion) | copy-start | bytes 49156
  18.8 23.9 %slice-start = ((s8[5242880]{0:T(1024)(128)(4,1)}), s8[1048576]{0:T(1024)(128)(4,1)S(1)}, s32[]{:S(2)}) async-start(s8[5242880]{0:T(1024)(128)(4,1)} %bitcast.82), calls=%async_computation.1 | async-start | bytes 2097152
  26.7 15.9 %slice-start.1 = ((s8[5242880]{0:T(1024)(128)(4,1)}), s8[4194304]{0:T(1024)(128)(4,1)S(1)}, s32[]{:S(2)}) async-start(s8[5242880]{0:T(1024)(128)(4,1)} %bitcast.82), calls=%async_computation.2 | async-start | bytes 8388608
  26.7 15.9 %copy-start.10 = (bf16[2,640,1536]{2,1,0:T(8,128)(2,1)S(1)}, bf16[2,640,1536]{2,1,0:T(8,128)(2,1)}, u32[]{:S(2)}) copy-start(bf16[2,640,1536]{2,1,0:T(8,128)(2,1)} %param.13) | copy-start | bytes 11796484
  56.0 28.7 %copy-start.8 = (bf16[2,1536,640]{2,1,0:T(8,128)(2,1)S(1)}, bf16[2,1536,640]{2,1,0:T(8,128)(2,1)}, u32[]{:S(2)}) copy-start(bf16[2,1536,640]{2,1,0:T(8,128)(2,1)} %param.15) | copy-start | bytes 11796484
  98.3 2.4 copy-start.5
  98.3 17.4 %copy-start.12 = (f32[4096]{0:T(1024)}, f32[4096]{0:T(1024)S(1)}, u32[]{:S(2)}) copy-start(f32[4096]{0:T(1024)S(1)} %get-tuple-element.26) | copy-start | bytes 49156
  215.2 16.0 %copy-start.6 = (bf16[4096,640]{0,1:T(8,128)(2,1)S(1)}, bf16[4096,640]{0,1:T(8,128)(2,1)}, u32[]{:S(2)}) copy-start(bf16[4096,640]{0,1:T(8,128)(2,1)} %copy-done.5) | copy-start | bytes 15728644
  215.2 16.0 %copy-start.11 = (bf16[2,640,1536]{2,1,0:T(8,128)(2,1)S(1)}, bf16[2,640,1536]{2,1,0:T(8,128)(2,1)}, u32[]{:S(2)}) copy-start(bf16[2,640,1536]{2,1,0:T(8,128)(2,1)} %param.13) | copy-start | bytes 11796484
  231.2 18.5 %copy-start.13 = (f32[4096]{0:T(1024)S(1)}, f32[4096]{0:T(1024)}, u32[]{:S(2)}) copy-start(f32[4096]{0:T(1024)} %copy-done.12) | copy-start | bytes 49156
  261.7 17.5 %copy-start.7 = (bf16[4096,640]{0,1:T(8,128)(2,1)S(1)}, bf16[4096,640]{0,1:T(8,128)(2,1)}, u32[]{:S(2)}) copy-start(bf16[4096,640]{0,1:T(8,128)(2,1)} %fusion.45) | copy-start | bytes 15728644
  261.7 17.5 %copy-start.9 = (bf16[2,1536,640]{2,1,0:T(8,128)(2,1)S(1)}, bf16[2,1536,640]{2,1,0:T(8,128)(2,1)}, u32[]{:S(2)}) copy-start(bf16[2,1536,640]{2,1,0:T(8,128)(2,1)} %param.15) | copy-start | bytes 11796484
  279.1 12.9 %copy-start.15 = (f32[4096]{0:T(1024)S(1)}, f32[4096]{0:T(1024)}, u32[]{:S(2)}) copy-start(f32[4096]{0:T(1024)} %copy-done.14) | copy-start | bytes 49156
  589.5 9.7 %copy-start = (bf16[1,640,1536]{2,1,0:T(8,128)(2,1)S(1)}, bf16[1,640,1536]{2,1,0:T(8,128)(2,1)}, u32[]{:S(2)}) copy-start(bf16[1,640,1536]{2,1,0:T(8,128)(2,1)} %get-tuple-element.9) | copy-start | bytes 5898244
  589.5 9.7 %copy-start.1 = (bf16[1,640,1536]{2,1,0:T(8,128)(2,1)S(1)}, bf16[1,640,1536]{2,1,0:T(8,128)(2,1)}, u32[]{:S(2)}) copy-start(bf16[1,640,1536]{2,1,0:T(8,128)(2,1)} %get-tuple-element.10) | copy-start | bytes 5898244
  603.8 18.2 %copy-start.2 = (bf16[1,640,1536]{2,1,0:T(8,128)(2,1)S(1)}, bf16[1,640,1536]{2,1,0:T(8,128)(2,1)}, u32[]{:S(2)}) copy-start(bf16[1,640,1536]{2,1,0:T(8,128)(2,1)} %get-tuple-element.10) | copy-start | bytes 5898244
  603.8 18.2 %copy-start.3 = (bf16[1,640,1536]{2,1,0:T(8,128)(2,1)S(1)}, bf16[1,640,1536]{2,1,0:T(8,128)(2,1)}, u32[]{:S(2)}) copy-start(bf16[1,640,1536]{2,1,0:T(8,128)(2,1)} %get-tuple-element.11) | copy-start | bytes 5898244
  603.8 18.2 %copy-start.4 = (bf16[1,640,1536]{2,1,0:T(8,128)(2,1)S(1)}, bf16[1,640,1536]{2,1,0:T(8,128)(2,1)}, u32[]{:S(2)}) copy-start(bf16[1,640,1536]{2,1,0:T(8,128)(2,1)} %get-tuple-element.12) | copy-start | bytes 5898244
Sparse Core Ops, SparseCore 0:
  340.4 249.1 all-reduce.2
where the time goes:
time: 665 us; the launch traced here: 655 us
  matrix products  299 us (45%)
  waiting for transfers between devices  249 us (37%)
  other arithmetic  71.7 us (11%)
  local copies, waits for them, and re-layouts  18.2 us (3%)
  between operations  16.6 us (2%)
    psum x1, waiting for transfers between devices, step(): summed[number] = [lax.psum(by_w[name], 'dp') for name in NAMES]  249 us
    dot_general x5, matrix products, layer(): gate = jnp.dot(a, w['w_gate'], preferred_element_type=jnp.float32)  116 us
    dot_general x5, matrix products, layer(): up = jnp.dot(a, w['w_up'], preferred_element_type=jnp.float32)  101 us
    dot_general x5, matrix products, matmul(): jnp.dot(a, w, preferred_element_type=jnp.float32).astype(jnp.bfloat16)  82.2 us
    convert_element_type x2, other arithmetic, adamw(): return ((w - 0.02 * step).astype(jnp.bfloat16), m, v)  43.8 us
    unnamed x38, local copies, waits for them, and re-layouts  18.2 us
  transfers between devices with their start and end apart: 1, of which 1 were waited for; matrix products, arithmetic and copies ran while one was open for 0% of the time, Pallas kernels for 0%

commit v1 on v0

v1 whole, which is shorter than its diff:
```python
import functools

import jax
import jax.numpy as jnp
from jax import lax
from jax.experimental import pallas as pl
from jax.experimental.pallas import tpu as pltpu
from jax.sharding import PartitionSpec as P

BF16, F32 = jnp.bfloat16, jnp.float32
MESH = pl.DeviceIdType.MESH
LANES = 128
FORWARD_TILE, TILE, BLOCK = 512, 1024, 256
PLAIN, BY_ROWS = ((1,), (0,)), ((1,), (1,))


def dot(a, b, contract=PLAIN):
    return lax.dot_general(a, b, (contract, ((), ())), preferred_element_type=F32)


def scale_of(wide):
    return lax.rsqrt(jnp.mean(wide * wide, -1, keepdims=True) + 1e-6)


def normed(h):
    wide = h.astype(F32)
    return (wide * scale_of(wide)).astype(BF16)


def forward_kernel(x_ref, dy_ref, wg_ref, wu_ref, wd_ref, h_ref, a0_ref, a0t_ref, a1_ref, a1t_ref, dyt_ref):
    x = x_ref[...]
    a0 = normed(x)
    a0_ref[...] = a0
    a0t_ref[...] = a0.T
    dyt_ref[...] = dy_ref[...].T
    gate = dot(a0, wg_ref[...])
    up = dot(a0, wu_ref[...])
    z = (gate * jax.nn.sigmoid(gate) * up).astype(BF16)
    h = (x.astype(F32) + dot(z, wd_ref[...]).astype(BF16).astype(F32)).astype(BF16)
    h_ref[...] = h
    a1 = normed(h)
    a1_ref[...] = a1
    a1t_ref[...] = a1.T


def forward(x, dy, w_gate, w_up, w_down):
    tokens, d = x.shape[1:]
    ff = w_gate.shape[2]
    tile = min(FORWARD_TILE, tokens)
    rows = pl.BlockSpec((tile, d), lambda i: (i, 0))
    turned = pl.BlockSpec((d, tile), lambda i: (0, i))
    given = pl.BlockSpec((None, tile, d), lambda i: (0, i, 0))
    wide, tall = jax.ShapeDtypeStruct((tokens, d), BF16), jax.ShapeDtypeStruct((d, tokens), BF16)
    return pl.pallas_call(
        forward_kernel,
        grid=(tokens // tile,),
        in_specs=[given, given]
        + [pl.BlockSpec((None, d, ff), lambda i: (0, 0, 0))] * 2
        + [pl.BlockSpec((None, ff, d), lambda i: (0, 0, 0))],
        out_specs=[rows, rows, turned, rows, turned, turned],
        out_shape=[wide, wide, tall, wide, tall, tall],
        compiler_params=pltpu.CompilerParams(vmem_limit_bytes=63 << 20),
        cost_estimate=pl.CostEstimate(flops=6 * tokens * d * ff, bytes_accessed=16 * tokens * d, transcendentals=tokens * ff),
        name="forward",
    )(x, dy, w_gate, w_up, w_down)


def when(condition, do):
    if isinstance(condition, bool):
        if condition:
            do()
    else:
        pl.when(condition)(do)


def main_kernel(
    n, h_hbm, a0_hbm, a0t_hbm, a1_hbm, a1t_hbm, dy_hbm, dyt_hbm, wg_hbm, wu_hbm, wd_hbm,
    g1_ref, g0_ref, total_ref,
    a, at, g, gt, da, hbuf, wgu, wd, acc_gu, acc_d, own, from_left, from_right, squares, parts,
    in_sem, w_sem, h_sem, send_sem, recv_sem, part_send, part_recv, credit,
):
    tokens, d = a.shape
    block = wd.shape[1]
    blocks = wg_hbm.shape[2] // block
    units, half = 2 * blocks, n // 2
    tile = hbuf.shape[1]
    tiles = tokens // tile
    slots, shard_rows = own.shape[0], own.shape[2]
    me = lax.axis_index("dp")
    right, left = lax.rem(me + 1, n), lax.rem(me + n - 1, n)

    def loads(t, first, second):
        rows = pl.ds(pl.multiple_of(t * tile, tile), tile)
        return [
            pltpu.make_async_copy(first.at[rows], a.at[rows], in_sem.at[0, t]),
            pltpu.make_async_copy(second.at[:, rows], at.at[:, rows], in_sem.at[1, t]),
        ]

    def gradient_loads(t):
        rows = pl.ds(pl.multiple_of(t * tile, tile), tile)
        return [
            pltpu.make_async_copy(dy_hbm.at[rows], g.at[rows], in_sem.at[2, t]),
            pltpu.make_async_copy(dyt_hbm.at[:, rows], gt.at[:, rows], in_sem.at[3, t]),
        ]

    def weight_loads(b):
        last = jnp.int32(b < blocks) if isinstance(b, int) else (b < blocks).astype(jnp.int32)
        columns = pl.ds(pl.multiple_of((b - blocks * (1 - last)) * block, block), block)
        slot = lax.rem(b, 2)
        return [
            pltpu.make_async_copy(wg_hbm.at[last, :, columns], wgu.at[slot, :, pl.ds(0, block)], w_sem.at[0, slot]),
            pltpu.make_async_copy(wu_hbm.at[last, :, columns], wgu.at[slot, :, pl.ds(block, block)], w_sem.at[1, slot]),
            pltpu.make_async_copy(wd_hbm.at[last, columns, :], wd.at[slot], w_sem.at[2, slot]),
        ]

    def state_load(t):
        rows = pl.ds(pl.multiple_of(t * tile, tile), tile)
        slot = lax.rem(t, 2)
        return pltpu.make_async_copy(h_hbm.at[rows], hbuf.at[slot], h_sem.at[slot])

    def ring_copy(u, k, way):
        slot = lax.rem(u, slots)
        ahead = half - k if way == 0 else n - half + k
        shard = lax.rem(me + ahead, n)
        rows = pl.ds(0, shard_rows)
        if k == 0:
            rows = pl.ds(way * (shard_rows // 2), shard_rows // 2)
        return pltpu.make_async_remote_copy(
            src_ref=own.at[slot, shard, rows],
            dst_ref=(from_left, from_right)[way].at[slot, k, rows],
            send_sem=send_sem.at[way, slot, k],
            recv_sem=recv_sem.at[way, slot, k],
            device_id={"dp": (right, left)[way]},
            device_id_type=MESH,
        )

    def event(u, e):
        slot = lax.rem(u, slots)
        if e == 0:

            def take():
                pl.semaphore_wait(credit.at[0], 1)
                pl.semaphore_wait(credit.at[1], 1)

            when(u >= slots, take)
        else:
            for way in (0, 1):
                ring_copy(u, e - 1, way).wait()
        if 0 < e < half:
            for way in (0, 1):
                shard = lax.rem(me + (half - e if way == 0 else n - half + e), n)
                rows = pl.ds(0, shard_rows) if e > 1 else pl.ds(way * (shard_rows // 2), shard_rows // 2)
                came = (from_left, from_right)[way][slot, e - 1, rows].astype(F32)
                own[slot, shard, rows] = (own[slot, shard, rows].astype(F32) + came).astype(BF16)
        if e < half:
            for way in (0, 1):
                ring_copy(u, e, way).start()
        else:
            came = from_left[slot, e - 1].astype(F32) + from_right[slot, e - 1].astype(F32)
            done = (own[slot, me].astype(F32) + came).astype(BF16)

            def keep(ref, index):
                def do():
                    ref[index] = done

                return do

            when(u < blocks, keep(g1_ref, jnp.minimum(u, blocks - 1)))
            when(u >= blocks, keep(g0_ref, jnp.maximum(u - blocks, 0)))
            wide = done.astype(F32)
            squares[...] += jnp.sum((wide * wide).reshape(shard_rows // 8, 8, LANES), 0)

            def give():
                pl.semaphore_signal(credit.at[0], 1, device_id={"dp": left}, device_id_type=MESH)
                pl.semaphore_signal(credit.at[1], 1, device_id={"dp": right}, device_id_type=MESH)

            when(u < units - slots, give)

    def events(b, t):
        for e in range(half + 1):
            lag, at_tile = divmod(5 * e // 2, tiles)
            u = b - 1 - lag
            if isinstance(b, int):
                if t == at_tile and 0 <= u < units:
                    event(u, e)
            else:

                @pl.when((t == at_tile) & (u >= 0))
                def _(u=u, e=e):
                    event(u, e)

    def steps(b, t, last):
        rows = pl.ds(pl.multiple_of(t * tile, tile), tile)
        slot = lax.rem(b, 2)
        gu = dot(a[rows], wgu[slot])
        dz = dot(g[rows], wd[slot], BY_ROWS).astype(BF16).astype(F32)
        gate, up = gu[:, :block], gu[:, block:]
        s = jax.nn.sigmoid(gate)
        silu = gate * s
        z = (silu * up).astype(BF16)
        dgate = (dz * up * (s + silu * (1 - s))).astype(BF16)
        dup = (dz * silu).astype(BF16)
        dgu = jnp.concatenate([dgate, dup], 1)
        acc_d[...] += dot(gt[:, rows], z)
        acc_gu[...] += dot(at[:, rows], dgu)
        if last:
            da[rows] += dot(dgu, wgu[slot], BY_ROWS)

    def pack(b):
        slot = lax.rem(b, slots)
        of_d, of_block = d // n, block // n
        for s in range(n):
            for c in range(2 * block // LANES):
                piece = acc_gu[pl.ds(s * of_d, of_d), pl.ds(c * LANES, LANES)]
                own[slot, s, pl.ds(c * of_d, of_d)] = piece.astype(BF16)
        base = 2 * block // LANES * of_d
        for c in range(d // LANES):
            turned = acc_d[pl.ds(c * LANES, LANES)].T.astype(BF16)
            for s in range(n):
                own[slot, s, pl.ds(base + c * of_block, of_block)] = turned[s * of_block : (s + 1) * of_block]

    def one_block(b, last):
        @pl.when(b + 1 < units)
        def _():
            for copy in weight_loads(b + 1):
                copy.start()

        for copy in weight_loads(b):
            copy.wait()
        acc_gu[...] = jnp.zeros_like(acc_gu)
        acc_d[...] = jnp.zeros_like(acc_d)

        @pl.loop(0, tiles)
        def _(t):
            @pl.when(b == (0 if last else blocks))
            def _():
                for copy in loads(t, a1_hbm, a1t_hbm) if last else loads(t, a0_hbm, a0t_hbm):
                    copy.wait()
                if last:
                    for copy in gradient_loads(t):
                        copy.wait()

            steps(b, t, last)
            if last:

                @pl.when(b == blocks - 1)
                def _():
                    for copy in loads(t, a0_hbm, a0t_hbm):
                        copy.start()

            events(b, t)

        pack(b)

    for t in range(tiles):
        for copy in loads(t, a1_hbm, a1t_hbm) + gradient_loads(t):
            copy.start()
        if t == 0:
            for copy in weight_loads(0):
                copy.start()
    for t in range(min(2, tiles)):
        state_load(t).start()
    barrier = pltpu.get_barrier_semaphore()
    for k in range(1, n):
        pl.semaphore_signal(barrier, 1, device_id={"dp": lax.rem(me + k, n)}, device_id_type=MESH)
    squares[...] = jnp.zeros_like(squares)

    @pl.loop(0, tiles)
    def _(t):
        da[pl.ds(pl.multiple_of(t * tile, tile), tile)] = jnp.zeros((tile, d), F32)

    pl.semaphore_wait(barrier, n - 1)

    @pl.loop(0, blocks)
    def _(b):
        one_block(b, True)

    @pl.loop(0, tiles)
    def _(t):
        state_load(t).wait()
        slot = lax.rem(t, 2)
        part = min(256, tile)

        @pl.loop(0, tile // part)
        def _(i):
            inner = pl.ds(pl.multiple_of(i * part, part), part)
            rows = pl.ds(pl.multiple_of(t * tile + i * part, part), part)
            wide = hbuf[slot, inner].astype(F32)
            scale = scale_of(wide)
            by_a = da[rows].astype(BF16).astype(F32)
            along = jnp.mean(by_a * wide, -1, keepdims=True)
            by_h = (by_a * scale - wide * (scale * scale * scale * along)).astype(BF16)
            out = (g[rows].astype(F32) + by_h.astype(F32)).astype(BF16)
            g[rows] = out
            gt[:, rows] = out.T

        @pl.when(t + 2 < tiles)
        def _():
            state_load(t + 2).start()

    @pl.loop(blocks, units)
    def _(b):
        one_block(b, False)

    for b in range(units, units + 1 + (5 * half // 2) // tiles):
        for t in range(tiles):
            events(b, t)

    def part_copy(k):
        return pltpu.make_async_remote_copy(
            src_ref=squares,
            dst_ref=parts.at[me],
            send_sem=part_send.at[k - 1],
            recv_sem=part_recv.at[k - 1],
            device_id={"dp": lax.rem(me + k, n)},
            device_id_type=MESH,
        )

    for k in range(1, n):
        part_copy(k).start()
    parts[me] = squares[...]
    for k in range(1, n):
        part_copy(k).wait()
    total = parts[0]
    for k in range(1, n):
        total = total + parts[k]
    total_ref[...] = total


def reduced(n, h, a0, a0t, a1, a1t, dy, dyt, w_gate, w_up, w_down):
    tokens, d = h.shape
    ff = w_gate.shape[2]
    block, tile = BLOCK, min(TILE, tokens // 4)
    tiles, blocks, half = tokens // tile, ff // block, n // 2
    shard_rows = 3 * d * block // (n * LANES)
    slots = (5 * half // 2) // tiles + 2
    shard = jax.ShapeDtypeStruct((blocks, shard_rows, LANES), BF16)
    anywhere, vmem = pl.BlockSpec(memory_space=pl.ANY), pl.BlockSpec(memory_space=pltpu.VMEM)
    return pl.pallas_call(
        functools.partial(main_kernel, n),
        in_specs=[anywhere] * 10,
        out_specs=[vmem] * 3,
        out_shape=[shard, shard, jax.ShapeDtypeStruct((8, LANES), F32)],
        scratch_shapes=[
            pltpu.VMEM((tokens, d), BF16),
            pltpu.VMEM((d, tokens), BF16),
            pltpu.VMEM((tokens, d), BF16),
            pltpu.VMEM((d, tokens), BF16),
            pltpu.VMEM((tokens, d), F32),
            pltpu.VMEM((2, tile, d), BF16),
            pltpu.VMEM((2, d, 2 * block), BF16),
            pltpu.VMEM((2, block, d), BF16),
            pltpu.VMEM((d, 2 * block), F32),
            pltpu.VMEM((d, block), F32),
            pltpu.VMEM((slots, n, shard_rows, LANES), BF16),
            pltpu.VMEM((slots, half, shard_rows, LANES), BF16),
            pltpu.VMEM((slots, half, shard_rows, LANES), BF16),
            pltpu.VMEM((8, LANES), F32),
            pltpu.VMEM((n, 8, LANES), F32),
            pltpu.SemaphoreType.DMA((4, tiles)),
            pltpu.SemaphoreType.DMA((3, 2)),
            pltpu.SemaphoreType.DMA((2,)),
            pltpu.SemaphoreType.DMA((2, slots, half)),
            pltpu.SemaphoreType.DMA((2, slots, half)),
            pltpu.SemaphoreType.DMA((n - 1,)),
            pltpu.SemaphoreType.DMA((n - 1,)),
            pltpu.SemaphoreType.REGULAR((2,)),
        ],
        compiler_params=pltpu.CompilerParams(collective_id=0, has_side_effects=True, vmem_limit_bytes=63 << 20),
        cost_estimate=pl.CostEstimate(flops=28 * tokens * d * ff, bytes_accessed=16 * tokens * d, transcendentals=2 * tokens * ff),
        name="reduced",
    )(h, a0, a0t, a1, a1t, dy, dyt, w_gate, w_up, w_down)


def update_kernel(count, n_terms, n_aliased, shards, total_ref, *refs):
    terms, refs = refs[:n_terms], refs[n_terms:]
    w, m, v = refs[:3], refs[3:6], refs[6:9]
    new_w, new_m, new_v = (refs[9 + n_aliased + 3 * i : 12 + n_aliased + 3 * i] for i in range(3))
    factor = jnp.minimum(1.0, 0.5 * lax.rsqrt(jnp.sum(total_ref[...], keepdims=True) / count + 1e-30))

    def apply(units, take):
        of_d, block = w[0].shape[0], w[0].shape[1] // units
        of_block, d = w[2].shape[1:]
        slabs = block // LANES

        def one(i, where, term):
            term = term.astype(F32) * factor
            m_new = 0.9 * m[i][where] + 0.1 * term
            v_new = 0.95 * v[i][where] + 0.05 * term * term
            wide = w[i][where].astype(F32)
            new_m[i][where] = m_new
            new_v[i][where] = v_new
            new_w[i][where] = (wide - 0.02 * (m_new * lax.rsqrt(v_new + 1e-8) + 0.1 * wide)).astype(BF16)

        for j in range(units):
            for i in range(2):
                for c in range(slabs):
                    row = (i * slabs + c) * of_d
                    one(i, (slice(None), pl.ds(j * block + c * LANES, LANES)), take(j, row, of_d))
            for c in range(d // LANES):
                one(2, (j, slice(None), pl.ds(c * LANES, LANES)), take(j, 2 * slabs * of_d + c * of_block, of_block))

    units, rows = terms[0].shape[:2]

    def from_one(ref):
        return lambda j, row, size: ref[j, pl.ds(row, size)]

    def from_halves(j, row, size):
        if row + size <= rows:
            return terms[0][j, pl.ds(row, size)]
        if row >= rows:
            return terms[1][j, pl.ds(row - rows, size)]
        first = rows - row
        return jnp.concatenate([terms[0][j, pl.ds(row, first)], terms[1][j, pl.ds(0, size - first)]], 0)

    full = (2 * w[0].shape[1] * w[0].shape[0] + units * w[2].shape[1] * w[2].shape[2]) // (units * LANES)
    if rows < full:
        apply(units, from_halves)
    elif n_terms == 1:
        apply(units, from_one(terms[0]))
    else:
        for i in range(n_terms):

            @pl.when(pl.program_id(0) == i)
            def _(i=i):
                apply(units, from_one(terms[i]))


def update(layer, shards, terms, total, weights, m, v, so_far):
    _, d, ff = weights[0].shape
    _, blocks, n, of_block, _ = weights[2].shape
    cut = 2
    of_d = d // n
    flat = pl.BlockSpec((None, of_d, ff // cut), lambda i, c, shards: (layer, shards[i], c))
    tall = pl.BlockSpec((None, blocks // cut, None, of_block, d), lambda i, c, shards: (layer, c, shards[i], 0, 0))
    term = pl.BlockSpec((blocks // cut, *terms[0].shape[1:]), lambda i, c, shards: (c, 0, 0))
    arrays = [*weights, *m, *v]
    specs = [flat, flat, tall] * 3
    aliased = list(so_far) if so_far is not None else []
    first = 2 + len(terms) + len(arrays)
    n_shards = shards.shape[0]
    bytes_accessed = n_shards * 20 * 3 * d * ff // n
    return pl.pallas_call(
        functools.partial(update_kernel, 3 * weights[0].size, len(terms), len(aliased)),
        grid_spec=pltpu.PrefetchScalarGridSpec(
            num_scalar_prefetch=1,
            grid=(n_shards, cut),
            in_specs=[pl.BlockSpec((8, LANES), lambda i, c, shards: (0, 0))]
            + [term] * len(terms)
            + specs
            + [pl.BlockSpec(memory_space=pl.ANY)] * len(aliased),
            out_specs=specs,
        ),
        out_shape=[jax.ShapeDtypeStruct(one.shape, one.dtype) for one in arrays],
        input_output_aliases={first + i: i for i in range(len(aliased))},
        compiler_params=pltpu.CompilerParams(vmem_limit_bytes=63 << 20),
        cost_estimate=pl.CostEstimate(flops=300 * bytes_accessed, bytes_accessed=bytes_accessed, transcendentals=0),
        name=f"update_{layer}",
    )(shards, total, *terms, *arrays, *aliased)


def solution(mesh):
    n = mesh.shape["dp"]
    half = n // 2

    def step(x, dy, *arrays):
        weights, m, v = (list(arrays[i : i + 3]) for i in (0, 3, 6))
        h, a0, a0t, a1, a1t, dyt = forward(x, dy, *weights)
        g1, g0, total = reduced(n, h, a0, a0t, a1, a1t, dy[0], dyt, *weights)

        layers, ff, d = weights[2].shape
        split = (layers, ff // BLOCK, n, BLOCK // n, d)
        for group in (weights, m, v):
            group[2] = group[2].reshape(split)
        me = lax.axis_index("dp")

        def sent(value, by):
            return lax.ppermute(value, "dp", [(i, (i + by) % n) for i in range(n)])

        rows = g1.shape[1]
        out = None
        came = {1: [(g1, g1)], 0: [(g0, g0)]}
        for k in range(half + 1):
            for layer in (1, 0):
                if k:
                    rightward, leftward = came[layer][-1]
                    if k == half:
                        rightward, leftward = rightward[:, : rows // 2], leftward[:, rows // 2 :]
                    came[layer].append((sent(rightward, 1), sent(leftward, -1)))
        for k in range(half + 1):
            for layer in (1, 0):
                terms = came[layer][k][:1] if k == 0 else came[layer][k]
                places = [me - k] if k in (0, half) else [me - k, me + k]
                shards = jnp.stack([lax.rem(place + n, n) for place in places]).astype(jnp.int32)
                out = update(layer, shards, terms, total, weights, m, v, out)
        out = list(out)
        for i in (2, 5, 8):
            out[i] = out[i].reshape(layers, ff, d)
        return tuple(out)

    return jax.shard_map(
        step,
        mesh=mesh,
        in_specs=(P(("rep", "dp"), None, None),) * 2 + (P(None, None, None),) * 9,
        out_specs=(P("rep", None, None),) * 9,
        check_vma=False,
    )
```

time: 665 us -> 371 us (0.56); the launches traced: 655 us -> 370 us
  Pallas kernels: 0 us -> 306 us
  matrix products: 299 us -> 0 us
  waiting for transfers between devices: 249 us -> 30.6 us
  other arithmetic: 71.7 us -> 1.87 us
  starting transfers between devices: 0.06 us -> 24.8 us
  between operations: 16.6 us -> 0.94 us
  local copies, waits for them, and re-layouts: 18.2 us -> 6.12 us
    pallas_call x0 -> x12, Pallas kernels: none -> 306 us  [the longest x1 196 us: reduced(): pl.pallas_call(functools.partial(main_kernel, n), in_specs=[anywhere] * 1...]
    dot_general x15 -> x0, matrix products: 299 us -> none  [the longest x5 116 us: layer(): gate = jnp.dot(a, w['w_gate'], preferred_element_type=jnp.float32)]
    psum x1 -> x0, waiting for transfers between devices: 249 us -> none  [step(): summed[number] = [lax.psum(by_w[name], 'dp') for name in NAMES]]
    convert_element_type x2 -> x0, other arithmetic: 43.8 us -> none  [adamw(): return ((w - 0.02 * step).astype(jnp.bfloat16), m, v)]
    ppermute x0 -> x16, waiting for transfers between devices: none -> 30.6 us  [sent(): return lax.ppermute(value, 'dp', [(i, (i + by) % n) for i in range(n)])]
    ppermute x0 -> x16, starting transfers between devices: none -> 24.8 us  [sent(): return lax.ppermute(value, 'dp', [(i, (i + by) % n) for i in range(n)])]
    unnamed x38 -> x4, local copies, waits for them, and re-layouts: 18.2 us -> 0.01 us
    reduce_sum x4 -> x0, other arithmetic: 15.9 us -> none  [the longest x3 12.3 us: step(): jnp.sum(g * g)]
  transfers between devices with their start and end apart: 1 -> 16, of which waited for: 1 -> 4; matrix products, arithmetic and copies ran while one was open for 0% -> 2% of each run, Pallas kernels for 0% -> 18%
where the time goes in v1:
time: 371 us; the launch traced here: 370 us
  Pallas kernels  306 us (82%)
  waiting for transfers between devices  30.6 us (8%)
  starting transfers between devices  24.8 us (7%)
  local copies, waits for them, and re-layouts  6.12 us (2%)
    pallas_call x1, Pallas kernels, reduced(): pl.pallas_call(functools.partial(main_kernel, n), in_specs=[anywhere] * 1...  196 us
    pallas_call x10, Pallas kernels, update(): pl.pallas_call(functools.partial(update_kernel, 3 * weights[0].size, len(...  70.7 us
    pallas_call x1, Pallas kernels, forward(): pl.pallas_call(forward_kernel, grid=(tokens // tile,), in_specs=[given, g...  39.6 us
    ppermute x16, waiting for transfers between devices, sent(): return lax.ppermute(value, 'dp', [(i, (i + by) % n) for i in range(n)])  30.6 us
    ppermute x16, starting transfers between devices, sent(): return lax.ppermute(value, 'dp', [(i, (i + by) % n) for i in range(n)])  24.8 us
  transfers between devices with their start and end apart: 16, of which 4 were waited for; matrix products, arithmetic and copies ran while one was open for 2% of the time, Pallas kernels for 18%

profile of v1, /device:TPU:28, one launch (start us, length us, event | category | flops | bytes accessed | tf_op | source)
XLA Modules:
  0.0 370.5 jit_solution(6772933774082308067)
XLA Ops:
  0.6 39.6 %forward.1 = (bf16[4096,640]{1,0:T(8,128)(2,1)}, bf16[4096,640]{1,0:T(8,128)(2,1)}, bf16[640,4096]{1,0:T(8,128)(2,1)}, bf16[4096,640]{1,0:T(8,128)(2,1)}, bf16[6...) custom-call(bf16[1,4096,640]{2,1,0:T(8,128)(2,1)} %x_ref.1, bf16[1,4096,640]{2,1,0:T(8,128)(2,1)} %dy_ref.1, ...), custom_call_target="tpu_custom_call" | custom-call | flops 24159191040 | bytes 41943040 | tf_op jit(solution)/shard_map/forward/pallas_call | solution.py:54
  40.3 195.8 %reduced.1 = (bf16[6,480,128]{2,1,0:T(8,128)(2,1)}, bf16[6,480,128]{2,1,0:T(8,128)(2,1)}, f32[8,128]{1,0:T(8,128)}) custom-call(bf16[4096,640]{1,0:T(8,128)(2,1)} %get-tuple-element.108.h_hbm, bf16[4096,640]{1,0:T(8,128)(2,1)} %get-tuple-element.109.a0_hbm, bf16[640,4096]{1,0:T(8,128)(2,1)} %get-tuple-element.110.a0t_hbm, ...), custom_call_target="tpu_custom_call" | custom-call | flops 112742891520 | bytes 41943040 | tf_op jit(solution)/shard_map/reduced/pallas_call | solution.py:339
  236.1 2.1 collective-permute-start.12
  238.2 0.2 collective-permute-start.8
  238.4 0.9 collective-permute-start
  239.3 2.4 collective-permute-start.4
  241.6 0.6 pad_add_fusion.2.shards
  242.3 0.6 pad_add_fusion.1.shards
  242.9 0.7 pad_add_fusion.shards
  243.5 4.4 %update_1.5 = (bf16[2,640,1536]{2,1,0:T(8,128)(2,1)}, bf16[2,640,1536]{2,1,0:T(8,128)(2,1)}, bf16[2,6,8,32,640]{4,3,2,1,0:T(8,128)(2,1)}, f32[2,640,1536]{2,1,0:...) custom-call(s32[1]{0:T(128)} %bitcast.11.shards, ...), custom_call_target="tpu_custom_call" | custom-call | flops 2211840000 | bytes 7372800 | tf_op jit(solution)/shard_map/update_1/pallas_call | solution.py:443
  247.9 4.4 %update_0.5 = (bf16[2,640,1536]{2,1,0:T(8,128)(2,1)}, bf16[2,640,1536]{2,1,0:T(8,128)(2,1)}, bf16[2,6,8,32,640]{4,3,2,1,0:T(8,128)(2,1)}, f32[2,640,1536]{2,1,0:...) custom-call(s32[1]{0:T(128)} %bitcast.11.shards, ...), custom_call_target="tpu_custom_call", output_to_operand_aliasing={{0}: (12, {}), {1}: (13, {}), {2}: (14, {}), {3}: (15, {}),... | custom-call | flops 2211840000 | bytes 7372800 | tf_op jit(solution)/shard_map/update_0/pallas_call | solution.py:443
  252.3 3.4 collective-permute-done.12.refs_1_
  255.8 3.0 collective-permute-start.13
  258.7 0.0 collective-permute-done.8.refs_0_
  258.8 0.0 collective-permute-start.9
  258.8 15.8 %collective-permute-done.refs_0_ = bf16[6,480,128]{2,1,0:T(8,128)(2,1)} collective-permute-done((bf16[6,480,128]{2,1,0:T(8,128)(2,1)}, bf16[6,480,128]{2,1,0:T(8,128)(2,1)}, u32[]{:S(2)}, u32[]{:S(2)}) %collective-permute-start) | collective-permute-done | bytes 737312 | tf_op jit(solution)/shard_map/ppermute | solution.py:478
  274.5 0.0 collective-permute-start.1
  274.5 0.0 collective-permute-done.4.refs_1_
  274.6 3.2 collective-permute-start.5
  277.8 8.8 %update_1.6 = (bf16[2,640,1536]{2,1,0:T(8,128)(2,1)}, bf16[2,640,1536]{2,1,0:T(8,128)(2,1)}, bf16[2,6,8,32,640]{4,3,2,1,0:T(8,128)(2,1)}, f32[2,640,1536]{2,1,0:...) custom-call(s32[2]{0:T(128)} %pad_add_fusion.2.shards, ...), custom_call_target="tpu_custom_call", output_to_operand_aliasing={{0}: (13, {}), {1}: (14, {}), {2}: (15, {}), {3}: (16, {}),... | custom-call | flops 4423680000 | bytes 14745600 | tf_op jit(solution)/shard_map/update_1/pallas_call | solution.py:443
  286.6 8.9 %update_0.6 = (bf16[2,640,1536]{2,1,0:T(8,128)(2,1)}, bf16[2,640,1536]{2,1,0:T(8,128)(2,1)}, bf16[2,6,8,32,640]{4,3,2,1,0:T(8,128)(2,1)}, f32[2,640,1536]{2,1,0:...) custom-call(s32[2]{0:T(128)} %pad_add_fusion.2.shards, ...), custom_call_target="tpu_custom_call", output_to_operand_aliasing={{0}: (13, {}), {1}: (14, {}), {2}: (15, {}), {3}: (16, {}),... | custom-call | flops 4423680000 | bytes 14745600 | tf_op jit(solution)/shard_map/update_0/pallas_call | solution.py:443
  295.4 0.0 collective-permute-done.9.refs_0_
  295.4 0.1 collective-permute-start.10
  295.6 0.0 collective-permute-done.13.refs_1_
  295.6 3.2 collective-permute-start.14
  298.8 7.4 %collective-permute-done.1.refs_0_ = bf16[6,480,128]{2,1,0:T(8,128)(2,1)} collective-permute-done((bf16[6,480,128]{2,1,0:T(8,128)(2,1)}, bf16[6,480,128]{2,1,0:T(8,128)(2,1)}, u32[]{:S(2)}, u32[]{:S(2)}) %collective-permute-start.1) | collective-permute-done | bytes 737312 | tf_op jit(solution)/shard_map/ppermute | solution.py:478
  306.1 0.0 collective-permute-start.2
  306.1 0.0 collective-permute-done.5.refs_1_
  306.2 3.2 collective-permute-start.6
  309.4 8.8 %update_1.7 = (bf16[2,640,1536]{2,1,0:T(8,128)(2,1)}, bf16[2,640,1536]{2,1,0:T(8,128)(2,1)}, bf16[2,6,8,32,640]{4,3,2,1,0:T(8,128)(2,1)}, f32[2,640,1536]{2,1,0:...) custom-call(s32[2]{0:T(128)} %pad_add_fusion.1.shards, ...), custom_call_target="tpu_custom_call", output_to_operand_aliasing={{0}: (13, {}), {1}: (14, {}), {2}: (15, {}), {3}: (16, {}),... | custom-call | flops 4423680000 | bytes 14745600 | tf_op jit(solution)/shard_map/update_1/pallas_call | solution.py:443
  318.2 8.9 %update_0.7 = (bf16[2,640,1536]{2,1,0:T(8,128)(2,1)}, bf16[2,640,1536]{2,1,0:T(8,128)(2,1)}, bf16[2,6,8,32,640]{4,3,2,1,0:T(8,128)(2,1)}, f32[2,640,1536]{2,1,0:...) custom-call(s32[2]{0:T(128)} %pad_add_fusion.1.shards, ...), custom_call_target="tpu_custom_call", output_to_operand_aliasing={{0}: (13, {}), {1}: (14, {}), {2}: (15, {}), {3}: (16, {}),... | custom-call | flops 4423680000 | bytes 14745600 | tf_op jit(solution)/shard_map/update_0/pallas_call | solution.py:443
  327.0 0.0 collective-permute-done.10.refs_0_
  327.0 1.8 slice.18
  328.8 0.0 collective-permute-start.11
  328.8 1.7 slice.19
  330.6 3.2 collective-permute-start.15
  333.8 4.0 %collective-permute-done.2.refs_0_ = bf16[6,480,128]{2,1,0:T(8,128)(2,1)S(1)} collective-permute-done((bf16[6,480,128]{2,1,0:T(8,128)(2,1)}, bf16[6,480,128]{2,1,0:T(8,128)(2,1)S(1)}, u32[]{:S(2)}, u32[]{:S(2)}) %collective-permute-start.2) | collective-permute-done | bytes 737312 | tf_op jit(solution)/shard_map/ppermute | solution.py:478
  337.7 0.8 slice.16
  338.6 0.0 collective-permute-start.3
  338.6 0.0 collective-permute-done.6.refs_1_
  338.6 1.8 slice.17
  340.4 3.2 collective-permute-start.7
  343.6 8.8 %update_1.8 = (bf16[2,640,1536]{2,1,0:T(8,128)(2,1)}, bf16[2,640,1536]{2,1,0:T(8,128)(2,1)}, bf16[2,6,8,32,640]{4,3,2,1,0:T(8,128)(2,1)}, f32[2,640,1536]{2,1,0:...) custom-call(s32[2]{0:T(128)} %pad_add_fusion.shards, ...), custom_call_target="tpu_custom_call", output_to_operand_aliasing={{0}: (13, {}), {1}: (14, {}), {2}: (15, {}), {3}: (16, {}),... | custom-call | flops 4423680000 | bytes 14745600 | tf_op jit(solution)/shard_map/update_1/pallas_call | solution.py:443
  352.4 8.9 %update_0.8 = (bf16[2,640,1536]{2,1,0:T(8,128)(2,1)}, bf16[2,640,1536]{2,1,0:T(8,128)(2,1)}, bf16[2,6,8,32,640]{4,3,2,1,0:T(8,128)(2,1)}, f32[2,640,1536]{2,1,0:...) custom-call(s32[2]{0:T(128)} %pad_add_fusion.shards, ...), custom_call_target="tpu_custom_call", output_to_operand_aliasing={{0}: (13, {}), {1}: (14, {}), {2}: (15, {}), {3}: (16, {}),... | custom-call | flops 4423680000 | bytes 14745600 | tf_op jit(solution)/shard_map/update_0/pallas_call | solution.py:443
  361.2 0.0 collective-permute-done.11.refs_0_
  361.3 4.5 %update_1.9 = (bf16[2,640,1536]{2,1,0:T(8,128)(2,1)}, bf16[2,640,1536]{2,1,0:T(8,128)(2,1)}, bf16[2,6,8,32,640]{4,3,2,1,0:T(8,128)(2,1)}, f32[2,640,1536]{2,1,0:...) custom-call(s32[1]{0:T(128)} %bitcast.shards, ...), custom_call_target="tpu_custom_call", output_to_operand_aliasing={{0}: (13, {}), {1}: (14, {}), {2}: (15, {}), {3}: (16, {}),... | custom-call | flops 2211840000 | bytes 7372800 | tf_op jit(solution)/shard_map/update_1/pallas_call | solution.py:443
  365.8 0.0 collective-permute-done.3.refs_0_
  365.8 4.5 %update_0.9 = (bf16[2,640,1536]{2,1,0:T(8,128)(2,1)}, bf16[2,640,1536]{2,1,0:T(8,128)(2,1)}, bf16[2,6,8,32,640]{4,3,2,1,0:T(8,128)(2,1)}, f32[2,640,1536]{2,1,0:...) custom-call(s32[1]{0:T(128)} %bitcast.shards, ...), custom_call_target="tpu_custom_call", output_to_operand_aliasing={{0}: (13, {}), {1}: (14, {}), {2}: (15, {}), {3}: (16, {}),... | custom-call | flops 2211840000 | bytes 7372800 | tf_op jit(solution)/shard_map/update_0/pallas_call | solution.py:443
  (7 shorter events, 0.0 us)
Async XLA Ops:
  236.1 19.6 %collective-permute-start.12 = (bf16[6,480,128]{2,1,0:T(8,128)(2,1)}, bf16[6,480,128]{2,1,0:T(8,128)(2,1)S(1)}, u32[]{:S(2)}, u32[]{:S(2)}) collective-permute-start(bf16[6,480,128]{2,1,0:T(8,128)(2,1)} %get-tuple-element.116.refs_0_), channel_id=1, source_target_pairs={{0,7},{1,0},{2,1},{3,2},{4,3},{5,4},{6,5},{7,6},{8,15},{9,8},{10,9... | collective-permute-start | bytes 2211848 | tf_op jit(solution)/shard_map/ppermute | solution.py:478
  238.2 20.6 %collective-permute-start.8 = (bf16[6,480,128]{2,1,0:T(8,128)(2,1)}, bf16[6,480,128]{2,1,0:T(8,128)(2,1)}, u32[]{:S(2)}, u32[]{:S(2)}) collective-permute-start(bf16[6,480,128]{2,1,0:T(8,128)(2,1)} %get-tuple-element.116.refs_0_), channel_id=1, source_target_pairs={{0,1},{1,2},{2,3},{3,4},{4,5},{5,6},{6,7},{7,0},{8,9},{9,10},{10,1... | collective-permute-start | bytes 2211848 | tf_op jit(solution)/shard_map/ppermute | solution.py:478
  238.4 36.1 %collective-permute-start = (bf16[6,480,128]{2,1,0:T(8,128)(2,1)}, bf16[6,480,128]{2,1,0:T(8,128)(2,1)}, u32[]{:S(2)}, u32[]{:S(2)}) collective-permute-start(bf16[6,480,128]{2,1,0:T(8,128)(2,1)} %get-tuple-element.115.refs_0_), channel_id=1, source_target_pairs={{0,1},{1,2},{2,3},{3,4},{4,5},{5,6},{6,7},{7,0},{8,9},{9,10},{10,1... | collective-permute-start | bytes 2211848 | tf_op jit(solution)/shard_map/ppermute | solution.py:478
  239.3 35.3 %collective-permute-start.4 = (bf16[6,480,128]{2,1,0:T(8,128)(2,1)}, bf16[6,480,128]{2,1,0:T(8,128)(2,1)}, u32[]{:S(2)}, u32[]{:S(2)}) collective-permute-start(bf16[6,480,128]{2,1,0:T(8,128)(2,1)} %get-tuple-element.115.refs_0_), channel_id=1, source_target_pairs={{0,7},{1,0},{2,1},{3,2},{4,3},{5,4},{6,5},{7,6},{8,15},{9,8},{10,9... | collective-permute-start | bytes 2211848 | tf_op jit(solution)/shard_map/ppermute | solution.py:478
  255.7 22.0 %copy-start.1 = (bf16[6,480,128]{2,1,0:T(8,128)(2,1)}, bf16[6,480,128]{2,1,0:T(8,128)(2,1)S(1)}, u32[]{:S(2)}) copy-start(bf16[6,480,128]{2,1,0:T(8,128)(2,1)S(1)} %collective-permute-done.12.refs_1_) | copy-start | bytes 2211844
  255.8 39.8 %collective-permute-start.13 = (bf16[6,480,128]{2,1,0:T(8,128)(2,1)S(1)}, bf16[6,480,128]{2,1,0:T(8,128)(2,1)}, u32[]{:S(2)}, u32[]{:S(2)}) collective-permute-start(bf16[6,480,128]{2,1,0:T(8,128)(2,1)S(1)} %collective-permute-done.12.refs_1_), channel_id=1, source_target_pairs={{0,7},{1,0},{2,1},{3,2},{4,3},{5,4},{6,5},{7,6},{8,15},{9,8},{10,9... | collective-permute-start | bytes 2211848 | tf_op jit(solution)/shard_map/ppermute | solution.py:478
  258.8 36.7 %collective-permute-start.9 = (bf16[6,480,128]{2,1,0:T(8,128)(2,1)}, bf16[6,480,128]{2,1,0:T(8,128)(2,1)}, u32[]{:S(2)}, u32[]{:S(2)}) collective-permute-start(bf16[6,480,128]{2,1,0:T(8,128)(2,1)} %collective-permute-done.8.refs_0_), channel_id=1, source_target_pairs={{0,1},{1,2},{2,3},{3,4},{4,5},{5,6},{6,7},{7,0},{8,9},{9,10},{10,1... | collective-permute-start | bytes 2211848 | tf_op jit(solution)/shard_map/ppermute | solution.py:478
  274.5 31.6 %collective-permute-start.1 = (bf16[6,480,128]{2,1,0:T(8,128)(2,1)}, bf16[6,480,128]{2,1,0:T(8,128)(2,1)}, u32[]{:S(2)}, u32[]{:S(2)}) collective-permute-start(bf16[6,480,128]{2,1,0:T(8,128)(2,1)} %collective-permute-done.refs_0_), channel_id=1, source_target_pairs={{0,1},{1,2},{2,3},{3,4},{4,5},{5,6},{6,7},{7,0},{8,9},{9,10},{10,1... | collective-permute-start | bytes 2211848 | tf_op jit(solution)/shard_map/ppermute | solution.py:478
  274.6 31.6 %collective-permute-start.5 = (bf16[6,480,128]{2,1,0:T(8,128)(2,1)}, bf16[6,480,128]{2,1,0:T(8,128)(2,1)}, u32[]{:S(2)}, u32[]{:S(2)}) collective-permute-start(bf16[6,480,128]{2,1,0:T(8,128)(2,1)} %collective-permute-done.4.refs_1_), channel_id=1, source_target_pairs={{0,7},{1,0},{2,1},{3,2},{4,3},{5,4},{6,5},{7,6},{8,15},{9,8},{10,9... | collective-permute-start | bytes 2211848 | tf_op jit(solution)/shard_map/ppermute | solution.py:478
  295.4 31.6 %collective-permute-start.10 = (bf16[6,480,128]{2,1,0:T(8,128)(2,1)}, bf16[6,480,128]{2,1,0:T(8,128)(2,1)}, u32[]{:S(2)}, u32[]{:S(2)}) collective-permute-start(bf16[6,480,128]{2,1,0:T(8,128)(2,1)} %collective-permute-done.9.refs_0_), channel_id=1, source_target_pairs={{0,1},{1,2},{2,3},{3,4},{4,5},{5,6},{6,7},{7,0},{8,9},{9,10},{10,1... | collective-permute-start | bytes 2211848 | tf_op jit(solution)/shard_map/ppermute | solution.py:478
  295.6 33.2 %collective-permute-start.14 = (bf16[6,480,128]{2,1,0:T(8,128)(2,1)}, bf16[6,480,128]{2,1,0:T(8,128)(2,1)}, u32[]{:S(2)}, u32[]{:S(2)}) collective-permute-start(bf16[6,480,128]{2,1,0:T(8,128)(2,1)} %collective-permute-done.13.refs_1_), channel_id=1, source_target_pairs={{0,7},{1,0},{2,1},{3,2},{4,3},{5,4},{6,5},{7,6},{8,15},{9,8},{10,9... | collective-permute-start | bytes 2211848 | tf_op jit(solution)/shard_map/ppermute | solution.py:478
  306.1 31.6 %collective-permute-start.2 = (bf16[6,480,128]{2,1,0:T(8,128)(2,1)}, bf16[6,480,128]{2,1,0:T(8,128)(2,1)S(1)}, u32[]{:S(2)}, u32[]{:S(2)}) collective-permute-start(bf16[6,480,128]{2,1,0:T(8,128)(2,1)} %collective-permute-done.1.refs_0_), channel_id=1, source_target_pairs={{0,1},{1,2},{2,3},{3,4},{4,5},{5,6},{6,7},{7,0},{8,9},{9,10},{10,1... | collective-permute-start | bytes 2211848 | tf_op jit(solution)/shard_map/ppermute | solution.py:478
  306.2 32.4 %collective-permute-start.6 = (bf16[6,480,128]{2,1,0:T(8,128)(2,1)}, bf16[6,480,128]{2,1,0:T(8,128)(2,1)}, u32[]{:S(2)}, u32[]{:S(2)}) collective-permute-start(bf16[6,480,128]{2,1,0:T(8,128)(2,1)} %collective-permute-done.5.refs_1_), channel_id=1, source_target_pairs={{0,7},{1,0},{2,1},{3,2},{4,3},{5,4},{6,5},{7,6},{8,15},{9,8},{10,9... | collective-permute-start | bytes 2211848 | tf_op jit(solution)/shard_map/ppermute | solution.py:478
  328.8 32.4 %collective-permute-start.11 = (bf16[6,240,128]{2,1,0:T(8,128)(2,1)}, bf16[6,240,128]{2,1,0:T(8,128)(2,1)}, u32[]{:S(2)}, u32[]{:S(2)}) collective-permute-start(bf16[6,240,128]{2,1,0:T(8,128)(2,1)} %slice.18), channel_id=1, source_target_pairs={{0,1},{1,2},{2,3},{3,4},{4,5},{5,6},{6,7},{7,0},{8,9},{9,10},{10,1... | collective-permute-start | bytes 1105928 | tf_op jit(solution)/shard_map/ppermute | solution.py:478
  330.6 30.7 %collective-permute-start.15 = (bf16[6,240,128]{2,1,0:T(8,128)(2,1)}, bf16[6,240,128]{2,1,0:T(8,128)(2,1)}, u32[]{:S(2)}, u32[]{:S(2)}) collective-permute-start(bf16[6,240,128]{2,1,0:T(8,128)(2,1)} %slice.19), channel_id=1, source_target_pairs={{0,7},{1,0},{2,1},{3,2},{4,3},{5,4},{6,5},{7,6},{8,15},{9,8},{10,9... | collective-permute-start | bytes 1105928 | tf_op jit(solution)/shard_map/ppermute | solution.py:478
  337.7 14.6 %copy-start = (bf16[6,480,128]{2,1,0:T(8,128)(2,1)}, bf16[6,480,128]{2,1,0:T(8,128)(2,1)S(1)}, u32[]{:S(2)}) copy-start(bf16[6,480,128]{2,1,0:T(8,128)(2,1)S(1)} %collective-permute-done.2.refs_0_) | copy-start | bytes 2211844
  338.6 27.2 %collective-permute-start.3 = (bf16[6,240,128]{2,1,0:T(8,128)(2,1)}, bf16[6,240,128]{2,1,0:T(8,128)(2,1)}, u32[]{:S(2)}, u32[]{:S(2)}) collective-permute-start(bf16[6,240,128]{2,1,0:T(8,128)(2,1)} %slice.16), channel_id=1, source_target_pairs={{0,1},{1,2},{2,3},{3,4},{4,5},{5,6},{6,7},{7,0},{8,9},{9,10},{10,1... | collective-permute-start | bytes 1105928 | tf_op jit(solution)/shard_map/ppermute | solution.py:478
  340.4 25.4 %collective-permute-start.7 = (bf16[6,240,128]{2,1,0:T(8,128)(2,1)}, bf16[6,240,128]{2,1,0:T(8,128)(2,1)}, u32[]{:S(2)}, u32[]{:S(2)}) collective-permute-start(bf16[6,240,128]{2,1,0:T(8,128)(2,1)} %slice.17), channel_id=1, source_target_pairs={{0,7},{1,0},{2,1},{3,2},{4,3},{5,4},{6,5},{7,6},{8,15},{9,8},{10,9... | collective-permute-start | bytes 1105928 | tf_op jit(solution)/shard_map/ppermute | solution.py:478

commit v2 on v1

v2 whole, which is shorter than its diff:
```python
import functools

import jax
import jax.numpy as jnp
from jax import lax
from jax.experimental import pallas as pl
from jax.experimental.pallas import tpu as pltpu
from jax.sharding import PartitionSpec as P

BF16, F32 = jnp.bfloat16, jnp.float32
MESH = pl.DeviceIdType.MESH
LANES = 128
BLOCK = 256
PLAIN, BY_ROWS = ((1,), (0,)), ((1,), (1,))


def dot(a, b, contract=PLAIN):
    return lax.dot_general(a, b, (contract, ((), ())), preferred_element_type=F32)


def scale_of(wide):
    return lax.rsqrt(jnp.mean(wide * wide, -1, keepdims=True) + 1e-6)


def normed(h):
    wide = h.astype(F32)
    return (wide * scale_of(wide)).astype(BF16)


def when(condition, do):
    if isinstance(condition, bool):
        if condition:
            do()
    else:
        pl.when(condition)(do)


def at_ring(e):
    return 5 * e // 2


def at_gather(e, half):
    return at_ring(half) + (3 + 4 * e if e else 0)


def main_kernel(
    n, x_hbm, dy_hbm, wg_hbm, wu_hbm, wd_hbm,
    g1_hbm, g0a_ref, g0b_ref, total_ref, a0_hbm, a0t_hbm, h_hbm, dgu_hbm,
    a, at, g, gt, wide, wgu, wd, acc_gu, acc_d, dgu, own, from_left, from_right, kept, squares, parts,
    x_sem, dy_sem, wide_sem, w_sem, dgu_sem, in_sem, send_sem, recv_sem, there_sem, here_sem, kept_sem, part_send, part_recv, credit,
):
    tokens, d = a.shape
    ff = wg_hbm.shape[2]
    block = wd.shape[1]
    blocks = ff // block
    units, half = 2 * blocks, n // 2
    tile = dgu.shape[1]
    tiles = tokens // tile
    small = tile // 2
    smalls = tokens // small
    slots, shard_rows = own.shape[0], own.shape[2]
    me = lax.axis_index("dp")
    right, left = lax.rem(me + 1, n), lax.rem(me + n - 1, n)

    def span(i, size):
        return pl.ds(i * size, size) if isinstance(i, int) else pl.ds(pl.multiple_of(i * size, size), size)

    def dy_load(i):
        return pltpu.make_async_copy(dy_hbm.at[0, span(i, small)], g.at[span(i, small)], dy_sem.at[i])

    def wide_loads(layer):
        return [
            pltpu.make_async_copy(wg_hbm.at[layer], wide.at[:, pl.ds(0, ff)], wide_sem.at[0]),
            pltpu.make_async_copy(wu_hbm.at[layer], wide.at[:, pl.ds(ff, ff)], wide_sem.at[1]),
        ]

    def a0_loads(t):
        return [
            pltpu.make_async_copy(a0_hbm.at[span(t, tile)], a.at[span(t, tile)], in_sem.at[0, t]),
            pltpu.make_async_copy(a0t_hbm.at[:, span(t, tile)], at.at[:, span(t, tile)], in_sem.at[1, t]),
        ]

    def weight_loads(b):
        last = jnp.int32(b < blocks) if isinstance(b, int) else (b < blocks).astype(jnp.int32)
        columns = pl.ds(pl.multiple_of((b - blocks * (1 - last)) * block, block), block)
        slot = lax.rem(b, 2)
        return [
            pltpu.make_async_copy(wg_hbm.at[last, :, columns], wgu.at[slot, :, pl.ds(0, block)], w_sem.at[0, slot]),
            pltpu.make_async_copy(wu_hbm.at[last, :, columns], wgu.at[slot, :, pl.ds(block, block)], w_sem.at[1, slot]),
            pltpu.make_async_copy(wd_hbm.at[last, columns, :], wd.at[slot], w_sem.at[2, slot]),
        ]

    def ring_copy(u, k, way):
        slot = lax.rem(u, slots)
        ahead = half - k if way == 0 else n - half + k
        shard = lax.rem(me + ahead, n)
        rows = pl.ds(0, shard_rows)
        if k == 0:
            rows = pl.ds(way * (shard_rows // 2), shard_rows // 2)
        return pltpu.make_async_remote_copy(
            src_ref=own.at[slot, shard, rows],
            dst_ref=(from_left, from_right)[way].at[slot, k, rows],
            send_sem=send_sem.at[way, slot, k],
            recv_sem=recv_sem.at[way, slot, k],
            device_id={"dp": (right, left)[way]},
            device_id_type=MESH,
        )

    def ring_event(u, e, last):
        slot = lax.rem(u, slots)
        if e == 0:

            def take():
                pl.semaphore_wait(credit.at[0], 1)
                pl.semaphore_wait(credit.at[1], 1)

            when(u >= slots, take)
        else:
            for way in (0, 1):
                ring_copy(u, e - 1, way).wait()
        if 0 < e < half:
            for way in (0, 1):
                shard = lax.rem(me + (half - e if way == 0 else n - half + e), n)
                rows = pl.ds(0, shard_rows) if e > 1 else pl.ds(way * (shard_rows // 2), shard_rows // 2)
                came = (from_left, from_right)[way][slot, e - 1, rows].astype(F32)
                own[slot, shard, rows] = (own[slot, shard, rows].astype(F32) + came).astype(BF16)
        if e < half:
            for way in (0, 1):
                ring_copy(u, e, way).start()
        else:
            came = from_left[slot, e - 1].astype(F32) + from_right[slot, e - 1].astype(F32)
            done = (own[slot, me].astype(F32) + came).astype(BF16)
            if last:
                kept[u] = done
            else:

                def keep(ref, place):
                    def do():
                        ref[place] = done

                    return do

                cut = blocks + blocks // 2
                when(u < cut, keep(g0a_ref, jnp.minimum(u - blocks, blocks // 2 - 1)))
                when(u >= cut, keep(g0b_ref, jnp.maximum(u - cut, 0)))
            exact = done.astype(F32)
            squares[...] += jnp.sum((exact * exact).reshape(shard_rows // 8, 8, LANES), 0)

            def give():
                pl.semaphore_signal(credit.at[0], 1, device_id={"dp": left}, device_id_type=MESH)
                pl.semaphore_signal(credit.at[1], 1, device_id={"dp": right}, device_id_type=MESH)

            when(u < units - slots, give)

    def gather_copy(u, k, way):
        rows = pl.ds(0, shard_rows)
        if k == half - 1:
            rows = pl.ds(way * (shard_rows // 2), shard_rows // 2)
        place = (k, n - k)[way]
        after = (k + 1, n - k - 1)[way]
        return pltpu.make_async_remote_copy(
            src_ref=kept.at[u, rows] if k == 0 else g1_hbm.at[place, u, rows],
            dst_ref=g1_hbm.at[after, u, rows],
            send_sem=there_sem.at[way, u, k],
            recv_sem=here_sem.at[way, u, k],
            device_id={"dp": (right, left)[way]},
            device_id_type=MESH,
        )

    def kept_copy(u):
        return pltpu.make_async_copy(kept.at[u], g1_hbm.at[0, u], kept_sem.at[u])

    def gather_event(u, e):
        if e == 0:
            kept_copy(u).start()
        else:
            for way in (0, 1):
                gather_copy(u, e - 1, way).wait()
        if e < half:
            for way in (0, 1):
                gather_copy(u, e, way).start()
        else:
            kept_copy(u).wait()

    between = tiles * blocks
    second = between + smalls

    def events(now, phase):
        for last in (True, False):
            base, first = (0, 0) if last else (second, blocks)
            jobs = [(at_ring(e), functools.partial(ring_event, e=e, last=last)) for e in range(half + 1)]
            if last:
                jobs += [(at_gather(e, half), functools.partial(gather_event, e=e)) for e in range(half + 1)]
            for lag, job in jobs:
                earliest, latest = base + tiles + lag, base + tiles * blocks + lag
                lo, hi = ((0, between), (between, second), (second, second + between), (second + between, 1 << 30))[phase]
                if latest < lo or earliest >= hi:
                    continue
                since = now - earliest
                if isinstance(now, int):
                    if since >= 0 and since % tiles == 0 and since // tiles < blocks:
                        job(first + since // tiles)
                else:

                    @pl.when((since >= 0) & (lax.rem(since + 64 * tiles, tiles) == 0) & (since < tiles * blocks))
                    def _(job=job, since=since, first=first):
                        job(first + lax.div(since, tiles))

    def forward(x_in, a0_out, a0t_out, h_out, wd0):
        def x_load(i, slot):
            return pltpu.make_async_copy(x_hbm.at[0, span(i, small)], x_in.at[slot], x_sem.at[slot])

        def stores(i, slot):
            return [
                pltpu.make_async_copy(a0_out.at[slot], a0_hbm.at[span(i, small)], in_sem.at[0, slot]),
                pltpu.make_async_copy(a0t_out.at[slot], a0t_hbm.at[:, span(i, small)], in_sem.at[1, slot]),
                pltpu.make_async_copy(h_out.at[slot], h_hbm.at[span(i, small)], dgu_sem.at[0, slot]),
            ]

        wd0_load = pltpu.make_async_copy(wd_hbm.at[0], wd0, wide_sem.at[2])
        x_load(0, 0).start()
        for copy in wide_loads(0):
            copy.start()
        wd0_load.start()
        for i in range(smalls):
            dy_load(i).start()
        for copy in weight_loads(0):
            copy.start()
        barrier = pltpu.get_barrier_semaphore()
        for k in range(1, n):
            pl.semaphore_signal(barrier, 1, device_id={"dp": lax.rem(me + k, n)}, device_id_type=MESH)
        squares[...] = jnp.zeros_like(squares)
        for copy in wide_loads(0):
            copy.wait()
        wd0_load.wait()

        @pl.loop(0, smalls)
        def _(i):
            slot = lax.rem(i, 2)
            x_load(i, slot).wait()

            @pl.when(i + 1 < smalls)
            def _():
                x_load(i + 1, 1 - slot).start()

            dy_load(i).wait()

            @pl.when(i >= 2)
            def _():
                for copy in stores(i - 2, slot):
                    copy.wait()

            gt[:, span(i, small)] = g[span(i, small)].T
            part = small // 2
            for c in range(2):
                here = pl.ds(c * part, part)
                rows = pl.ds(pl.multiple_of(i * small + c * part, part), part)
                x = x_in[slot, here]
                a0 = normed(x)
                a0_out[slot, here] = a0
                a0t_out[slot, :, here] = a0.T
                gate = dot(a0, wide[:, :ff])
                up = dot(a0, wide[:, ff:])
                z = (gate * jax.nn.sigmoid(gate) * up).astype(BF16)
                h = (x.astype(F32) + dot(z, wd0[...]).astype(BF16).astype(F32)).astype(BF16)
                h_out[slot, here] = h
                a1 = normed(h)
                a[rows] = a1
                at[:, rows] = a1.T
            for copy in stores(i, slot):
                copy.start()

        for i in range(max(smalls - 2, 0), smalls):
            for copy in stores(i, i % 2):
                copy.wait()
        pl.semaphore_wait(barrier, n - 1)

    def dgu_stores(b, t, slot):
        return [
            pltpu.make_async_copy(
                dgu.at[slot, :, pl.ds(i * block, block)],
                dgu_hbm.at[span(t, tile), pl.ds(pl.multiple_of(i * ff + b * block, block), block)],
                dgu_sem.at[i, slot],
            )
            for i in (0, 1)
        ]

    def steps(b, t, last):
        rows = span(t, tile)
        slot = lax.rem(b, 2)
        gu = dot(a[rows], wgu[slot])
        dz = dot(g[rows], wd[slot], BY_ROWS).astype(BF16).astype(F32)
        gate, up = gu[:, :block], gu[:, block:]
        s = jax.nn.sigmoid(gate)
        silu = gate * s
        z = (silu * up).astype(BF16)
        dgate = (dz * up * (s + silu * (1 - s))).astype(BF16)
        dup = (dz * silu).astype(BF16)
        both = jnp.concatenate([dgate, dup], 1)
        if last:
            dgu[lax.rem(t, 2)] = both
        acc_d[...] += dot(gt[:, rows], z)
        acc_gu[...] += dot(at[:, rows], both)

    def pack(b):
        slot = lax.rem(b, slots)
        of_d, of_block = d // n, block // n
        for s in range(n):
            for c in range(2 * block // LANES):
                piece = acc_gu[pl.ds(s * of_d, of_d), pl.ds(c * LANES, LANES)]
                own[slot, s, pl.ds(c * of_d, of_d)] = piece.astype(BF16)
        base = 2 * block // LANES * of_d
        for c in range(d // LANES):
            turned = acc_d[pl.ds(c * LANES, LANES)].T.astype(BF16)
            for s in range(n):
                own[slot, s, pl.ds(base + c * of_block, of_block)] = turned[s * of_block : (s + 1) * of_block]

    def one_block(b, last):
        @pl.when(b + 1 < units)
        def _():
            for copy in weight_loads(b + 1):
                copy.start()

        for copy in weight_loads(b):
            copy.wait()
        acc_gu[...] = jnp.zeros_like(acc_gu)
        acc_d[...] = jnp.zeros_like(acc_d)

        @pl.loop(0, tiles)
        def _(t):
            if last:

                @pl.when((b > 0) | (t > 1))
                def _():
                    for copy in dgu_stores(b, t, lax.rem(t, 2)):
                        copy.wait()

            else:

                @pl.when(b == blocks)
                def _():
                    for copy in a0_loads(t):
                        copy.wait()

            steps(b, t, last)
            if last:
                for copy in dgu_stores(b, t, lax.rem(t, 2)):
                    copy.start()
                events(b * tiles + t, 0)
            else:
                events(second + (b - blocks) * tiles + t, 2)

        pack(b)

    def way_back(d_in, h_in):
        def in_loads(i, slot):
            return [
                pltpu.make_async_copy(dgu_hbm.at[span(i, small)], d_in.at[slot], dy_sem.at[slot]),
                pltpu.make_async_copy(h_hbm.at[span(i, small)], h_in.at[slot], dy_sem.at[2 + slot]),
            ]

        for copy in in_loads(0, 0):
            copy.start()
        for t in range(tiles):
            for copy in a0_loads(t):
                copy.start()
        for copy in wide_loads(1):
            copy.wait()

        @pl.loop(0, smalls)
        def _(i):
            slot = lax.rem(i, 2)
            for copy in in_loads(i, slot):
                copy.wait()

            @pl.when(i + 1 < smalls)
            def _():
                for copy in in_loads(i + 1, 1 - slot):
                    copy.start()

            part = small // 2
            for c in range(2):
                here = pl.ds(c * part, part)
                rows = pl.ds(pl.multiple_of(i * small + c * part, part), part)
                by_a = dot(d_in[slot, here], wide[...], BY_ROWS).astype(BF16).astype(F32)
                h = h_in[slot, here].astype(F32)
                scale = scale_of(h)
                along = jnp.mean(by_a * h, -1, keepdims=True)
                by_h = (by_a * scale - h * (scale * scale * scale * along)).astype(BF16)
                out = (g[rows].astype(F32) + by_h.astype(F32)).astype(BF16)
                g[rows] = out
                gt[:, rows] = out.T
            events(between + i, 1)

    pl.run_scoped(
        forward,
        pltpu.VMEM((2, small, d), BF16),
        pltpu.VMEM((2, small, d), BF16),
        pltpu.VMEM((2, d, small), BF16),
        pltpu.VMEM((2, small, d), BF16),
        pltpu.VMEM((ff, d), BF16),
    )
    for copy in wide_loads(1):
        copy.start()

    @pl.loop(0, blocks)
    def _(b):
        one_block(b, True)

    for t in (tiles - 2, tiles - 1):
        for copy in dgu_stores(blocks - 1, t, t % 2):
            copy.wait()
    pl.run_scoped(way_back, pltpu.VMEM((2, small, 2 * ff), BF16), pltpu.VMEM((2, small, d), BF16))

    @pl.loop(blocks, units)
    def _(b):
        one_block(b, False)

    for now in range(second + between, second + between + at_ring(half) + 1):
        events(now, 3)

    def part_copy(k):
        return pltpu.make_async_remote_copy(
            src_ref=squares,
            dst_ref=parts.at[me],
            send_sem=part_send.at[k - 1],
            recv_sem=part_recv.at[k - 1],
            device_id={"dp": lax.rem(me + k, n)},
            device_id_type=MESH,
        )

    for k in range(1, n):
        part_copy(k).start()
    parts[me] = squares[...]
    for k in range(1, n):
        part_copy(k).wait()
    total = parts[0]
    for k in range(1, n):
        total = total + parts[k]
    total_ref[...] = total


def reduced(n, x, dy, w_gate, w_up, w_down):
    tokens, d = x.shape[1:]
    ff = w_gate.shape[2]
    block, tile = BLOCK, tokens // 4
    tiles, blocks, half = tokens // tile, ff // block, n // 2
    small, smalls = tile // 2, 2 * tiles
    shard_rows = 3 * d * block // (n * LANES)
    slots = at_ring(half) // tiles + 2
    anywhere, vmem = pl.BlockSpec(memory_space=pl.ANY), pl.BlockSpec(memory_space=pltpu.VMEM)
    dma = pltpu.SemaphoreType.DMA
    return pl.pallas_call(
        functools.partial(main_kernel, n),
        in_specs=[anywhere] * 5,
        out_specs=[anywhere, vmem, vmem, vmem] + [anywhere] * 4,
        out_shape=[
            jax.ShapeDtypeStruct((n, blocks, shard_rows, LANES), BF16),
            jax.ShapeDtypeStruct((blocks // 2, shard_rows, LANES), BF16),
            jax.ShapeDtypeStruct((blocks // 2, shard_rows, LANES), BF16),
            jax.ShapeDtypeStruct((8, LANES), F32),
            jax.ShapeDtypeStruct((tokens, d), BF16),
            jax.ShapeDtypeStruct((d, tokens), BF16),
            jax.ShapeDtypeStruct((tokens, d), BF16),
            jax.ShapeDtypeStruct((tokens, 2 * ff), BF16),
        ],
        scratch_shapes=[
            pltpu.VMEM((tokens, d), BF16),
            pltpu.VMEM((d, tokens), BF16),
            pltpu.VMEM((tokens, d), BF16),
            pltpu.VMEM((d, tokens), BF16),
            pltpu.VMEM((d, 2 * ff), BF16),
            pltpu.VMEM((2, d, 2 * block), BF16),
            pltpu.VMEM((2, block, d), BF16),
            pltpu.VMEM((d, 2 * block), F32),
            pltpu.VMEM((d, block), F32),
            pltpu.VMEM((2, tile, 2 * block), BF16),
            pltpu.VMEM((slots, n, shard_rows, LANES), BF16),
            pltpu.VMEM((slots, half, shard_rows, LANES), BF16),
            pltpu.VMEM((slots, half, shard_rows, LANES), BF16),
            pltpu.VMEM((blocks, shard_rows, LANES), BF16),
            pltpu.VMEM((8, LANES), F32),
            pltpu.VMEM((n, 8, LANES), F32),
            dma((2,)),
            dma((smalls,)),
            dma((3,)),
            dma((3, 2)),
            dma((2, 2)),
            dma((2, tiles)),
            dma((2, slots, half)),
            dma((2, slots, half)),
            dma((2, blocks, half)),
            dma((2, blocks, half)),
            dma((blocks,)),
            dma((n - 1,)),
            dma((n - 1,)),
            pltpu.SemaphoreType.REGULAR((2,)),
        ],
        compiler_params=pltpu.CompilerParams(collective_id=0, has_side_effects=True, vmem_limit_bytes=67_043_328),
        cost_estimate=pl.CostEstimate(flops=34 * tokens * d * ff, bytes_accessed=16 * tokens * d, transcendentals=3 * tokens * ff),
        name="reduced",
    )(x, dy, w_gate, w_up, w_down)[:4]


def update_kernel(count, n_terms, n_aliased, shards, total_ref, *refs):
    terms, refs = refs[:n_terms], refs[n_terms:]
    w, m, v = refs[:3], refs[3:6], refs[6:9]
    new_w, new_m, new_v = (refs[9 + n_aliased + 3 * i : 12 + n_aliased + 3 * i] for i in range(3))
    factor = jnp.minimum(1.0, 0.5 * lax.rsqrt(jnp.sum(total_ref[...], keepdims=True) / count + 1e-30))
    units = terms[0].shape[0]
    of_d, block = w[0].shape[0], w[0].shape[1] // units
    of_block, d = w[2].shape[1:]
    slabs = block // LANES

    def one(i, where, term):
        term = term.astype(F32) * factor
        m_new = 0.9 * m[i][where] + 0.1 * term
        v_new = 0.95 * v[i][where] + 0.05 * term * term
        wide = w[i][where].astype(F32)
        new_m[i][where] = m_new
        new_v[i][where] = v_new
        new_w[i][where] = (wide - 0.02 * (m_new * lax.rsqrt(v_new + 1e-8) + 0.1 * wide)).astype(BF16)

    def apply(term):
        for j in range(units):
            for i in range(2):
                for c in range(slabs):
                    one(i, (slice(None), pl.ds(j * block + c * LANES, LANES)), term[j, pl.ds((i * slabs + c) * of_d, of_d)])
            for c in range(d // LANES):
                one(2, (j, slice(None), pl.ds(c * LANES, LANES)), term[j, pl.ds(2 * slabs * of_d + c * of_block, of_block)])

    if n_terms == 1:
        apply(terms[0])
    else:
        for k, term in enumerate(terms):

            @pl.when(pl.program_id(0) * 2 + pl.program_id(1) == k)
            def _(term=term):
                apply(term)


def update(layer, shards, terms, total, weights, m, v, so_far):
    _, d, ff = weights[0].shape
    _, blocks, n, of_block, _ = weights[2].shape
    of_d = d // n
    flat = pl.BlockSpec((None, of_d, ff // 2), lambda i, c, shards: (layer, shards[i], c))
    tall = pl.BlockSpec((None, blocks // 2, None, of_block, d), lambda i, c, shards: (layer, c, shards[i], 0, 0))
    if isinstance(terms, tuple):
        array, first = terms
        terms = [array]
        term = pl.BlockSpec((None, blocks // 2, *array.shape[2:]), lambda i, c, shards: (first + i, c, 0, 0))
    else:
        term = pl.BlockSpec(terms[0].shape, lambda i, c, shards: (0, 0, 0))
    arrays = [*weights, *m, *v]
    specs = [flat, flat, tall] * 3
    aliased = list(so_far) if so_far is not None else []
    start = 2 + len(terms) + len(arrays)
    n_shards = shards.shape[0]
    bytes_accessed = n_shards * 22 * 3 * d * ff // n
    return pl.pallas_call(
        functools.partial(update_kernel, 3 * weights[0].size, len(terms), len(aliased)),
        grid_spec=pltpu.PrefetchScalarGridSpec(
            num_scalar_prefetch=1,
            grid=(n_shards, 2),
            in_specs=[pl.BlockSpec((8, LANES), lambda i, c, shards: (0, 0))]
            + [term] * len(terms)
            + specs
            + [pl.BlockSpec(memory_space=pl.ANY)] * len(aliased),
            out_specs=specs,
        ),
        out_shape=[jax.ShapeDtypeStruct(one.shape, one.dtype) for one in arrays],
        input_output_aliases={start + i: i for i in range(len(aliased))},
        compiler_params=pltpu.CompilerParams(vmem_limit_bytes=63 << 20),
        cost_estimate=pl.CostEstimate(flops=300 * bytes_accessed, bytes_accessed=bytes_accessed, transcendentals=0),
        name=f"update_{layer}",
    )(shards, total, *terms, *arrays, *aliased)


def solution(mesh):
    n = mesh.shape["dp"]
    half = n // 2

    def step(x, dy, *arrays):
        weights, m, v = (list(arrays[i : i + 3]) for i in (0, 3, 6))
        g1, g0a, g0b, total = reduced(n, x, dy, *weights)

        layers, ff, d = weights[2].shape
        split = (layers, ff // BLOCK, n, BLOCK // n, d)
        for group in (weights, m, v):
            group[2] = group[2].reshape(split)
        back = lax.rem(lax.axis_index("dp") + n - jnp.arange(n, dtype=jnp.int32), n)

        def sent(value, by):
            return lax.ppermute(value, "dp", [(i, (i + by) % n) for i in range(n)])

        came = [(g0a, g0b)]
        right, left = (g0a, g0b), (g0a, g0b)
        for k in range(1, half):
            a = sent(right[0], 1), sent(left[0], -1)
            b = sent(right[1], 1), sent(left[1], -1)
            right, left = (a[0], b[0]), (a[1], b[1])
            came.append((*right, *left))
        came.append((sent(right[0], 1), sent(left[1], -1)))

        def after(places, *values):
            return lax.optimization_barrier((places, *values))[0]

        out = update(1, back[:half], (g1, 0), total, weights, m, v, None)
        out = update(1, after(back[half:], *came[1][0::2]), (g1, half), total, weights, m, v, out)
        for k in range(half + 1):
            places = jnp.stack([back[k]] if k in (0, half) else [back[k], back[n - k]])
            if k == 0:
                places = after(places, *came[1][1::2])
            elif k == 1:
                places = after(places, *came[2][0::2])
            out = update(0, places, list(came[k]), total, weights, m, v, out)
        out = list(out)
        for i in (2, 5, 8):
            out[i] = out[i].reshape(layers, ff, d)
        return tuple(out)

    return jax.shard_map(
        step,
        mesh=mesh,
        in_specs=(P(("rep", "dp"), None, None),) * 2 + (P(None, None, None),) * 9,
        out_specs=(P("rep", None, None),) * 9,
        check_vma=False,
    )
```

time: 371 us -> 352 us (0.949)
  waiting for transfers between devices: 30.6 us -> 0.04 us
  Pallas kernels: 306 us -> 323 us
  starting transfers between devices: 24.8 us -> 19.4 us
  local copies, waits for them, and re-layouts: 6.12 us -> 2.15 us
    ppermute x16 -> x14, waiting for transfers between devices: 30.6 us -> 0.04 us  [sent(): return lax.ppermute(value, 'dp', [(i, (i + by) % n) for i in range(n)])]
    pallas_call x2 -> x1, Pallas kernels: 235 us -> 254 us  [reduced(): pl.pallas_call(functools.partial(main_kernel, n), in_specs=[anywhere] * 5...]
    ppermute x16 -> x14, starting transfers between devices: 24.8 us -> 19.4 us  [sent(): return lax.ppermute(value, 'dp', [(i, (i + by) % n) for i in range(n)])]
    slice x4 -> x2, local copies, waits for them, and re-layouts: 6.11 us -> 1.3 us  [the longest x1 0.69 us: step(): places = jnp.stack([back[k]] if k in (0, half) else [back[k], back[n - k]])]
    pallas_call x10 -> x7, Pallas kernels: 70.7 us -> 68.9 us  [update(): pl.pallas_call(functools.partial(update_kernel, 3 * weights[0].size, len(...]
  transfers between devices with their start and end apart: 16 -> 14, of which waited for: 4 -> 0; matrix products, arithmetic and copies ran while one was open for 2% -> 2% of each run, Pallas kernels for 18% -> 18%
where the time goes in v2:
time: 352 us; the launch traced here: 351 us
  Pallas kernels  323 us (92%)
  starting transfers between devices  19.4 us (6%)
  other arithmetic  5.49 us (2%)
    pallas_call x1, Pallas kernels, reduced(): pl.pallas_call(functools.partial(main_kernel, n), in_specs=[anywhere] * 5...  254 us
    pallas_call x7, Pallas kernels, update(): pl.pallas_call(functools.partial(update_kernel, 3 * weights[0].size, len(...  68.9 us
    ppermute x14, starting transfers between devices, sent(): return lax.ppermute(value, 'dp', [(i, (i + by) % n) for i in range(n)])  19.4 us
  transfers between devices with their start and end apart: 14, of which 0 were waited for; matrix products, arithmetic and copies ran while one was open for 2% of the time, Pallas kernels for 18%

profile of v2, /device:TPU:28, one launch (start us, length us, event | category | flops | bytes accessed | tf_op | source)
XLA Modules:
  0.0 351.3 jit_solution(5994611944903954624)
XLA Ops:
  0.6 254.4 %reduced.1 = (bf16[8,6,480,128]{3,2,1,0:T(8,128)(2,1)}, bf16[3,480,128]{2,1,0:T(8,128)(2,1)}, bf16[3,480,128]{2,1,0:T(8,128)(2,1)}, f32[8,128]{1,0:T(8,128)}, bf...) custom-call(bf16[1,4096,640]{2,1,0:T(8,128)(2,1)} %x_hbm.1, ...), custom_call_target="tpu_custom_call" | custom-call | flops 136902082560 | bytes 41943040 | tf_op jit(solution)/shard_map/reduced/pallas_call | solution.py:453
  255.0 0.6 collective-permute-start
  255.6 2.8 collective-permute-start.11
  258.3 0.0 collective-permute-start.4
  258.4 2.0 collective-permute-start.8
  260.4 0.6 fusion.1
  261.0 15.4 %update_1.2 = (bf16[2,640,1536]{2,1,0:T(8,128)(2,1)}, bf16[2,640,1536]{2,1,0:T(8,128)(2,1)}, bf16[2,6,8,32,640]{4,3,2,1,0:T(8,128)(2,1)}, f32[2,640,1536]{2,1,0:...) custom-call(s32[4]{0:T(128)} %get-tuple-element.149.shards, ...), custom_call_target="tpu_custom_call" | custom-call | flops 9732096000 | bytes 32440320 | tf_op jit(solution)/shard_map/update_1/pallas_call | solution.py:560
  276.4 0.7 fusion.2
  277.0 1.8 pad_add_fusion.2.shards
  278.9 1.8 pad_add_fusion.1.shards
  280.6 1.9 pad_add_fusion.shards
  282.5 0.0 collective-permute-done.refs_0_
  282.5 0.0 collective-permute-done.11.refs_2_
  282.5 0.0 copy-start.3
  282.5 0.1 collective-permute-start.1
  282.7 3.2 collective-permute-start.12
  285.9 0.0 collective-permute-done.4.refs_3_
  285.9 0.0 collective-permute-start.5
  285.9 0.0 collective-permute-done.8.refs_1_
  285.9 2.0 collective-permute-start.9
  287.9 15.4 %update_1.3 = (bf16[2,640,1536]{2,1,0:T(8,128)(2,1)}, bf16[2,640,1536]{2,1,0:T(8,128)(2,1)}, bf16[2,6,8,32,640]{4,3,2,1,0:T(8,128)(2,1)}, f32[2,640,1536]{2,1,0:...) custom-call(s32[4]{0:T(128)} %get-tuple-element.84.shards, ...), custom_call_target="tpu_custom_call", output_to_operand_aliasing={{0}: (12, {}), {1}: (13, {}), {2}: (14, {}), {3}: (15, {}),... | custom-call | flops 9732096000 | bytes 32440320 | tf_op jit(solution)/shard_map/update_1/pallas_call | solution.py:560
  303.3 0.0 copy-done.2
  303.3 0.0 copy-done.3
  303.3 5.2 %update_0.5 = (bf16[2,640,1536]{2,1,0:T(8,128)(2,1)}, bf16[2,640,1536]{2,1,0:T(8,128)(2,1)}, bf16[2,6,8,32,640]{4,3,2,1,0:T(8,128)(2,1)}, f32[2,640,1536]{2,1,0:...) custom-call(s32[1]{0:T(128)} %get-tuple-element.83.shards, ...), custom_call_target="tpu_custom_call", output_to_operand_aliasing={{0}: (13, {}), {1}: (14, {}), {2}: (15, {}), {3}: (16, {}),... | custom-call | flops 2433024000 | bytes 8110080 | tf_op jit(solution)/shard_map/update_0/pallas_call | solution.py:560
  308.5 0.0 collective-permute-done.1.refs_0_
  308.5 0.0 collective-permute-done.12.refs_2_
  308.6 0.1 collective-permute-start.2
  308.7 3.2 collective-permute-start.13
  311.9 0.0 collective-permute-done.5.refs_3_
  311.9 0.1 collective-permute-start.6
  312.0 0.0 collective-permute-done.9.refs_1_
  312.0 1.9 collective-permute-start.10
  313.9 9.3 %update_0.6 = (bf16[2,640,1536]{2,1,0:T(8,128)(2,1)}, bf16[2,640,1536]{2,1,0:T(8,128)(2,1)}, bf16[2,6,8,32,640]{4,3,2,1,0:T(8,128)(2,1)}, f32[2,640,1536]{2,1,0:...) custom-call(s32[2]{0:T(128)} %pad_add_fusion.2.shards, ...), custom_call_target="tpu_custom_call", output_to_operand_aliasing={{0}: (15, {}), {1}: (16, {}), {2}: (17, {}), {3}: (18, {}),... | custom-call | flops 4866048000 | bytes 16220160 | tf_op jit(solution)/shard_map/update_0/pallas_call | solution.py:560
  323.2 9.2 %update_0.7 = (bf16[2,640,1536]{2,1,0:T(8,128)(2,1)}, bf16[2,640,1536]{2,1,0:T(8,128)(2,1)}, bf16[2,6,8,32,640]{4,3,2,1,0:T(8,128)(2,1)}, f32[2,640,1536]{2,1,0:...) custom-call(s32[2]{0:T(128)} %pad_add_fusion.1.shards, ...), custom_call_target="tpu_custom_call", output_to_operand_aliasing={{0}: (15, {}), {1}: (16, {}), {2}: (17, {}), {3}: (18, {}),... | custom-call | flops 4866048000 | bytes 16220160 | tf_op jit(solution)/shard_map/update_0/pallas_call | solution.py:560
  332.4 0.0 collective-permute-done.2.refs_0_
  332.4 0.1 collective-permute-start.3
  332.5 0.0 collective-permute-done.6.refs_3_
  332.5 3.2 collective-permute-start.7
  335.7 0.0 collective-permute-done.13.refs_2_
  335.7 0.0 collective-permute-done.10.refs_1_
  335.8 9.1 %update_0.8 = (bf16[2,640,1536]{2,1,0:T(8,128)(2,1)}, bf16[2,640,1536]{2,1,0:T(8,128)(2,1)}, bf16[2,6,8,32,640]{4,3,2,1,0:T(8,128)(2,1)}, f32[2,640,1536]{2,1,0:...) custom-call(s32[2]{0:T(128)} %pad_add_fusion.shards, ...), custom_call_target="tpu_custom_call", output_to_operand_aliasing={{0}: (15, {}), {1}: (16, {}), {2}: (17, {}), {3}: (18, {}),... | custom-call | flops 4866048000 | bytes 16220160 | tf_op jit(solution)/shard_map/update_0/pallas_call | solution.py:560
  344.8 0.0 collective-permute-done.3.refs_0_
  344.9 0.0 copy-start
  344.9 0.0 collective-permute-done.7.refs_1_
  344.9 0.0 copy-start.1
  344.9 0.7 copy-done
  345.6 0.1 copy-done.1
  345.7 5.4 %update_0.9 = (bf16[2,640,1536]{2,1,0:T(8,128)(2,1)}, bf16[2,640,1536]{2,1,0:T(8,128)(2,1)}, bf16[2,6,8,32,640]{4,3,2,1,0:T(8,128)(2,1)}, f32[2,640,1536]{2,1,0:...) custom-call(s32[1]{0:T(128)} %get-tuple-element.158.shards, ...), custom_call_target="tpu_custom_call", output_to_operand_aliasing={{0}: (13, {}), {1}: (14, {}), {2}: (15, {}), {3}: (16, {}),... | custom-call | flops 2433024000 | bytes 8110080 | tf_op jit(solution)/shard_map/update_0/pallas_call | solution.py:560
  (2 shorter events, 0.0 us)
Async XLA Ops:
  255.0 27.5 %collective-permute-start = (bf16[3,480,128]{2,1,0:T(8,128)(2,1)}, bf16[3,480,128]{2,1,0:T(8,128)(2,1)S(1)}, u32[]{:S(2)}, u32[]{:S(2)}) collective-permute-start(bf16[3,480,128]{2,1,0:T(8,128)(2,1)} %get-tuple-element.80.refs_0_), channel_id=1, source_target_pairs={{0,1},{1,2},{2,3},{3,4},{4,5},{5,6},{6,7},{7,0},{8,9},{9,10},{10,1... | collective-permute-start | bytes 1105928 | tf_op jit(solution)/shard_map/ppermute | solution.py:594
  255.6 26.9 %collective-permute-start.11 = (bf16[3,480,128]{2,1,0:T(8,128)(2,1)}, bf16[3,480,128]{2,1,0:T(8,128)(2,1)S(1)}, u32[]{:S(2)}, u32[]{:S(2)}) collective-permute-start(bf16[3,480,128]{2,1,0:T(8,128)(2,1)} %get-tuple-element.80.refs_0_), channel_id=1, source_target_pairs={{0,7},{1,0},{2,1},{3,2},{4,3},{5,4},{6,5},{7,6},{8,15},{9,8},{10,9... | collective-permute-start | bytes 1105928 | tf_op jit(solution)/shard_map/ppermute | solution.py:594
  258.3 27.5 %collective-permute-start.4 = (bf16[3,480,128]{2,1,0:T(8,128)(2,1)}, bf16[3,480,128]{2,1,0:T(8,128)(2,1)}, u32[]{:S(2)}, u32[]{:S(2)}) collective-permute-start(bf16[3,480,128]{2,1,0:T(8,128)(2,1)} %get-tuple-element.81.refs_1_), channel_id=1, source_target_pairs={{0,7},{1,0},{2,1},{3,2},{4,3},{5,4},{6,5},{7,6},{8,15},{9,8},{10,9... | collective-permute-start | bytes 1105928 | tf_op jit(solution)/shard_map/ppermute | solution.py:594
  258.4 27.5 %collective-permute-start.8 = (bf16[3,480,128]{2,1,0:T(8,128)(2,1)}, bf16[3,480,128]{2,1,0:T(8,128)(2,1)}, u32[]{:S(2)}, u32[]{:S(2)}) collective-permute-start(bf16[3,480,128]{2,1,0:T(8,128)(2,1)} %get-tuple-element.81.refs_1_), channel_id=1, source_target_pairs={{0,1},{1,2},{2,3},{3,4},{4,5},{5,6},{6,7},{7,0},{8,9},{9,10},{10,1... | collective-permute-start | bytes 1105928 | tf_op jit(solution)/shard_map/ppermute | solution.py:594
  282.5 20.7 %copy-start.2 = (bf16[3,480,128]{2,1,0:T(8,128)(2,1)}, bf16[3,480,128]{2,1,0:T(8,128)(2,1)S(1)}, u32[]{:S(2)}) copy-start(bf16[3,480,128]{2,1,0:T(8,128)(2,1)S(1)} %collective-permute-done.refs_0_) | copy-start | bytes 1105924
  282.5 20.7 %copy-start.3 = (bf16[3,480,128]{2,1,0:T(8,128)(2,1)}, bf16[3,480,128]{2,1,0:T(8,128)(2,1)S(1)}, u32[]{:S(2)}) copy-start(bf16[3,480,128]{2,1,0:T(8,128)(2,1)S(1)} %collective-permute-done.11.refs_2_) | copy-start | bytes 1105924
  282.5 26.0 %collective-permute-start.1 = (bf16[3,480,128]{2,1,0:T(8,128)(2,1)S(1)}, bf16[3,480,128]{2,1,0:T(8,128)(2,1)}, u32[]{:S(2)}, u32[]{:S(2)}) collective-permute-start(bf16[3,480,128]{2,1,0:T(8,128)(2,1)S(1)} %collective-permute-done.refs_0_), channel_id=1, source_target_pairs={{0,1},{1,2},{2,3},{3,4},{4,5},{5,6},{6,7},{7,0},{8,9},{9,10},{10,1... | collective-permute-start | bytes 1105928 | tf_op jit(solution)/shard_map/ppermute | solution.py:594
  282.7 25.9 %collective-permute-start.12 = (bf16[3,480,128]{2,1,0:T(8,128)(2,1)S(1)}, bf16[3,480,128]{2,1,0:T(8,128)(2,1)}, u32[]{:S(2)}, u32[]{:S(2)}) collective-permute-start(bf16[3,480,128]{2,1,0:T(8,128)(2,1)S(1)} %collective-permute-done.11.refs_2_), channel_id=1, source_target_pairs={{0,7},{1,0},{2,1},{3,2},{4,3},{5,4},{6,5},{7,6},{8,15},{9,8},{10,9... | collective-permute-start | bytes 1105928 | tf_op jit(solution)/shard_map/ppermute | solution.py:594
  285.9 26.0 %collective-permute-start.5 = (bf16[3,480,128]{2,1,0:T(8,128)(2,1)}, bf16[3,480,128]{2,1,0:T(8,128)(2,1)}, u32[]{:S(2)}, u32[]{:S(2)}) collective-permute-start(bf16[3,480,128]{2,1,0:T(8,128)(2,1)} %collective-permute-done.4.refs_3_), channel_id=1, source_target_pairs={{0,7},{1,0},{2,1},{3,2},{4,3},{5,4},{6,5},{7,6},{8,15},{9,8},{10,9... | collective-permute-start | bytes 1105928 | tf_op jit(solution)/shard_map/ppermute | solution.py:594
  285.9 26.1 %collective-permute-start.9 = (bf16[3,480,128]{2,1,0:T(8,128)(2,1)}, bf16[3,480,128]{2,1,0:T(8,128)(2,1)}, u32[]{:S(2)}, u32[]{:S(2)}) collective-permute-start(bf16[3,480,128]{2,1,0:T(8,128)(2,1)} %collective-permute-done.8.refs_1_), channel_id=1, source_target_pairs={{0,1},{1,2},{2,3},{3,4},{4,5},{5,6},{6,7},{7,0},{8,9},{9,10},{10,1... | collective-permute-start | bytes 1105928 | tf_op jit(solution)/shard_map/ppermute | solution.py:594
  308.6 23.8 %collective-permute-start.2 = (bf16[3,480,128]{2,1,0:T(8,128)(2,1)}, bf16[3,480,128]{2,1,0:T(8,128)(2,1)}, u32[]{:S(2)}, u32[]{:S(2)}) collective-permute-start(bf16[3,480,128]{2,1,0:T(8,128)(2,1)} %collective-permute-done.1.refs_0_), channel_id=1, source_target_pairs={{0,1},{1,2},{2,3},{3,4},{4,5},{5,6},{6,7},{7,0},{8,9},{9,10},{10,1... | collective-permute-start | bytes 1105928 | tf_op jit(solution)/shard_map/ppermute | solution.py:594
  308.7 27.1 %collective-permute-start.13 = (bf16[3,480,128]{2,1,0:T(8,128)(2,1)}, bf16[3,480,128]{2,1,0:T(8,128)(2,1)}, u32[]{:S(2)}, u32[]{:S(2)}) collective-permute-start(bf16[3,480,128]{2,1,0:T(8,128)(2,1)} %collective-permute-done.12.refs_2_), channel_id=1, source_target_pairs={{0,7},{1,0},{2,1},{3,2},{4,3},{5,4},{6,5},{7,6},{8,15},{9,8},{10,9... | collective-permute-start | bytes 1105928 | tf_op jit(solution)/shard_map/ppermute | solution.py:594
  311.9 20.6 %collective-permute-start.6 = (bf16[3,480,128]{2,1,0:T(8,128)(2,1)}, bf16[3,480,128]{2,1,0:T(8,128)(2,1)}, u32[]{:S(2)}, u32[]{:S(2)}) collective-permute-start(bf16[3,480,128]{2,1,0:T(8,128)(2,1)} %collective-permute-done.5.refs_3_), channel_id=1, source_target_pairs={{0,7},{1,0},{2,1},{3,2},{4,3},{5,4},{6,5},{7,6},{8,15},{9,8},{10,9... | collective-permute-start | bytes 1105928 | tf_op jit(solution)/shard_map/ppermute | solution.py:594
  312.0 23.8 %collective-permute-start.10 = (bf16[3,480,128]{2,1,0:T(8,128)(2,1)}, bf16[3,480,128]{2,1,0:T(8,128)(2,1)}, u32[]{:S(2)}, u32[]{:S(2)}) collective-permute-start(bf16[3,480,128]{2,1,0:T(8,128)(2,1)} %collective-permute-done.9.refs_1_), channel_id=1, source_target_pairs={{0,1},{1,2},{2,3},{3,4},{4,5},{5,6},{6,7},{7,0},{8,9},{9,10},{10,1... | collective-permute-start | bytes 1105928 | tf_op jit(solution)/shard_map/ppermute | solution.py:594
  332.4 12.4 %collective-permute-start.3 = (bf16[3,480,128]{2,1,0:T(8,128)(2,1)}, bf16[3,480,128]{2,1,0:T(8,128)(2,1)S(1)}, u32[]{:S(2)}, u32[]{:S(2)}) collective-permute-start(bf16[3,480,128]{2,1,0:T(8,128)(2,1)} %collective-permute-done.2.refs_0_), channel_id=1, source_target_pairs={{0,1},{1,2},{2,3},{3,4},{4,5},{5,6},{6,7},{7,0},{8,9},{9,10},{10,1... | collective-permute-start | bytes 1105928 | tf_op jit(solution)/shard_map/ppermute | solution.py:594
  332.5 12.3 %collective-permute-start.7 = (bf16[3,480,128]{2,1,0:T(8,128)(2,1)}, bf16[3,480,128]{2,1,0:T(8,128)(2,1)S(1)}, u32[]{:S(2)}, u32[]{:S(2)}) collective-permute-start(bf16[3,480,128]{2,1,0:T(8,128)(2,1)} %collective-permute-done.6.refs_3_), channel_id=1, source_target_pairs={{0,7},{1,0},{2,1},{3,2},{4,3},{5,4},{6,5},{7,6},{8,15},{9,8},{10,9... | collective-permute-start | bytes 1105928 | tf_op jit(solution)/shard_map/ppermute | solution.py:594
  344.9 0.7 copy-start
  344.9 0.8 copy-start.1

commit v3 on v2

--- a/solution.py
+++ b/solution.py
@@ -7,6 +7,7 @@
 from jax.experimental.pallas import tpu as pltpu
 from jax.sharding import PartitionSpec as P
 
+
 BF16, F32 = jnp.bfloat16, jnp.float32
 MESH = pl.DeviceIdType.MESH
 LANES = 128
@@ -40,12 +41,12 @@
 
 
 def at_gather(e, half):
-    return at_ring(half) + (3 + 4 * e if e else 0)
+    return at_ring(half) + 3 * e
 
 
 def main_kernel(
     n, x_hbm, dy_hbm, wg_hbm, wu_hbm, wd_hbm,
-    g1_hbm, g0a_ref, g0b_ref, total_ref, a0_hbm, a0t_hbm, h_hbm, dgu_hbm,
+    g1_hbm, g0a_ref, g0b_ref, total_ref, a0t_hbm, h_hbm, dgu_hbm, gu_hbm,
     a, at, g, gt, wide, wgu, wd, acc_gu, acc_d, dgu, own, from_left, from_right, kept, squares, parts,
     x_sem, dy_sem, wide_sem, w_sem, dgu_sem, in_sem, send_sem, recv_sem, there_sem, here_sem, kept_sem, part_send, part_recv, credit,
 ):
@@ -58,6 +59,8 @@
     tiles = tokens // tile
     small = tile // 2
     smalls = tokens // small
+    chunk = small // 2
+    chunks = tokens // chunk
     slots, shard_rows = own.shape[0], own.shape[2]
     me = lax.axis_index("dp")
     right, left = lax.rem(me + 1, n), lax.rem(me + n - 1, n)
@@ -66,7 +69,7 @@
         return pl.ds(i * size, size) if isinstance(i, int) else pl.ds(pl.multiple_of(i * size, size), size)
 
     def dy_load(i):
-        return pltpu.make_async_copy(dy_hbm.at[0, span(i, small)], g.at[span(i, small)], dy_sem.at[i])
+        return pltpu.make_async_copy(dy_hbm.at[0, span(i, chunk)], g.at[span(i, chunk)], dy_sem.at[i])
 
     def wide_loads(layer):
         return [
@@ -74,21 +77,20 @@
             pltpu.make_async_copy(wu_hbm.at[layer], wide.at[:, pl.ds(ff, ff)], wide_sem.at[1]),
         ]
 
-    def a0_loads(t):
-        return [
-            pltpu.make_async_copy(a0_hbm.at[span(t, tile)], a.at[span(t, tile)], in_sem.at[0, t]),
-            pltpu.make_async_copy(a0t_hbm.at[:, span(t, tile)], at.at[:, span(t, tile)], in_sem.at[1, t]),
-        ]
-
-    def weight_loads(b):
-        last = jnp.int32(b < blocks) if isinstance(b, int) else (b < blocks).astype(jnp.int32)
-        columns = pl.ds(pl.multiple_of((b - blocks * (1 - last)) * block, block), block)
+    def a0t_load(t):
+        return pltpu.make_async_copy(a0t_hbm.at[:, span(t, tile)], at.at[:, span(t, tile)], in_sem.at[t])
+
+    def gu_loads(b):
         slot = lax.rem(b, 2)
         return [
-            pltpu.make_async_copy(wg_hbm.at[last, :, columns], wgu.at[slot, :, pl.ds(0, block)], w_sem.at[0, slot]),
-            pltpu.make_async_copy(wu_hbm.at[last, :, columns], wgu.at[slot, :, pl.ds(block, block)], w_sem.at[1, slot]),
-            pltpu.make_async_copy(wd_hbm.at[last, columns, :], wd.at[slot], w_sem.at[2, slot]),
+            pltpu.make_async_copy(ref.at[1, :, span(b, block)], wgu.at[slot, :, pl.ds(i * block, block)], w_sem.at[i, slot])
+            for i, ref in enumerate((wg_hbm, wu_hbm))
         ]
+
+    def down_load(b):
+        last = jnp.int32(b < blocks) if isinstance(b, int) else (b < blocks).astype(jnp.int32)
+        slot = lax.rem(b, 2)
+        return pltpu.make_async_copy(wd_hbm.at[last, span(b - blocks * (1 - last), block), :], wd.at[slot], w_sem.at[2, slot])
 
     def ring_copy(u, k, way):
         slot = lax.rem(u, slots)
@@ -206,73 +208,100 @@
                     def _(job=job, since=since, first=first):
                         job(first + lax.div(since, tiles))
 
-    def forward(x_in, a0_out, a0t_out, h_out, wd0):
-        def x_load(i, slot):
-            return pltpu.make_async_copy(x_hbm.at[0, span(i, small)], x_in.at[slot], x_sem.at[slot])
-
-        def stores(i, slot):
+    def forward(x_in, a0t_out, h_out, z, gu_out, wd0):
+        def x_load(i):
+            slot = lax.rem(i, 4)
+            return pltpu.make_async_copy(x_hbm.at[0, span(i, chunk)], x_in.at[slot], x_sem.at[slot])
+
+        def first_stores(i):
+            slot = lax.rem(i, 2)
             return [
-                pltpu.make_async_copy(a0_out.at[slot], a0_hbm.at[span(i, small)], in_sem.at[0, slot]),
-                pltpu.make_async_copy(a0t_out.at[slot], a0t_hbm.at[:, span(i, small)], in_sem.at[1, slot]),
-                pltpu.make_async_copy(h_out.at[slot], h_hbm.at[span(i, small)], dgu_sem.at[0, slot]),
+                pltpu.make_async_copy(a0t_out.at[slot], a0t_hbm.at[:, span(i, chunk)], in_sem.at[slot]),
+                pltpu.make_async_copy(gu_out.at[slot], gu_hbm.at[span(i, chunk)], dgu_sem.at[0, slot]),
             ]
 
+        def second_store(i):
+            slot = lax.rem(i, 2)
+            return pltpu.make_async_copy(h_out.at[slot], h_hbm.at[span(i, chunk)], dgu_sem.at[1, slot])
+
+        def first(i):
+            slot = lax.rem(i, 2)
+            a0 = normed(x_in[lax.rem(i, 4)])
+            a0t_out[slot] = a0.T
+            cut = 2 * block
+            for c in range(ff // cut):
+                gate = dot(a0, wide[:, c * cut : (c + 1) * cut])
+                up = dot(a0, wide[:, ff + c * cut : ff + (c + 1) * cut])
+                gu_out[slot, :, pl.ds(c * cut, cut)] = gate
+                gu_out[slot, :, pl.ds(ff + c * cut, cut)] = up
+                z[slot, :, pl.ds(c * cut, cut)] = (gate * jax.nn.sigmoid(gate) * up).astype(BF16)
+
+        def second(i):
+            slot = lax.rem(i, 2)
+            rows = span(i, chunk)
+            h = (x_in[lax.rem(i, 4)].astype(F32) + dot(z[slot], wd0[...]).astype(BF16).astype(F32)).astype(BF16)
+            h_out[slot] = h
+            a1 = normed(h)
+            a[rows] = a1
+            at[:, rows] = a1.T
+            gt[:, rows] = g[rows].T
+
         wd0_load = pltpu.make_async_copy(wd_hbm.at[0], wd0, wide_sem.at[2])
-        x_load(0, 0).start()
+        x_load(0).start()
         for copy in wide_loads(0):
             copy.start()
         wd0_load.start()
-        for i in range(smalls):
+        for i in (1, 2):
+            x_load(i).start()
+        for i in range(chunks):
             dy_load(i).start()
-        for copy in weight_loads(0):
+        for copy in gu_loads(0):
             copy.start()
+        down_load(0).start()
         barrier = pltpu.get_barrier_semaphore()
         for k in range(1, n):
             pl.semaphore_signal(barrier, 1, device_id={"dp": lax.rem(me + k, n)}, device_id_type=MESH)
         squares[...] = jnp.zeros_like(squares)
+        x_load(0).wait()
         for copy in wide_loads(0):
             copy.wait()
+        first(0)
+        for copy in first_stores(0):
+            copy.start()
         wd0_load.wait()
 
-        @pl.loop(0, smalls)
+        @pl.loop(1, chunks)
         def _(i):
-            slot = lax.rem(i, 2)
-            x_load(i, slot).wait()
-
-            @pl.when(i + 1 < smalls)
-            def _():
-                x_load(i + 1, 1 - slot).start()
-
-            dy_load(i).wait()
+            x_load(i).wait()
+            dy_load(i - 1).wait()
 
             @pl.when(i >= 2)
             def _():
-                for copy in stores(i - 2, slot):
+                for copy in first_stores(i - 2):
                     copy.wait()
 
-            gt[:, span(i, small)] = g[span(i, small)].T
-            part = small // 2
-            for c in range(2):
-                here = pl.ds(c * part, part)
-                rows = pl.ds(pl.multiple_of(i * small + c * part, part), part)
-                x = x_in[slot, here]
-                a0 = normed(x)
-                a0_out[slot, here] = a0
-                a0t_out[slot, :, here] = a0.T
-                gate = dot(a0, wide[:, :ff])
-                up = dot(a0, wide[:, ff:])
-                z = (gate * jax.nn.sigmoid(gate) * up).astype(BF16)
-                h = (x.astype(F32) + dot(z, wd0[...]).astype(BF16).astype(F32)).astype(BF16)
-                h_out[slot, here] = h
-                a1 = normed(h)
-                a[rows] = a1
-                at[:, rows] = a1.T
-            for copy in stores(i, slot):
+            @pl.when(i >= 3)
+            def _():
+                second_store(i - 3).wait()
+
+            second(i - 1)
+            first(i)
+            for copy in first_stores(i):
                 copy.start()
-
-        for i in range(max(smalls - 2, 0), smalls):
-            for copy in stores(i, i % 2):
+            second_store(i - 1).start()
+
+            @pl.when(i + 2 < chunks)
+            def _():
+                x_load(i + 2).start()
+
+        dy_load(chunks - 1).wait()
+        second_store(chunks - 3).wait()
+        second(chunks - 1)
+        second_store(chunks - 1).start()
+        for i in (chunks - 2, chunks - 1):
+            for copy in first_stores(i):
                 copy.wait()
+            second_store(i).wait()
         pl.semaphore_wait(barrier, n - 1)
 
     def dgu_stores(b, t, slot):
@@ -285,10 +314,10 @@
             for i in (0, 1)
         ]
 
-    def steps(b, t, last):
+    def steps(b, t, gu_in):
         rows = span(t, tile)
         slot = lax.rem(b, 2)
-        gu = dot(a[rows], wgu[slot])
+        gu = gu_in[lax.rem(t, 2)] if gu_in is not None else dot(a[rows], wgu[slot])
         dz = dot(g[rows], wd[slot], BY_ROWS).astype(BF16).astype(F32)
         gate, up = gu[:, :block], gu[:, block:]
         s = jax.nn.sigmoid(gate)
@@ -297,7 +326,7 @@
         dgate = (dz * up * (s + silu * (1 - s))).astype(BF16)
         dup = (dz * silu).astype(BF16)
         both = jnp.concatenate([dgate, dup], 1)
-        if last:
+        if gu_in is None:
             dgu[lax.rem(t, 2)] = both
         acc_d[...] += dot(gt[:, rows], z)
         acc_gu[...] += dot(at[:, rows], both)
@@ -315,42 +344,79 @@
             for s in range(n):
                 own[slot, s, pl.ds(base + c * of_block, of_block)] = turned[s * of_block : (s + 1) * of_block]
 
-    def one_block(b, last):
-        @pl.when(b + 1 < units)
-        def _():
-            for copy in weight_loads(b + 1):
-                copy.start()
-
-        for copy in weight_loads(b):
-            copy.wait()
+    def clear():
         acc_gu[...] = jnp.zeros_like(acc_gu)
         acc_d[...] = jnp.zeros_like(acc_d)
 
+    def last_block(b):
+        @pl.when(b + 1 < blocks)
+        def _():
+            for copy in gu_loads(b + 1):
+                copy.start()
+
+        down_load(b + 1).start()
+        for copy in gu_loads(b):
+            copy.wait()
+        down_load(b).wait()
+        clear()
+
         @pl.loop(0, tiles)
         def _(t):
-            if last:
-
-                @pl.when((b > 0) | (t > 1))
-                def _():
-                    for copy in dgu_stores(b, t, lax.rem(t, 2)):
-                        copy.wait()
-
-            else:
-
+            @pl.when((b > 0) | (t > 1))
+            def _():
+                for copy in dgu_stores(b, t, lax.rem(t, 2)):
+                    copy.wait()
+
+            steps(b, t, None)
+            for copy in dgu_stores(b, t, lax.rem(t, 2)):
+                copy.start()
+            events(b * tiles + t, 0)
+
+        pack(b)
+
+    def first_blocks(gu_in):
+        def tile_loads(b, t):
+            slot = lax.rem(t, 2)
+            return [
+                pltpu.make_async_copy(
+                    gu_hbm.at[span(t, tile), pl.ds(pl.multiple_of(i * ff + (b - blocks) * block, block), block)],
+                    gu_in.at[slot, :, pl.ds(i * block, block)],
+                    dgu_sem.at[i, slot],
+                )
+                for i in (0, 1)
+            ]
+
+        for copy in tile_loads(blocks, 0):
+            copy.start()
+
+        @pl.loop(blocks, units)
+        def _(b):
+            @pl.when(b + 1 < units)
+            def _():
+                down_load(b + 1).start()
+
+            down_load(b).wait()
+            clear()
+
+            @pl.loop(0, tiles)
+            def _(t):
                 @pl.when(b == blocks)
                 def _():
-                    for copy in a0_loads(t):
-                        copy.wait()
-
-            steps(b, t, last)
-            if last:
-                for copy in dgu_stores(b, t, lax.rem(t, 2)):
-                    copy.start()
-                events(b * tiles + t, 0)
-            else:
+                    a0t_load(t).wait()
+
+                for copy in tile_loads(b, t):
+                    copy.wait()
+                ends = t == tiles - 1
+
+                @pl.when((b + 1 < units) | jnp.logical_not(ends))
+                def _():
+                    for copy in tile_loads(jnp.where(ends, b + 1, b), jnp.where(ends, 0, t + 1)):
+                        copy.start()
+
+                steps(b, t, gu_in)
                 events(second + (b - blocks) * tiles + t, 2)
 
-        pack(b)
+            pack(b)
 
     def way_back(d_in, h_in):
         def in_loads(i, slot):
@@ -362,8 +428,7 @@
         for copy in in_loads(0, 0):
             copy.start()
         for t in range(tiles):
-            for copy in a0_loads(t):
-                copy.start()
+            a0t_load(t).start()
         for copy in wide_loads(1):
             copy.wait()
 
@@ -394,10 +459,11 @@
 
     pl.run_scoped(
         forward,
-        pltpu.VMEM((2, small, d), BF16),
-        pltpu.VMEM((2, small, d), BF16),
-        pltpu.VMEM((2, d, small), BF16),
-        pltpu.VMEM((2, small, d), BF16),
+        pltpu.VMEM((4, chunk, d), BF16),
+        pltpu.VMEM((2, d, chunk), BF16),
+        pltpu.VMEM((2, chunk, d), BF16),
+        pltpu.VMEM((2, chunk, ff), BF16),
+        pltpu.VMEM((2, chunk, 2 * ff), F32),
         pltpu.VMEM((ff, d), BF16),
     )
     for copy in wide_loads(1):
@@ -405,17 +471,13 @@
 
     @pl.loop(0, blocks)
     def _(b):
-        one_block(b, True)
+        last_block(b)
 
     for t in (tiles - 2, tiles - 1):
         for copy in dgu_stores(blocks - 1, t, t % 2):
             copy.wait()
     pl.run_scoped(way_back, pltpu.VMEM((2, small, 2 * ff), BF16), pltpu.VMEM((2, small, d), BF16))
-
-    @pl.loop(blocks, units)
-    def _(b):
-        one_block(b, False)
-
+    pl.run_scoped(first_blocks, pltpu.VMEM((2, tile, 2 * block), F32))
     for now in range(second + between, second + between + at_ring(half) + 1):
         events(now, 3)
 
@@ -445,7 +507,7 @@
     ff = w_gate.shape[2]
     block, tile = BLOCK, tokens // 4
     tiles, blocks, half = tokens // tile, ff // block, n // 2
-    small, smalls = tile // 2, 2 * tiles
+    smalls = 2 * tiles
     shard_rows = 3 * d * block // (n * LANES)
     slots = at_ring(half) // tiles + 2
     anywhere, vmem = pl.BlockSpec(memory_space=pl.ANY), pl.BlockSpec(memory_space=pltpu.VMEM)
@@ -459,10 +521,10 @@
             jax.ShapeDtypeStruct((blocks // 2, shard_rows, LANES), BF16),
             jax.ShapeDtypeStruct((blocks // 2, shard_rows, LANES), BF16),
             jax.ShapeDtypeStruct((8, LANES), F32),
-            jax.ShapeDtypeStruct((tokens, d), BF16),
             jax.ShapeDtypeStruct((d, tokens), BF16),
             jax.ShapeDtypeStruct((tokens, d), BF16),
             jax.ShapeDtypeStruct((tokens, 2 * ff), BF16),
+            jax.ShapeDtypeStruct((tokens, 2 * ff), F32),
         ],
         scratch_shapes=[
             pltpu.VMEM((tokens, d), BF16),
@@ -481,12 +543,12 @@
             pltpu.VMEM((blocks, shard_rows, LANES), BF16),
             pltpu.VMEM((8, LANES), F32),
             pltpu.VMEM((n, 8, LANES), F32),
-            dma((2,)),
-            dma((smalls,)),
+            dma((4,)),
+            dma((2 * smalls,)),
             dma((3,)),
             dma((3, 2)),
             dma((2, 2)),
-            dma((2, tiles)),
+            dma((tiles,)),
             dma((2, slots, half)),
             dma((2, slots, half)),
             dma((2, blocks, half)),
@@ -502,78 +564,112 @@
     )(x, dy, w_gate, w_up, w_down)[:4]
 
 
-def update_kernel(count, n_terms, n_aliased, shards, total_ref, *refs):
-    terms, refs = refs[:n_terms], refs[n_terms:]
-    w, m, v = refs[:3], refs[3:6], refs[6:9]
-    new_w, new_m, new_v = (refs[9 + n_aliased + 3 * i : 12 + n_aliased + 3 * i] for i in range(3))
+def update_kernel(n, layer, places, count, n_terms, *refs):
+    n_items = 2 * len(places)
+    total_ref, terms, (w, m, v) = refs[0], refs[1 : 1 + n_terms], (refs[1 + n_terms + 3 * i : 4 + n_terms + 3 * i] for i in range(3))
+    *refs, flat_w, tall_w, flat, tall, grads, in_sem, out_sem = refs[10 + n_terms :]
+    new = [refs[len(refs) - 9 + 3 * i : len(refs) - 6 + 3 * i] for i in range(3)]
+    _, units, _, _ = grads.shape
+    _, _, of_d, width = flat_w.shape
+    of_block, d = tall_w.shape[2:]
+    block = width // units
+    slabs = block // LANES
+    me = lax.axis_index("dp")
+
+    def place(k):
+        if isinstance(k, int):
+            return places[k // 2]
+        found = jnp.int32(places[0])
+        for i, at in enumerate(places):
+            found = jnp.where(lax.div(k, 2) == i, at, found)
+        return found
+
+    def copies(k, arrays, back):
+        shard = lax.rem(me + n - place(k), n)
+        half = lax.rem(k, 2)
+        across = pl.ds(pl.multiple_of(shard * of_d, of_d), of_d), pl.ds(pl.multiple_of(half * width, width), width)
+        pairs = []
+        for kind, (first, second, third) in enumerate(arrays):
+            for i, ref in enumerate((first, second)):
+                pairs.append((ref.at[layer, *across], flat_w.at[k, i] if kind == 0 else flat.at[k, kind - 1, i]))
+            pairs.append((third.at[layer, pl.ds(half * units, units), shard], tall_w.at[k] if kind == 0 else tall.at[k, kind - 1]))
+        sem = out_sem.at[k] if back else in_sem.at[k]
+        return [pltpu.make_async_copy(*(pair[::-1] if back else pair), sem) for pair in pairs]
+
+    def term_copy(k):
+        if n_terms == 1:
+            ref = terms[0].at[place(k), pl.ds(k % 2 * units, units)]
+        else:
+            ref = terms[k]
+        return pltpu.make_async_copy(ref, grads.at[k], in_sem.at[k])
+
+    for k in range(n_items):
+        for copy in [term_copy(k), *copies(k, (w, m, v), False)]:
+            copy.start()
     factor = jnp.minimum(1.0, 0.5 * lax.rsqrt(jnp.sum(total_ref[...], keepdims=True) / count + 1e-30))
-    units = terms[0].shape[0]
-    of_d, block = w[0].shape[0], w[0].shape[1] // units
-    of_block, d = w[2].shape[1:]
-    slabs = block // LANES
-
-    def one(i, where, term):
-        term = term.astype(F32) * factor
-        m_new = 0.9 * m[i][where] + 0.1 * term
-        v_new = 0.95 * v[i][where] + 0.05 * term * term
-        wide = w[i][where].astype(F32)
-        new_m[i][where] = m_new
-        new_v[i][where] = v_new
-        new_w[i][where] = (wide - 0.02 * (m_new * lax.rsqrt(v_new + 1e-8) + 0.1 * wide)).astype(BF16)
-
-    def apply(term):
+
+    @pl.loop(0, n_items)
+    def _(k):
+        pltpu.make_async_copy(grads.at[k], grads.at[k], in_sem.at[k]).wait()
+        for copy in copies(k, (w, m, v), False):
+            copy.wait()
+
+        def one(w_ref, m_ref, v_ref, where, term):
+            term = term.astype(F32) * factor
+            m_new = 0.9 * m_ref[where] + 0.1 * term
+            v_new = 0.95 * v_ref[where] + 0.05 * term * term
+            wide = w_ref[where].astype(F32)
+            m_ref[where] = m_new
+            v_ref[where] = v_new
+            w_ref[where] = (wide - 0.02 * (m_new * lax.rsqrt(v_new + 1e-8) + 0.1 * wide)).astype(BF16)
+
         for j in range(units):
             for i in range(2):
                 for c in range(slabs):
-                    one(i, (slice(None), pl.ds(j * block + c * LANES, LANES)), term[j, pl.ds((i * slabs + c) * of_d, of_d)])
+                    where = slice(None), pl.ds(j * block + c * LANES, LANES)
+                    term = grads[k, j, pl.ds((i * slabs + c) * of_d, of_d)]
+                    one(flat_w.at[k, i], flat.at[k, 0, i], flat.at[k, 1, i], where, term)
             for c in range(d // LANES):
-                one(2, (j, slice(None), pl.ds(c * LANES, LANES)), term[j, pl.ds(2 * slabs * of_d + c * of_block, of_block)])
-
-    if n_terms == 1:
-        apply(terms[0])
-    else:
-        for k, term in enumerate(terms):
-
-            @pl.when(pl.program_id(0) * 2 + pl.program_id(1) == k)
-            def _(term=term):
-                apply(term)
-
-
-def update(layer, shards, terms, total, weights, m, v, so_far):
+                where = j, slice(None), pl.ds(c * LANES, LANES)
+                term = grads[k, j, pl.ds(2 * slabs * of_d + c * of_block, of_block)]
+                one(tall_w.at[k], tall.at[k, 0], tall.at[k, 1], where, term)
+        for copy in copies(k, new, True):
+            copy.start()
+
+    @pl.loop(0, n_items)
+    def _(k):
+        for copy in copies(k, new, True):
+            copy.wait()
+
+
+def update(layer, places, terms, total, weights, m, v, so_far):
     _, d, ff = weights[0].shape
     _, blocks, n, of_block, _ = weights[2].shape
-    of_d = d // n
-    flat = pl.BlockSpec((None, of_d, ff // 2), lambda i, c, shards: (layer, shards[i], c))
-    tall = pl.BlockSpec((None, blocks // 2, None, of_block, d), lambda i, c, shards: (layer, c, shards[i], 0, 0))
-    if isinstance(terms, tuple):
-        array, first = terms
-        terms = [array]
-        term = pl.BlockSpec((None, blocks // 2, *array.shape[2:]), lambda i, c, shards: (first + i, c, 0, 0))
-    else:
-        term = pl.BlockSpec(terms[0].shape, lambda i, c, shards: (0, 0, 0))
+    of_d, units = d // n, blocks // 2
+    n_items = 2 * len(places)
     arrays = [*weights, *m, *v]
-    specs = [flat, flat, tall] * 3
     aliased = list(so_far) if so_far is not None else []
-    start = 2 + len(terms) + len(arrays)
-    n_shards = shards.shape[0]
-    bytes_accessed = n_shards * 22 * 3 * d * ff // n
+    start = 1 + len(terms) + len(arrays)
+    bytes_accessed = n_items * 11 * 3 * d * ff // n
+    anywhere = pl.BlockSpec(memory_space=pl.ANY)
     return pl.pallas_call(
-        functools.partial(update_kernel, 3 * weights[0].size, len(terms), len(aliased)),
-        grid_spec=pltpu.PrefetchScalarGridSpec(
-            num_scalar_prefetch=1,
-            grid=(n_shards, 2),
-            in_specs=[pl.BlockSpec((8, LANES), lambda i, c, shards: (0, 0))]
-            + [term] * len(terms)
-            + specs
-            + [pl.BlockSpec(memory_space=pl.ANY)] * len(aliased),
-            out_specs=specs,
-        ),
+        functools.partial(update_kernel, n, layer, places, 3 * weights[0].size, len(terms)),
+        in_specs=[pl.BlockSpec(memory_space=pltpu.VMEM)] + [anywhere] * (len(terms) + len(arrays) + len(aliased)),
+        out_specs=[anywhere] * len(arrays),
         out_shape=[jax.ShapeDtypeStruct(one.shape, one.dtype) for one in arrays],
+        scratch_shapes=[
+            pltpu.VMEM((n_items, 2, of_d, ff // 2), BF16),
+            pltpu.VMEM((n_items, units, of_block, d), BF16),
+            pltpu.VMEM((n_items, 2, 2, of_d, ff // 2), F32),
+            pltpu.VMEM((n_items, 2, units, of_block, d), F32),
+            pltpu.VMEM((n_items, units, *terms[0].shape[-2:]), BF16),
+            pltpu.SemaphoreType.DMA((n_items,)),
+            pltpu.SemaphoreType.DMA((n_items,)),
+        ],
         input_output_aliases={start + i: i for i in range(len(aliased))},
-        compiler_params=pltpu.CompilerParams(vmem_limit_bytes=63 << 20),
+        compiler_params=pltpu.CompilerParams(vmem_limit_bytes=67_043_328),
         cost_estimate=pl.CostEstimate(flops=300 * bytes_accessed, bytes_accessed=bytes_accessed, transcendentals=0),
-        name=f"update_{layer}",
-    )(shards, total, *terms, *arrays, *aliased)
+    )(total, *terms, *arrays, *aliased)
 
 
 def solution(mesh):
@@ -588,32 +684,27 @@
         split = (layers, ff // BLOCK, n, BLOCK // n, d)
         for group in (weights, m, v):
             group[2] = group[2].reshape(split)
-        back = lax.rem(lax.axis_index("dp") + n - jnp.arange(n, dtype=jnp.int32), n)
 
         def sent(value, by):
             return lax.ppermute(value, "dp", [(i, (i + by) % n) for i in range(n)])
 
-        came = [(g0a, g0b)]
+        rest = weights, m, v
+        came = [[g0a, g0b]]
         right, left = (g0a, g0b), (g0a, g0b)
-        for k in range(1, half):
+        for _ in range(1, half):
             a = sent(right[0], 1), sent(left[0], -1)
             b = sent(right[1], 1), sent(left[1], -1)
             right, left = (a[0], b[0]), (a[1], b[1])
-            came.append((*right, *left))
-        came.append((sent(right[0], 1), sent(left[1], -1)))
-
-        def after(places, *values):
-            return lax.optimization_barrier((places, *values))[0]
-
-        out = update(1, back[:half], (g1, 0), total, weights, m, v, None)
-        out = update(1, after(back[half:], *came[1][0::2]), (g1, half), total, weights, m, v, out)
-        for k in range(half + 1):
-            places = jnp.stack([back[k]] if k in (0, half) else [back[k], back[n - k]])
-            if k == 0:
-                places = after(places, *came[1][1::2])
-            elif k == 1:
-                places = after(places, *came[2][0::2])
-            out = update(0, places, list(came[k]), total, weights, m, v, out)
+            came.append([*right, *left])
+        came.append([sent(right[0], 1), sent(left[1], -1)])
+
+        jobs = [(1, list(range(k, k + n // 4)), [g1]) for k in range(0, n, n // 4)]
+        jobs.append((0, [0, 1, n - 1], came[0] + came[1]))
+        jobs += [(0, [k, n - k], came[k]) for k in range(2, half)]
+        jobs.append((0, [half], came[half]))
+        out = None
+        for layer, places, terms in jobs:
+            out = update(layer, places, terms, total, *rest, out)
         out = list(out)
         for i in (2, 5, 8):
             out[i] = out[i].reshape(layers, ff, d)

time: 352 us -> 334 us (0.949)
  Pallas kernels: 323 us -> 311 us
  other arithmetic: 5.49 us -> 0 us
    pallas_call x7 -> x8, Pallas kernels: 68.9 us -> 60.2 us  [update(): pl.pallas_call(functools.partial(update_kernel, n, layer, places, 3 * wei...]
    another operation x3 -> x0, other arithmetic: 5.48 us -> none  [step(): places = jnp.stack([back[k]] if k in (0, half) else [back[k], back[n - k]])]
  transfers between devices with their start and end apart: 14 -> 14, of which waited for: 0 -> 1; matrix products, arithmetic and copies ran while one was open for 2% -> 0% of each run, Pallas kernels for 18% -> 17%
where the time goes in v3:
time: 334 us; the launch traced here: 333 us
  Pallas kernels  311 us (93%)
  starting transfers between devices  21.1 us (6%)
    pallas_call x1, Pallas kernels, reduced(): pl.pallas_call(functools.partial(main_kernel, n), in_specs=[anywhere] * 5...  251 us
    pallas_call x8, Pallas kernels, update(): pl.pallas_call(functools.partial(update_kernel, n, layer, places, 3 * wei...  60.2 us
    ppermute x14, starting transfers between devices, sent(): return lax.ppermute(value, 'dp', [(i, (i + by) % n) for i in range(n)])  21.1 us
  transfers between devices with their start and end apart: 14, of which 1 were waited for; matrix products, arithmetic and copies ran while one was open for 0% of the time, Pallas kernels for 17%

profile of v3, /device:TPU:28, one launch (start us, length us, event | category | flops | bytes accessed | tf_op | source)
XLA Modules:
  0.0 333.4 jit_solution(18074394710719855403)
XLA Ops:
  0.6 251.0 %reduced.1 = (bf16[8,6,480,128]{3,2,1,0:T(8,128)(2,1)}, bf16[3,480,128]{2,1,0:T(8,128)(2,1)}, bf16[3,480,128]{2,1,0:T(8,128)(2,1)}, f32[8,128]{1,0:T(8,128)}, bf...) custom-call(bf16[1,4096,640]{2,1,0:T(8,128)(2,1)} %x_hbm.1, ...), custom_call_target="tpu_custom_call" | custom-call | flops 136902082560 | bytes 41943040 | tf_op jit(solution)/shard_map/reduced/pallas_call | solution.py:515
  251.7 0.9 collective-permute-start
  252.5 2.5 collective-permute-start.11
  255.0 0.4 collective-permute-start.4
  255.4 1.6 collective-permute-start.8
  257.0 7.7 %shard_map.178 = (bf16[2,640,1536]{2,1,0:T(8,128)(2,1)}, bf16[2,640,1536]{2,1,0:T(8,128)(2,1)}, bf16[2,6,8,32,640]{4,3,2,1,0:T(8,128)(2,1)}, f32[2,640,1536]{2,1...) custom-call(f32[8,128]{1,0:T(8,128)} %get-tuple-element.85.refs_0_, ...), custom_call_target="tpu_custom_call" | custom-call | flops 4866048000 | bytes 16220160 | tf_op jit(solution)/shard_map/pallas_call | solution.py:655
  264.7 7.7 %shard_map.179 = (bf16[2,640,1536]{2,1,0:T(8,128)(2,1)}, bf16[2,640,1536]{2,1,0:T(8,128)(2,1)}, bf16[2,6,8,32,640]{4,3,2,1,0:T(8,128)(2,1)}, f32[2,640,1536]{2,1...) custom-call(f32[8,128]{1,0:T(8,128)} %get-tuple-element.85.refs_0_, ...), custom_call_target="tpu_custom_call", output_to_operand_aliasing={{0}: (11, {}), {1}: (12, {}), {2}: (13, {}), {3}: (14, {}),... | custom-call | flops 4866048000 | bytes 16220160 | tf_op jit(solution)/shard_map/pallas_call | solution.py:655
  272.4 7.7 %shard_map.180 = (bf16[2,640,1536]{2,1,0:T(8,128)(2,1)}, bf16[2,640,1536]{2,1,0:T(8,128)(2,1)}, bf16[2,6,8,32,640]{4,3,2,1,0:T(8,128)(2,1)}, f32[2,640,1536]{2,1...) custom-call(f32[8,128]{1,0:T(8,128)} %get-tuple-element.85.refs_0_, ...), custom_call_target="tpu_custom_call", output_to_operand_aliasing={{0}: (11, {}), {1}: (12, {}), {2}: (13, {}), {3}: (14, {}),... | custom-call | flops 4866048000 | bytes 16220160 | tf_op jit(solution)/shard_map/pallas_call | solution.py:655
  280.1 7.7 %shard_map.181 = (bf16[2,640,1536]{2,1,0:T(8,128)(2,1)}, bf16[2,640,1536]{2,1,0:T(8,128)(2,1)}, bf16[2,6,8,32,640]{4,3,2,1,0:T(8,128)(2,1)}, f32[2,640,1536]{2,1...) custom-call(f32[8,128]{1,0:T(8,128)} %get-tuple-element.85.refs_0_, ...), custom_call_target="tpu_custom_call", output_to_operand_aliasing={{0}: (11, {}), {1}: (12, {}), {2}: (13, {}), {3}: (14, {}),... | custom-call | flops 4866048000 | bytes 16220160 | tf_op jit(solution)/shard_map/pallas_call | solution.py:655
  287.9 0.0 collective-permute-done.refs_3_
  287.9 0.1 collective-permute-start.1
  288.0 0.0 collective-permute-done.11.refs_5_
  288.0 3.2 collective-permute-start.12
  291.2 0.0 collective-permute-done.4.refs_6_
  291.2 0.4 collective-permute-start.5
  291.6 0.0 collective-permute-done.8.refs_4_
  291.6 1.6 collective-permute-start.9
  293.2 9.5 %shard_map.182 = (bf16[2,640,1536]{2,1,0:T(8,128)(2,1)}, bf16[2,640,1536]{2,1,0:T(8,128)(2,1)}, bf16[2,6,8,32,640]{4,3,2,1,0:T(8,128)(2,1)}, f32[2,640,1536]{2,1...) custom-call(f32[8,128]{1,0:T(8,128)} %get-tuple-element.85.refs_0_, ...), custom_call_target="tpu_custom_call", output_to_operand_aliasing={{0}: (16, {}), {1}: (17, {}), {2}: (18, {}), {3}: (19, {}),... | custom-call | flops 7299072000 | bytes 24330240 | tf_op jit(solution)/shard_map/pallas_call | solution.py:655
  302.7 0.0 collective-permute-done.1.refs_1_
  302.7 0.1 collective-permute-start.2
  302.9 0.1 collective-permute-done.5.refs_4_
  303.0 3.7 %collective-permute-start.6 = (bf16[3,480,128]{2,1,0:T(8,128)(2,1)}, bf16[3,480,128]{2,1,0:T(8,128)(2,1)}, u32[]{:S(2)}, u32[]{:S(2)}) collective-permute-start(bf16[3,480,128]{2,1,0:T(8,128)(2,1)} %collective-permute-done.5.refs_4_), channel_id=1, source_target_pairs={{0,7},{1,0},{2,1},{3,2},{4,3},{5,4},{6,5},{7,6},{8,15},{9,8},{10,9... | collective-permute-start | bytes 1105928 | tf_op jit(solution)/shard_map/ppermute | solution.py:689
  306.7 0.0 collective-permute-done.9.refs_2_
  306.7 0.0 collective-permute-start.10
  306.7 0.0 collective-permute-done.12.refs_3_
  306.7 3.2 collective-permute-start.13
  309.9 7.7 %shard_map.183 = (bf16[2,640,1536]{2,1,0:T(8,128)(2,1)}, bf16[2,640,1536]{2,1,0:T(8,128)(2,1)}, bf16[2,6,8,32,640]{4,3,2,1,0:T(8,128)(2,1)}, f32[2,640,1536]{2,1...) custom-call(f32[8,128]{1,0:T(8,128)} %get-tuple-element.85.refs_0_, ...), custom_call_target="tpu_custom_call", output_to_operand_aliasing={{0}: (14, {}), {1}: (15, {}), {2}: (16, {}), {3}: (17, {}),... | custom-call | flops 4866048000 | bytes 16220160 | tf_op jit(solution)/shard_map/pallas_call | solution.py:655
  317.6 0.0 collective-permute-done.2.refs_1_
  317.6 0.1 collective-permute-start.3
  317.7 0.0 collective-permute-done.6.refs_4_
  317.7 3.2 collective-permute-start.7
  320.9 0.0 collective-permute-done.10.refs_2_
  320.9 0.0 collective-permute-done.13.refs_3_
  320.9 7.7 %shard_map.184 = (bf16[2,640,1536]{2,1,0:T(8,128)(2,1)}, bf16[2,640,1536]{2,1,0:T(8,128)(2,1)}, bf16[2,6,8,32,640]{4,3,2,1,0:T(8,128)(2,1)}, f32[2,640,1536]{2,1...) custom-call(f32[8,128]{1,0:T(8,128)} %get-tuple-element.85.refs_0_, ...), custom_call_target="tpu_custom_call", output_to_operand_aliasing={{0}: (14, {}), {1}: (15, {}), {2}: (16, {}), {3}: (17, {}),... | custom-call | flops 4866048000 | bytes 16220160 | tf_op jit(solution)/shard_map/pallas_call | solution.py:655
  328.6 0.0 collective-permute-done.3.refs_1_
  328.6 0.0 collective-permute-done.7.refs_2_
  328.6 4.6 %shard_map.185 = (bf16[2,640,1536]{2,1,0:T(8,128)(2,1)}, bf16[2,640,1536]{2,1,0:T(8,128)(2,1)}, bf16[2,6,8,32,640]{4,3,2,1,0:T(8,128)(2,1)}, f32[2,640,1536]{2,1...) custom-call(f32[8,128]{1,0:T(8,128)} %get-tuple-element.85.refs_0_, ...), custom_call_target="tpu_custom_call", output_to_operand_aliasing={{0}: (12, {}), {1}: (13, {}), {2}: (14, {}), {3}: (15, {}),... | custom-call | flops 2433024000 | bytes 8110080 | tf_op jit(solution)/shard_map/pallas_call | solution.py:655
Async XLA Ops:
  251.7 36.2 %collective-permute-start = (bf16[3,480,128]{2,1,0:T(8,128)(2,1)}, bf16[3,480,128]{2,1,0:T(8,128)(2,1)}, u32[]{:S(2)}, u32[]{:S(2)}) collective-permute-start(bf16[3,480,128]{2,1,0:T(8,128)(2,1)} %get-tuple-element.86.refs_1_), channel_id=1, source_target_pairs={{0,1},{1,2},{2,3},{3,4},{4,5},{5,6},{6,7},{7,0},{8,9},{9,10},{10,1... | collective-permute-start | bytes 1105928 | tf_op jit(solution)/shard_map/ppermute | solution.py:689
  252.5 35.5 %collective-permute-start.11 = (bf16[3,480,128]{2,1,0:T(8,128)(2,1)}, bf16[3,480,128]{2,1,0:T(8,128)(2,1)}, u32[]{:S(2)}, u32[]{:S(2)}) collective-permute-start(bf16[3,480,128]{2,1,0:T(8,128)(2,1)} %get-tuple-element.86.refs_1_), channel_id=1, source_target_pairs={{0,7},{1,0},{2,1},{3,2},{4,3},{5,4},{6,5},{7,6},{8,15},{9,8},{10,9... | collective-permute-start | bytes 1105928 | tf_op jit(solution)/shard_map/ppermute | solution.py:689
  255.0 36.2 %collective-permute-start.4 = (bf16[3,480,128]{2,1,0:T(8,128)(2,1)}, bf16[3,480,128]{2,1,0:T(8,128)(2,1)}, u32[]{:S(2)}, u32[]{:S(2)}) collective-permute-start(bf16[3,480,128]{2,1,0:T(8,128)(2,1)} %get-tuple-element.87.refs_2_), channel_id=1, source_target_pairs={{0,7},{1,0},{2,1},{3,2},{4,3},{5,4},{6,5},{7,6},{8,15},{9,8},{10,9... | collective-permute-start | bytes 1105928 | tf_op jit(solution)/shard_map/ppermute | solution.py:689
  255.4 36.2 %collective-permute-start.8 = (bf16[3,480,128]{2,1,0:T(8,128)(2,1)}, bf16[3,480,128]{2,1,0:T(8,128)(2,1)}, u32[]{:S(2)}, u32[]{:S(2)}) collective-permute-start(bf16[3,480,128]{2,1,0:T(8,128)(2,1)} %get-tuple-element.87.refs_2_), channel_id=1, source_target_pairs={{0,1},{1,2},{2,3},{3,4},{4,5},{5,6},{6,7},{7,0},{8,9},{9,10},{10,1... | collective-permute-start | bytes 1105928 | tf_op jit(solution)/shard_map/ppermute | solution.py:689
  287.9 14.9 %collective-permute-start.1 = (bf16[3,480,128]{2,1,0:T(8,128)(2,1)}, bf16[3,480,128]{2,1,0:T(8,128)(2,1)}, u32[]{:S(2)}, u32[]{:S(2)}) collective-permute-start(bf16[3,480,128]{2,1,0:T(8,128)(2,1)} %collective-permute-done.refs_3_), channel_id=1, source_target_pairs={{0,1},{1,2},{2,3},{3,4},{4,5},{5,6},{6,7},{7,0},{8,9},{9,10},{10,1... | collective-permute-start | bytes 1105928 | tf_op jit(solution)/shard_map/ppermute | solution.py:689
  288.0 18.7 %collective-permute-start.12 = (bf16[3,480,128]{2,1,0:T(8,128)(2,1)}, bf16[3,480,128]{2,1,0:T(8,128)(2,1)}, u32[]{:S(2)}, u32[]{:S(2)}) collective-permute-start(bf16[3,480,128]{2,1,0:T(8,128)(2,1)} %collective-permute-done.11.refs_5_), channel_id=1, source_target_pairs={{0,7},{1,0},{2,1},{3,2},{4,3},{5,4},{6,5},{7,6},{8,15},{9,8},{10,9... | collective-permute-start | bytes 1105928 | tf_op jit(solution)/shard_map/ppermute | solution.py:689
  291.2 11.8 %collective-permute-start.5 = (bf16[3,480,128]{2,1,0:T(8,128)(2,1)}, bf16[3,480,128]{2,1,0:T(8,128)(2,1)}, u32[]{:S(2)}, u32[]{:S(2)}) collective-permute-start(bf16[3,480,128]{2,1,0:T(8,128)(2,1)} %collective-permute-done.4.refs_6_), channel_id=1, source_target_pairs={{0,7},{1,0},{2,1},{3,2},{4,3},{5,4},{6,5},{7,6},{8,15},{9,8},{10,9... | collective-permute-start | bytes 1105928 | tf_op jit(solution)/shard_map/ppermute | solution.py:689
  291.6 15.1 %collective-permute-start.9 = (bf16[3,480,128]{2,1,0:T(8,128)(2,1)}, bf16[3,480,128]{2,1,0:T(8,128)(2,1)}, u32[]{:S(2)}, u32[]{:S(2)}) collective-permute-start(bf16[3,480,128]{2,1,0:T(8,128)(2,1)} %collective-permute-done.8.refs_4_), channel_id=1, source_target_pairs={{0,1},{1,2},{2,3},{3,4},{4,5},{5,6},{6,7},{7,0},{8,9},{9,10},{10,1... | collective-permute-start | bytes 1105928 | tf_op jit(solution)/shard_map/ppermute | solution.py:689
  302.7 14.9 %collective-permute-start.2 = (bf16[3,480,128]{2,1,0:T(8,128)(2,1)}, bf16[3,480,128]{2,1,0:T(8,128)(2,1)}, u32[]{:S(2)}, u32[]{:S(2)}) collective-permute-start(bf16[3,480,128]{2,1,0:T(8,128)(2,1)} %collective-permute-done.1.refs_1_), channel_id=1, source_target_pairs={{0,1},{1,2},{2,3},{3,4},{4,5},{5,6},{6,7},{7,0},{8,9},{9,10},{10,1... | collective-permute-start | bytes 1105928 | tf_op jit(solution)/shard_map/ppermute | solution.py:689
  303.0 14.7 %collective-permute-start.6 = (bf16[3,480,128]{2,1,0:T(8,128)(2,1)}, bf16[3,480,128]{2,1,0:T(8,128)(2,1)}, u32[]{:S(2)}, u32[]{:S(2)}) collective-permute-start(bf16[3,480,128]{2,1,0:T(8,128)(2,1)} %collective-permute-done.5.refs_4_), channel_id=1, source_target_pairs={{0,7},{1,0},{2,1},{3,2},{4,3},{5,4},{6,5},{7,6},{8,15},{9,8},{10,9... | collective-permute-start | bytes 1105928 | tf_op jit(solution)/shard_map/ppermute | solution.py:689
  306.7 14.3 %collective-permute-start.10 = (bf16[3,480,128]{2,1,0:T(8,128)(2,1)}, bf16[3,480,128]{2,1,0:T(8,128)(2,1)}, u32[]{:S(2)}, u32[]{:S(2)}) collective-permute-start(bf16[3,480,128]{2,1,0:T(8,128)(2,1)} %collective-permute-done.9.refs_2_), channel_id=1, source_target_pairs={{0,1},{1,2},{2,3},{3,4},{4,5},{5,6},{6,7},{7,0},{8,9},{9,10},{10,1... | collective-permute-start | bytes 1105928 | tf_op jit(solution)/shard_map/ppermute | solution.py:689
  306.7 14.3 %collective-permute-start.13 = (bf16[3,480,128]{2,1,0:T(8,128)(2,1)}, bf16[3,480,128]{2,1,0:T(8,128)(2,1)}, u32[]{:S(2)}, u32[]{:S(2)}) collective-permute-start(bf16[3,480,128]{2,1,0:T(8,128)(2,1)} %collective-permute-done.12.refs_3_), channel_id=1, source_target_pairs={{0,7},{1,0},{2,1},{3,2},{4,3},{5,4},{6,5},{7,6},{8,15},{9,8},{10,9... | collective-permute-start | bytes 1105928 | tf_op jit(solution)/shard_map/ppermute | solution.py:689
  317.6 11.0 %collective-permute-start.3 = (bf16[3,480,128]{2,1,0:T(8,128)(2,1)}, bf16[3,480,128]{2,1,0:T(8,128)(2,1)}, u32[]{:S(2)}, u32[]{:S(2)}) collective-permute-start(bf16[3,480,128]{2,1,0:T(8,128)(2,1)} %collective-permute-done.2.refs_1_), channel_id=1, source_target_pairs={{0,1},{1,2},{2,3},{3,4},{4,5},{5,6},{6,7},{7,0},{8,9},{9,10},{10,1... | collective-permute-start | bytes 1105928 | tf_op jit(solution)/shard_map/ppermute | solution.py:689
  317.7 10.9 %collective-permute-start.7 = (bf16[3,480,128]{2,1,0:T(8,128)(2,1)}, bf16[3,480,128]{2,1,0:T(8,128)(2,1)}, u32[]{:S(2)}, u32[]{:S(2)}) collective-permute-start(bf16[3,480,128]{2,1,0:T(8,128)(2,1)} %collective-permute-done.6.refs_4_), channel_id=1, source_target_pairs={{0,7},{1,0},{2,1},{3,2},{4,3},{5,4},{6,5},{7,6},{8,15},{9,8},{10,9... | collective-permute-start | bytes 1105928 | tf_op jit(solution)/shard_map/ppermute | solution.py:689

commit v4 on v3

--- a/solution.py
+++ b/solution.py
@@ -11,7 +11,7 @@
 BF16, F32 = jnp.bfloat16, jnp.float32
 MESH = pl.DeviceIdType.MESH
 LANES = 128
-BLOCK = 256
+BLOCK, GATHERED = 256, 4
 PLAIN, BY_ROWS = ((1,), (0,)), ((1,), (1,))
 
 
@@ -41,14 +41,14 @@
 
 
 def at_gather(e, half):
-    return at_ring(half) + 3 * e
+    return at_ring(half) + 2 + (5 * e if e < 2 else 3 * e + 3)
 
 
 def main_kernel(
     n, x_hbm, dy_hbm, wg_hbm, wu_hbm, wd_hbm,
-    g1_hbm, g0a_ref, g0b_ref, total_ref, a0t_hbm, h_hbm, dgu_hbm, gu_hbm,
+    g1_hbm, ga_ref, gb_ref, total_ref, a0t_hbm, h_hbm, dgu_hbm, gu_hbm,
     a, at, g, gt, wide, wgu, wd, acc_gu, acc_d, dgu, own, from_left, from_right, kept, squares, parts,
-    x_sem, dy_sem, wide_sem, w_sem, dgu_sem, in_sem, send_sem, recv_sem, there_sem, here_sem, kept_sem, part_send, part_recv, credit,
+    x_sem, dy_sem, wide_sem, w_sem, dgu_sem, gu_sem, in_sem, send_sem, recv_sem, there_sem, here_sem, kept_sem, part_send, part_recv, credit,
 ):
     tokens, d = a.shape
     ff = wg_hbm.shape[2]
@@ -62,6 +62,7 @@
     chunk = small // 2
     chunks = tokens // chunk
     slots, shard_rows = own.shape[0], own.shape[2]
+    gathered = kept.shape[0]
     me = lax.axis_index("dp")
     right, left = lax.rem(me + 1, n), lax.rem(me + n - 1, n)
 
@@ -132,19 +133,19 @@
         else:
             came = from_left[slot, e - 1].astype(F32) + from_right[slot, e - 1].astype(F32)
             done = (own[slot, me].astype(F32) + came).astype(BF16)
+
+            def keep(ref, place):
+                def do():
+                    ref[jnp.clip(place, 0, ref.shape[0] - 1)] = done
+
+                return do
+
+            cut = gathered + ga_ref.shape[0]
             if last:
-                kept[u] = done
-            else:
-
-                def keep(ref, place):
-                    def do():
-                        ref[place] = done
-
-                    return do
-
-                cut = blocks + blocks // 2
-                when(u < cut, keep(g0a_ref, jnp.minimum(u - blocks, blocks // 2 - 1)))
-                when(u >= cut, keep(g0b_ref, jnp.maximum(u - cut, 0)))
+                when(u < gathered, keep(kept, u))
+            when((u >= gathered) & (u < cut), keep(ga_ref, u - gathered))
+            if not last:
+                when(u >= cut, keep(gb_ref, u - cut))
             exact = done.astype(F32)
             squares[...] += jnp.sum((exact * exact).reshape(shard_rows // 8, 8, LANES), 0)
 
@@ -190,21 +191,21 @@
     def events(now, phase):
         for last in (True, False):
             base, first = (0, 0) if last else (second, blocks)
-            jobs = [(at_ring(e), functools.partial(ring_event, e=e, last=last)) for e in range(half + 1)]
+            jobs = [(at_ring(e), blocks, functools.partial(ring_event, e=e, last=last)) for e in range(half + 1)]
             if last:
-                jobs += [(at_gather(e, half), functools.partial(gather_event, e=e)) for e in range(half + 1)]
-            for lag, job in jobs:
-                earliest, latest = base + tiles + lag, base + tiles * blocks + lag
+                jobs += [(at_gather(e, half), gathered, functools.partial(gather_event, e=e)) for e in range(half + 1)]
+            for lag, count, job in jobs:
+                earliest, latest = base + tiles + lag, base + tiles * count + lag
                 lo, hi = ((0, between), (between, second), (second, second + between), (second + between, 1 << 30))[phase]
                 if latest < lo or earliest >= hi:
                     continue
                 since = now - earliest
                 if isinstance(now, int):
-                    if since >= 0 and since % tiles == 0 and since // tiles < blocks:
+                    if since >= 0 and since % tiles == 0 and since // tiles < count:
                         job(first + since // tiles)
                 else:
 
-                    @pl.when((since >= 0) & (lax.rem(since + 64 * tiles, tiles) == 0) & (since < tiles * blocks))
+                    @pl.when((since >= 0) & (lax.rem(since + 64 * tiles, tiles) == 0) & (since < tiles * count))
                     def _(job=job, since=since, first=first):
                         job(first + lax.div(since, tiles))
 
@@ -214,10 +215,10 @@
             return pltpu.make_async_copy(x_hbm.at[0, span(i, chunk)], x_in.at[slot], x_sem.at[slot])
 
         def first_stores(i):
-            slot = lax.rem(i, 2)
+            slot = lax.rem(i, 3)
             return [
                 pltpu.make_async_copy(a0t_out.at[slot], a0t_hbm.at[:, span(i, chunk)], in_sem.at[slot]),
-                pltpu.make_async_copy(gu_out.at[slot], gu_hbm.at[span(i, chunk)], dgu_sem.at[0, slot]),
+                pltpu.make_async_copy(gu_out.at[slot], gu_hbm.at[span(i, chunk)], gu_sem.at[slot]),
             ]
 
         def second_store(i):
@@ -225,7 +226,7 @@
             return pltpu.make_async_copy(h_out.at[slot], h_hbm.at[span(i, chunk)], dgu_sem.at[1, slot])
 
         def first(i):
-            slot = lax.rem(i, 2)
+            slot = lax.rem(i, 3)
             a0 = normed(x_in[lax.rem(i, 4)])
             a0t_out[slot] = a0.T
             cut = 2 * block
@@ -234,7 +235,7 @@
                 up = dot(a0, wide[:, ff + c * cut : ff + (c + 1) * cut])
                 gu_out[slot, :, pl.ds(c * cut, cut)] = gate
                 gu_out[slot, :, pl.ds(ff + c * cut, cut)] = up
-                z[slot, :, pl.ds(c * cut, cut)] = (gate * jax.nn.sigmoid(gate) * up).astype(BF16)
+                z[lax.rem(i, 2), :, pl.ds(c * cut, cut)] = (gate * jax.nn.sigmoid(gate) * up).astype(BF16)
 
         def second(i):
             slot = lax.rem(i, 2)
@@ -275,13 +276,10 @@
             x_load(i).wait()
             dy_load(i - 1).wait()
 
-            @pl.when(i >= 2)
-            def _():
-                for copy in first_stores(i - 2):
-                    copy.wait()
-
             @pl.when(i >= 3)
             def _():
+                for copy in first_stores(i - 3):
+                    copy.wait()
                 second_store(i - 3).wait()
 
             second(i - 1)
@@ -298,10 +296,11 @@
         second_store(chunks - 3).wait()
         second(chunks - 1)
         second_store(chunks - 1).start()
-        for i in (chunks - 2, chunks - 1):
+        for i in (chunks - 3, chunks - 2, chunks - 1):
             for copy in first_stores(i):
                 copy.wait()
-            second_store(i).wait()
+            if i >= chunks - 2:
+                second_store(i).wait()
         pl.semaphore_wait(barrier, n - 1)
 
     def dgu_stores(b, t, slot):
@@ -460,10 +459,10 @@
     pl.run_scoped(
         forward,
         pltpu.VMEM((4, chunk, d), BF16),
-        pltpu.VMEM((2, d, chunk), BF16),
+        pltpu.VMEM((3, d, chunk), BF16),
         pltpu.VMEM((2, chunk, d), BF16),
         pltpu.VMEM((2, chunk, ff), BF16),
-        pltpu.VMEM((2, chunk, 2 * ff), F32),
+        pltpu.VMEM((3, chunk, 2 * ff), F32),
         pltpu.VMEM((ff, d), BF16),
     )
     for copy in wide_loads(1):
@@ -517,9 +516,9 @@
         in_specs=[anywhere] * 5,
         out_specs=[anywhere, vmem, vmem, vmem] + [anywhere] * 4,
         out_shape=[
-            jax.ShapeDtypeStruct((n, blocks, shard_rows, LANES), BF16),
-            jax.ShapeDtypeStruct((blocks // 2, shard_rows, LANES), BF16),
-            jax.ShapeDtypeStruct((blocks // 2, shard_rows, LANES), BF16),
+            jax.ShapeDtypeStruct((n, GATHERED, shard_rows, LANES), BF16),
+            jax.ShapeDtypeStruct((blocks - GATHERED // 2, shard_rows, LANES), BF16),
+            jax.ShapeDtypeStruct((blocks - GATHERED // 2, shard_rows, LANES), BF16),
             jax.ShapeDtypeStruct((8, LANES), F32),
             jax.ShapeDtypeStruct((d, tokens), BF16),
             jax.ShapeDtypeStruct((tokens, d), BF16),
@@ -540,7 +539,7 @@
             pltpu.VMEM((slots, n, shard_rows, LANES), BF16),
             pltpu.VMEM((slots, half, shard_rows, LANES), BF16),
             pltpu.VMEM((slots, half, shard_rows, LANES), BF16),
-            pltpu.VMEM((blocks, shard_rows, LANES), BF16),
+            pltpu.VMEM((GATHERED, shard_rows, LANES), BF16),
             pltpu.VMEM((8, LANES), F32),
             pltpu.VMEM((n, 8, LANES), F32),
             dma((4,)),
@@ -548,12 +547,13 @@
             dma((3,)),
             dma((3, 2)),
             dma((2, 2)),
+            dma((3,)),
             dma((tiles,)),
             dma((2, slots, half)),
             dma((2, slots, half)),
-            dma((2, blocks, half)),
-            dma((2, blocks, half)),
-            dma((blocks,)),
+            dma((2, GATHERED, half)),
+            dma((2, GATHERED, half)),
+            dma((GATHERED,)),
             dma((n - 1,)),
             dma((n - 1,)),
             pltpu.SemaphoreType.REGULAR((2,)),
@@ -564,52 +564,58 @@
     )(x, dy, w_gate, w_up, w_down)[:4]
 
 
-def update_kernel(n, layer, places, count, n_terms, *refs):
-    n_items = 2 * len(places)
+def update_kernel(n, pieces, count, n_terms, *refs):
     total_ref, terms, (w, m, v) = refs[0], refs[1 : 1 + n_terms], (refs[1 + n_terms + 3 * i : 4 + n_terms + 3 * i] for i in range(3))
     *refs, flat_w, tall_w, flat, tall, grads, in_sem, out_sem = refs[10 + n_terms :]
     new = [refs[len(refs) - 9 + 3 * i : len(refs) - 6 + 3 * i] for i in range(3)]
-    _, units, _, _ = grads.shape
+    units = grads.shape[1]
     _, _, of_d, width = flat_w.shape
     of_block, d = tall_w.shape[2:]
     block = width // units
     slabs = block // LANES
     me = lax.axis_index("dp")
 
-    def place(k):
+    def of(k, which):
         if isinstance(k, int):
-            return places[k // 2]
-        found = jnp.int32(places[0])
-        for i, at in enumerate(places):
-            found = jnp.where(lax.div(k, 2) == i, at, found)
+            return pieces[k][which]
+        found = jnp.int32(pieces[0][which])
+        for i, piece in enumerate(pieces):
+            if piece[which] != pieces[i - 1][which]:
+                found = jnp.where(k >= i, piece[which], found)
         return found
 
     def copies(k, arrays, back):
-        shard = lax.rem(me + n - place(k), n)
-        half = lax.rem(k, 2)
-        across = pl.ds(pl.multiple_of(shard * of_d, of_d), of_d), pl.ds(pl.multiple_of(half * width, width), width)
+        layer, pair, shard = of(k, 0), of(k, 1), lax.rem(me + n - of(k, 2), n)
+        across = pl.ds(pl.multiple_of(shard * of_d, of_d), of_d), pl.ds(pl.multiple_of(pair * width, width), width)
         pairs = []
         for kind, (first, second, third) in enumerate(arrays):
             for i, ref in enumerate((first, second)):
                 pairs.append((ref.at[layer, *across], flat_w.at[k, i] if kind == 0 else flat.at[k, kind - 1, i]))
-            pairs.append((third.at[layer, pl.ds(half * units, units), shard], tall_w.at[k] if kind == 0 else tall.at[k, kind - 1]))
+            pairs.append((third.at[layer, pl.ds(pair * units, units), shard], tall_w.at[k] if kind == 0 else tall.at[k, kind - 1]))
         sem = out_sem.at[k] if back else in_sem.at[k]
         return [pltpu.make_async_copy(*(pair[::-1] if back else pair), sem) for pair in pairs]
 
     def term_copy(k):
-        if n_terms == 1:
-            ref = terms[0].at[place(k), pl.ds(k % 2 * units, units)]
-        else:
-            ref = terms[k]
+        _, _, place, term, row = pieces[k]
+        ref = terms[term]
+        ref = ref.at[place, pl.ds(row, units)] if len(ref.shape) == 4 else ref.at[pl.ds(row, units)]
         return pltpu.make_async_copy(ref, grads.at[k], in_sem.at[k])
 
-    for k in range(n_items):
-        for copy in [term_copy(k), *copies(k, (w, m, v), False)]:
-            copy.start()
+    ahead = min(2, len(pieces))
+    for k in range(len(pieces)):
+        term_copy(k).start()
+        if k < ahead:
+            for copy in copies(k, (w, m, v), False):
+                copy.start()
     factor = jnp.minimum(1.0, 0.5 * lax.rsqrt(jnp.sum(total_ref[...], keepdims=True) / count + 1e-30))
 
-    @pl.loop(0, n_items)
+    @pl.loop(0, len(pieces))
     def _(k):
+        @pl.when(k + ahead < len(pieces))
+        def _():
+            for copy in copies(k + ahead, (w, m, v), False):
+                copy.start()
+
         pltpu.make_async_copy(grads.at[k], grads.at[k], in_sem.at[k]).wait()
         for copy in copies(k, (w, m, v), False):
             copy.wait()
@@ -636,39 +642,39 @@
         for copy in copies(k, new, True):
             copy.start()
 
-    @pl.loop(0, n_items)
+    @pl.loop(0, len(pieces))
     def _(k):
         for copy in copies(k, new, True):
             copy.wait()
 
 
-def update(layer, places, terms, total, weights, m, v, so_far):
-    _, d, ff = weights[0].shape
-    _, blocks, n, of_block, _ = weights[2].shape
-    of_d, units = d // n, blocks // 2
-    n_items = 2 * len(places)
+def update(pieces, terms, total, weights, m, v, so_far):
+    _, d, _ = weights[0].shape
+    _, _, n, of_block, _ = weights[2].shape
+    of_d, units, width, n_pieces = d // n, 2, 2 * BLOCK, len(pieces)
     arrays = [*weights, *m, *v]
     aliased = list(so_far) if so_far is not None else []
     start = 1 + len(terms) + len(arrays)
-    bytes_accessed = n_items * 11 * 3 * d * ff // n
+    bytes_accessed = n_pieces * 22 * 3 * d * width // n
     anywhere = pl.BlockSpec(memory_space=pl.ANY)
     return pl.pallas_call(
-        functools.partial(update_kernel, n, layer, places, 3 * weights[0].size, len(terms)),
+        functools.partial(update_kernel, n, pieces, 3 * weights[0].size, len(terms)),
         in_specs=[pl.BlockSpec(memory_space=pltpu.VMEM)] + [anywhere] * (len(terms) + len(arrays) + len(aliased)),
         out_specs=[anywhere] * len(arrays),
         out_shape=[jax.ShapeDtypeStruct(one.shape, one.dtype) for one in arrays],
         scratch_shapes=[
-            pltpu.VMEM((n_items, 2, of_d, ff // 2), BF16),
-            pltpu.VMEM((n_items, units, of_block, d), BF16),
-            pltpu.VMEM((n_items, 2, 2, of_d, ff // 2), F32),
-            pltpu.VMEM((n_items, 2, units, of_block, d), F32),
-            pltpu.VMEM((n_items, units, *terms[0].shape[-2:]), BF16),
-            pltpu.SemaphoreType.DMA((n_items,)),
-            pltpu.SemaphoreType.DMA((n_items,)),
+            pltpu.VMEM((n_pieces, 2, of_d, width), BF16),
+            pltpu.VMEM((n_pieces, units, of_block, d), BF16),
+            pltpu.VMEM((n_pieces, 2, 2, of_d, width), F32),
+            pltpu.VMEM((n_pieces, 2, units, of_block, d), F32),
+            pltpu.VMEM((n_pieces, units, *terms[0].shape[-2:]), BF16),
+            pltpu.SemaphoreType.DMA((n_pieces,)),
+            pltpu.SemaphoreType.DMA((n_pieces,)),
         ],
         input_output_aliases={start + i: i for i in range(len(aliased))},
         compiler_params=pltpu.CompilerParams(vmem_limit_bytes=67_043_328),
         cost_estimate=pl.CostEstimate(flops=300 * bytes_accessed, bytes_accessed=bytes_accessed, transcendentals=0),
+        name="update",
     )(total, *terms, *arrays, *aliased)
 
 
@@ -678,7 +684,7 @@
 
     def step(x, dy, *arrays):
         weights, m, v = (list(arrays[i : i + 3]) for i in (0, 3, 6))
-        g1, g0a, g0b, total = reduced(n, x, dy, *weights)
+        g1, ga, gb, total = reduced(n, x, dy, *weights)
 
         layers, ff, d = weights[2].shape
         split = (layers, ff // BLOCK, n, BLOCK // n, d)
@@ -689,22 +695,30 @@
             return lax.ppermute(value, "dp", [(i, (i + by) % n) for i in range(n)])
 
         rest = weights, m, v
-        came = [[g0a, g0b]]
-        right, left = (g0a, g0b), (g0a, g0b)
-        for _ in range(1, half):
-            a = sent(right[0], 1), sent(left[0], -1)
-            b = sent(right[1], 1), sent(left[1], -1)
-            right, left = (a[0], b[0]), (a[1], b[1])
-            came.append([*right, *left])
-        came.append([sent(right[0], 1), sent(left[1], -1)])
-
-        jobs = [(1, list(range(k, k + n // 4)), [g1]) for k in range(0, n, n // 4)]
-        jobs.append((0, [0, 1, n - 1], came[0] + came[1]))
-        jobs += [(0, [k, n - k], came[k]) for k in range(2, half)]
-        jobs.append((0, [half], came[half]))
+        pairs = ff // (2 * BLOCK)
+        here = GATHERED // 2
+        each = ga.shape[0] // 2
+        came = {("a", 0): [(0, ga)], ("b", 0): [(0, gb)]}
+        for k in range(1, half):
+            for which in "ab":
+                right, left = came[which, k - 1][0][1], came[which, k - 1][-1][1]
+                came[which, k] = [(k, sent(right, 1)), (n - k, sent(left, -1))]
+        came["a", half] = [(half, sent(came["a", half - 1][0][1], 1))]
+        came["b", half] = [(half, sent(came["b", half - 1][1][1], -1))]
+
+        jobs = [(range(0, 2), ["a0", "b0"]), (range(2, n - 2), []), (range(n - 2, n), ["a1"])]
+        jobs += [((), [f"b{k - 1}", f"a{k}"] if k < 3 else [f"b{k - 1}"]) for k in range(2, half)]
+        jobs += [((), [f"a{half - 1}"]), ((), [f"b{half - 1}"]), ((), [f"a{half}", f"b{half}"])]
         out = None
-        for layer, places, terms in jobs:
-            out = update(layer, places, terms, total, *rest, out)
+        for places, names in jobs:
+            terms, pieces = [g1] if places else [], [(1, pair, place, 0, 2 * pair) for place in places for pair in range(here)]
+            for name in names:
+                for place, array in came[name[0], int(name[1:])]:
+                    for i in range(each):
+                        pair = here + i + (each if name[0] == "b" else 0)
+                        pieces.append((1 if pair < pairs else 0, pair % pairs, place, len(terms), 2 * i))
+                    terms.append(array)
+            out = update(pieces, terms, total, *rest, out)
         out = list(out)
         for i in (2, 5, 8):
             out[i] = out[i].reshape(layers, ff, d)

time: 334 us -> 327 us (0.979)
  Pallas kernels: 311 us -> 299 us
  waiting for transfers between devices: 0.16 us -> 5.14 us
    pallas_call x1, Pallas kernels: 251 us -> 237 us  [reduced(): pl.pallas_call(functools.partial(main_kernel, n), in_specs=[anywhere] * 5...]
    ppermute x14, waiting for transfers between devices: 0.16 us -> 5.14 us  [sent(): return lax.ppermute(value, 'dp', [(i, (i + by) % n) for i in range(n)])]
where the time goes in v4:
time: 327 us; the launch traced here: 326 us
  Pallas kernels  299 us (91%)
  starting transfers between devices  21.2 us (6%)
  waiting for transfers between devices  5.14 us (2%)
    pallas_call x1, Pallas kernels, reduced(): pl.pallas_call(functools.partial(main_kernel, n), in_specs=[anywhere] * 5...  237 us
    pallas_call x8, Pallas kernels, update(): pl.pallas_call(functools.partial(update_kernel, n, pieces, 3 * weights[0]...  62.5 us
    ppermute x14, starting transfers between devices, sent(): return lax.ppermute(value, 'dp', [(i, (i + by) % n) for i in range(n)])  21.2 us
  transfers between devices with their start and end apart: 14, of which 1 were waited for; matrix products, arithmetic and copies ran while one was open for 0% of the time, Pallas kernels for 17%

profile of v4, /device:TPU:28, one launch (start us, length us, event | category | flops | bytes accessed | tf_op | source)
XLA Modules:
  0.0 326.3 jit_solution(2360903538653954039)
XLA Ops:
  0.6 236.5 %reduced.1 = (bf16[8,4,480,128]{3,2,1,0:T(8,128)(2,1)}, bf16[4,480,128]{2,1,0:T(8,128)(2,1)}, bf16[4,480,128]{2,1,0:T(8,128)(2,1)}, f32[8,128]{1,0:T(8,128)}, bf...) custom-call(bf16[1,4096,640]{2,1,0:T(8,128)(2,1)} %x_hbm.1, ...), custom_call_target="tpu_custom_call" | custom-call | flops 136902082560 | bytes 41943040 | tf_op jit(solution)/shard_map/reduced/pallas_call | solution.py:514
  237.2 1.7 collective-permute-start
  238.9 1.6 collective-permute-start.11
  240.5 1.2 collective-permute-start.4
  241.7 0.8 collective-permute-start.8
  242.6 9.5 %update.8 = (bf16[2,640,1536]{2,1,0:T(8,128)(2,1)}, bf16[2,640,1536]{2,1,0:T(8,128)(2,1)}, bf16[2,6,8,32,640]{4,3,2,1,0:T(8,128)(2,1)}, f32[2,640,1536]{2,1,0:T(...) custom-call(f32[8,128]{1,0:T(8,128)} %get-tuple-element.85.refs_0_, ...), custom_call_target="tpu_custom_call" | custom-call | flops 6488064000 | bytes 21626880 | tf_op jit(solution)/shard_map/update/pallas_call | solution.py:660
  252.1 9.5 %update.9 = (bf16[2,640,1536]{2,1,0:T(8,128)(2,1)}, bf16[2,640,1536]{2,1,0:T(8,128)(2,1)}, bf16[2,6,8,32,640]{4,3,2,1,0:T(8,128)(2,1)}, f32[2,640,1536]{2,1,0:T(...) custom-call(f32[8,128]{1,0:T(8,128)} %get-tuple-element.85.refs_0_, ...), custom_call_target="tpu_custom_call", output_to_operand_aliasing={{0}: (11, {}), {1}: (12, {}), {2}: (13, {}), {3}: (14, {}),... | custom-call | flops 6488064000 | bytes 21626880 | tf_op jit(solution)/shard_map/update/pallas_call | solution.py:660
  261.6 0.0 collective-permute-done.refs_2_
  261.6 0.5 collective-permute-start.1
  262.1 0.0 collective-permute-done.11.refs_3_
  262.1 2.8 collective-permute-start.12
  264.9 0.0 collective-permute-done.4.refs_2_
  264.9 1.2 collective-permute-start.5
  266.1 0.0 collective-permute-done.8.refs_1_
  266.1 0.8 collective-permute-start.9
  267.0 9.5 %update.10 = (bf16[2,640,1536]{2,1,0:T(8,128)(2,1)}, bf16[2,640,1536]{2,1,0:T(8,128)(2,1)}, bf16[2,6,8,32,640]{4,3,2,1,0:T(8,128)(2,1)}, f32[2,640,1536]{2,1,0:T...) custom-call(f32[8,128]{1,0:T(8,128)} %get-tuple-element.85.refs_0_, ...), custom_call_target="tpu_custom_call", output_to_operand_aliasing={{0}: (13, {}), {1}: (14, {}), {2}: (15, {}), {3}: (16, {}),... | custom-call | flops 6488064000 | bytes 21626880 | tf_op jit(solution)/shard_map/update/pallas_call | solution.py:660
  276.5 0.0 collective-permute-done.1.refs_3_
  276.5 0.1 collective-permute-start.2
  276.6 0.0 collective-permute-done.12.refs_4_
  276.6 3.2 collective-permute-start.13
  279.8 5.1 %collective-permute-done.5.refs_2_ = bf16[4,480,128]{2,1,0:T(8,128)(2,1)} collective-permute-done((bf16[4,480,128]{2,1,0:T(8,128)(2,1)}, bf16[4,480,128]{2,1,0:T(8,128)(2,1)}, u32[]{:S(2)}, u32[]{:S(2)}) %collective-permute-start.5) | collective-permute-done | bytes 491552 | tf_op jit(solution)/shard_map/ppermute | solution.py:695
  284.9 3.7 %collective-permute-start.6 = (bf16[4,480,128]{2,1,0:T(8,128)(2,1)}, bf16[4,480,128]{2,1,0:T(8,128)(2,1)}, u32[]{:S(2)}, u32[]{:S(2)}) collective-permute-start(bf16[4,480,128]{2,1,0:T(8,128)(2,1)} %collective-permute-done.5.refs_2_), channel_id=1, source_target_pairs={{0,7},{1,0},{2,1},{3,2},{4,3},{5,4},{6,5},{7,6},{8,15},{9,8},{10,9... | collective-permute-start | bytes 1474568 | tf_op jit(solution)/shard_map/ppermute | solution.py:695
  288.6 0.0 collective-permute-done.9.refs_1_
  288.6 0.0 collective-permute-start.10
  288.6 9.5 %update.11 = (bf16[2,640,1536]{2,1,0:T(8,128)(2,1)}, bf16[2,640,1536]{2,1,0:T(8,128)(2,1)}, bf16[2,6,8,32,640]{4,3,2,1,0:T(8,128)(2,1)}, f32[2,640,1536]{2,1,0:T...) custom-call(f32[8,128]{1,0:T(8,128)} %get-tuple-element.85.refs_0_, ...), custom_call_target="tpu_custom_call", output_to_operand_aliasing={{0}: (14, {}), {1}: (15, {}), {2}: (16, {}), {3}: (17, {}),... | custom-call | flops 6488064000 | bytes 21626880 | tf_op jit(solution)/shard_map/update/pallas_call | solution.py:660
  298.1 6.1 %update.12 = (bf16[2,640,1536]{2,1,0:T(8,128)(2,1)}, bf16[2,640,1536]{2,1,0:T(8,128)(2,1)}, bf16[2,6,8,32,640]{4,3,2,1,0:T(8,128)(2,1)}, f32[2,640,1536]{2,1,0:T...) custom-call(f32[8,128]{1,0:T(8,128)} %get-tuple-element.85.refs_0_, ...), custom_call_target="tpu_custom_call", output_to_operand_aliasing={{0}: (12, {}), {1}: (13, {}), {2}: (14, {}), {3}: (15, {}),... | custom-call | flops 3244032000 | bytes 10813440 | tf_op jit(solution)/shard_map/update/pallas_call | solution.py:660
  304.3 0.0 collective-permute-done.2.refs_1_
  304.3 0.3 collective-permute-start.3
  304.6 0.0 collective-permute-done.6.refs_2_
  304.6 3.1 collective-permute-start.7
  307.7 0.0 collective-permute-done.13.refs_2_
  307.8 6.1 %update.13 = (bf16[2,640,1536]{2,1,0:T(8,128)(2,1)}, bf16[2,640,1536]{2,1,0:T(8,128)(2,1)}, bf16[2,6,8,32,640]{4,3,2,1,0:T(8,128)(2,1)}, f32[2,640,1536]{2,1,0:T...) custom-call(f32[8,128]{1,0:T(8,128)} %get-tuple-element.85.refs_0_, ...), custom_call_target="tpu_custom_call", output_to_operand_aliasing={{0}: (12, {}), {1}: (13, {}), {2}: (14, {}), {3}: (15, {}),... | custom-call | flops 3244032000 | bytes 10813440 | tf_op jit(solution)/shard_map/update/pallas_call | solution.py:660
  313.8 0.0 collective-permute-done.10.refs_1_
  313.9 6.1 %update.14 = (bf16[2,640,1536]{2,1,0:T(8,128)(2,1)}, bf16[2,640,1536]{2,1,0:T(8,128)(2,1)}, bf16[2,6,8,32,640]{4,3,2,1,0:T(8,128)(2,1)}, f32[2,640,1536]{2,1,0:T...) custom-call(f32[8,128]{1,0:T(8,128)} %get-tuple-element.85.refs_0_, ...), custom_call_target="tpu_custom_call", output_to_operand_aliasing={{0}: (12, {}), {1}: (13, {}), {2}: (14, {}), {3}: (15, {}),... | custom-call | flops 3244032000 | bytes 10813440 | tf_op jit(solution)/shard_map/update/pallas_call | solution.py:660
  320.0 0.0 collective-permute-done.3.refs_1_
  320.0 0.0 collective-permute-done.7.refs_2_
  320.0 6.1 %update.15 = (bf16[2,640,1536]{2,1,0:T(8,128)(2,1)}, bf16[2,640,1536]{2,1,0:T(8,128)(2,1)}, bf16[2,6,8,32,640]{4,3,2,1,0:T(8,128)(2,1)}, f32[2,640,1536]{2,1,0:T...) custom-call(f32[8,128]{1,0:T(8,128)} %get-tuple-element.85.refs_0_, ...), custom_call_target="tpu_custom_call", output_to_operand_aliasing={{0}: (12, {}), {1}: (13, {}), {2}: (14, {}), {3}: (15, {}),... | custom-call | flops 3244032000 | bytes 10813440 | tf_op jit(solution)/shard_map/update/pallas_call | solution.py:660
Async XLA Ops:
  237.2 24.4 %collective-permute-start = (bf16[4,480,128]{2,1,0:T(8,128)(2,1)}, bf16[4,480,128]{2,1,0:T(8,128)(2,1)}, u32[]{:S(2)}, u32[]{:S(2)}) collective-permute-start(bf16[4,480,128]{2,1,0:T(8,128)(2,1)} %get-tuple-element.86.refs_2_), channel_id=1, source_target_pairs={{0,1},{1,2},{2,3},{3,4},{4,5},{5,6},{6,7},{7,0},{8,9},{9,10},{10,1... | collective-permute-start | bytes 1474568 | tf_op jit(solution)/shard_map/ppermute | solution.py:695
  238.9 23.2 %collective-permute-start.11 = (bf16[4,480,128]{2,1,0:T(8,128)(2,1)}, bf16[4,480,128]{2,1,0:T(8,128)(2,1)}, u32[]{:S(2)}, u32[]{:S(2)}) collective-permute-start(bf16[4,480,128]{2,1,0:T(8,128)(2,1)} %get-tuple-element.86.refs_2_), channel_id=1, source_target_pairs={{0,7},{1,0},{2,1},{3,2},{4,3},{5,4},{6,5},{7,6},{8,15},{9,8},{10,9... | collective-permute-start | bytes 1474568 | tf_op jit(solution)/shard_map/ppermute | solution.py:695
  240.5 24.4 %collective-permute-start.4 = (bf16[4,480,128]{2,1,0:T(8,128)(2,1)}, bf16[4,480,128]{2,1,0:T(8,128)(2,1)}, u32[]{:S(2)}, u32[]{:S(2)}) collective-permute-start(bf16[4,480,128]{2,1,0:T(8,128)(2,1)} %get-tuple-element.87.refs_3_), channel_id=1, source_target_pairs={{0,7},{1,0},{2,1},{3,2},{4,3},{5,4},{6,5},{7,6},{8,15},{9,8},{10,9... | collective-permute-start | bytes 1474568 | tf_op jit(solution)/shard_map/ppermute | solution.py:695
  241.7 24.4 %collective-permute-start.8 = (bf16[4,480,128]{2,1,0:T(8,128)(2,1)}, bf16[4,480,128]{2,1,0:T(8,128)(2,1)}, u32[]{:S(2)}, u32[]{:S(2)}) collective-permute-start(bf16[4,480,128]{2,1,0:T(8,128)(2,1)} %get-tuple-element.87.refs_3_), channel_id=1, source_target_pairs={{0,1},{1,2},{2,3},{3,4},{4,5},{5,6},{6,7},{7,0},{8,9},{9,10},{10,1... | collective-permute-start | bytes 1474568 | tf_op jit(solution)/shard_map/ppermute | solution.py:695
  261.6 14.9 %collective-permute-start.1 = (bf16[4,480,128]{2,1,0:T(8,128)(2,1)}, bf16[4,480,128]{2,1,0:T(8,128)(2,1)}, u32[]{:S(2)}, u32[]{:S(2)}) collective-permute-start(bf16[4,480,128]{2,1,0:T(8,128)(2,1)} %collective-permute-done.refs_2_), channel_id=1, source_target_pairs={{0,1},{1,2},{2,3},{3,4},{4,5},{5,6},{6,7},{7,0},{8,9},{9,10},{10,1... | collective-permute-start | bytes 1474568 | tf_op jit(solution)/shard_map/ppermute | solution.py:695
  262.1 14.5 %collective-permute-start.12 = (bf16[4,480,128]{2,1,0:T(8,128)(2,1)}, bf16[4,480,128]{2,1,0:T(8,128)(2,1)}, u32[]{:S(2)}, u32[]{:S(2)}) collective-permute-start(bf16[4,480,128]{2,1,0:T(8,128)(2,1)} %collective-permute-done.11.refs_3_), channel_id=1, source_target_pairs={{0,7},{1,0},{2,1},{3,2},{4,3},{5,4},{6,5},{7,6},{8,15},{9,8},{10,9... | collective-permute-start | bytes 1474568 | tf_op jit(solution)/shard_map/ppermute | solution.py:695
  264.9 20.0 %collective-permute-start.5 = (bf16[4,480,128]{2,1,0:T(8,128)(2,1)}, bf16[4,480,128]{2,1,0:T(8,128)(2,1)}, u32[]{:S(2)}, u32[]{:S(2)}) collective-permute-start(bf16[4,480,128]{2,1,0:T(8,128)(2,1)} %collective-permute-done.4.refs_2_), channel_id=1, source_target_pairs={{0,7},{1,0},{2,1},{3,2},{4,3},{5,4},{6,5},{7,6},{8,15},{9,8},{10,9... | collective-permute-start | bytes 1474568 | tf_op jit(solution)/shard_map/ppermute | solution.py:695
  266.1 22.5 %collective-permute-start.9 = (bf16[4,480,128]{2,1,0:T(8,128)(2,1)}, bf16[4,480,128]{2,1,0:T(8,128)(2,1)}, u32[]{:S(2)}, u32[]{:S(2)}) collective-permute-start(bf16[4,480,128]{2,1,0:T(8,128)(2,1)} %collective-permute-done.8.refs_1_), channel_id=1, source_target_pairs={{0,1},{1,2},{2,3},{3,4},{4,5},{5,6},{6,7},{7,0},{8,9},{9,10},{10,1... | collective-permute-start | bytes 1474568 | tf_op jit(solution)/shard_map/ppermute | solution.py:695
  276.5 27.8 %collective-permute-start.2 = (bf16[4,480,128]{2,1,0:T(8,128)(2,1)}, bf16[4,480,128]{2,1,0:T(8,128)(2,1)}, u32[]{:S(2)}, u32[]{:S(2)}) collective-permute-start(bf16[4,480,128]{2,1,0:T(8,128)(2,1)} %collective-permute-done.1.refs_3_), channel_id=1, source_target_pairs={{0,1},{1,2},{2,3},{3,4},{4,5},{5,6},{6,7},{7,0},{8,9},{9,10},{10,1... | collective-permute-start | bytes 1474568 | tf_op jit(solution)/shard_map/ppermute | solution.py:695
  276.6 31.1 %collective-permute-start.13 = (bf16[4,480,128]{2,1,0:T(8,128)(2,1)}, bf16[4,480,128]{2,1,0:T(8,128)(2,1)}, u32[]{:S(2)}, u32[]{:S(2)}) collective-permute-start(bf16[4,480,128]{2,1,0:T(8,128)(2,1)} %collective-permute-done.12.refs_4_), channel_id=1, source_target_pairs={{0,7},{1,0},{2,1},{3,2},{4,3},{5,4},{6,5},{7,6},{8,15},{9,8},{10,9... | collective-permute-start | bytes 1474568 | tf_op jit(solution)/shard_map/ppermute | solution.py:695
  284.9 19.7 %collective-permute-start.6 = (bf16[4,480,128]{2,1,0:T(8,128)(2,1)}, bf16[4,480,128]{2,1,0:T(8,128)(2,1)}, u32[]{:S(2)}, u32[]{:S(2)}) collective-permute-start(bf16[4,480,128]{2,1,0:T(8,128)(2,1)} %collective-permute-done.5.refs_2_), channel_id=1, source_target_pairs={{0,7},{1,0},{2,1},{3,2},{4,3},{5,4},{6,5},{7,6},{8,15},{9,8},{10,9... | collective-permute-start | bytes 1474568 | tf_op jit(solution)/shard_map/ppermute | solution.py:695
  288.6 25.2 %collective-permute-start.10 = (bf16[4,480,128]{2,1,0:T(8,128)(2,1)}, bf16[4,480,128]{2,1,0:T(8,128)(2,1)}, u32[]{:S(2)}, u32[]{:S(2)}) collective-permute-start(bf16[4,480,128]{2,1,0:T(8,128)(2,1)} %collective-permute-done.9.refs_1_), channel_id=1, source_target_pairs={{0,1},{1,2},{2,3},{3,4},{4,5},{5,6},{6,7},{7,0},{8,9},{9,10},{10,1... | collective-permute-start | bytes 1474568 | tf_op jit(solution)/shard_map/ppermute | solution.py:695
  304.3 15.7 %collective-permute-start.3 = (bf16[4,480,128]{2,1,0:T(8,128)(2,1)}, bf16[4,480,128]{2,1,0:T(8,128)(2,1)}, u32[]{:S(2)}, u32[]{:S(2)}) collective-permute-start(bf16[4,480,128]{2,1,0:T(8,128)(2,1)} %collective-permute-done.2.refs_1_), channel_id=1, source_target_pairs={{0,1},{1,2},{2,3},{3,4},{4,5},{5,6},{6,7},{7,0},{8,9},{9,10},{10,1... | collective-permute-start | bytes 1474568 | tf_op jit(solution)/shard_map/ppermute | solution.py:695
  304.6 15.4 %collective-permute-start.7 = (bf16[4,480,128]{2,1,0:T(8,128)(2,1)}, bf16[4,480,128]{2,1,0:T(8,128)(2,1)}, u32[]{:S(2)}, u32[]{:S(2)}) collective-permute-start(bf16[4,480,128]{2,1,0:T(8,128)(2,1)} %collective-permute-done.6.refs_2_), channel_id=1, source_target_pairs={{0,7},{1,0},{2,1},{3,2},{4,3},{5,4},{6,5},{7,6},{8,15},{9,8},{10,9... | collective-permute-start | bytes 1474568 | tf_op jit(solution)/shard_map/ppermute | solution.py:695
